TPU v7x, 256 devices: a whole 4x4x8 slice. The times are simulated.
256 devices in a mesh: dp: 64 (over z, y, core), cp: 4 (over x).
Axes of the slice: x: 4, y: 4, z: 8, core: 2. Of those that a mesh axis runs over, the one named last changes fastest.
Arguments:
- x_in: bfloat16 [128, 2048, 640], P('dp', 'cp')
- grad_y: bfloat16 [128, 2048, 640], P('dp', 'cp')
- ln_gamma: float32 [640], replicated
- ln_beta: float32 [640], replicated
- w_q: bfloat16 [640, 8, 80], replicated
- w_k: bfloat16 [640, 8, 80], replicated
- w_v: bfloat16 [640, 8, 80], replicated
- w_o: bfloat16 [8, 80, 640], replicated
- b_o: float32 [640], replicated
Outputs:
- output 1: bfloat16 [128, 2048, 640], P('dp', 'cp')
- output 2: bfloat16 [128, 2048, 640], P('dp', 'cp')
- output 3: float32 [640], replicated
- output 4: float32 [640], replicated
- output 5: float32 [640, 8, 80], replicated
- output 6: float32 [640, 8, 80], replicated
- output 7: float32 [640, 8, 80], replicated
- output 8: float32 [8, 80, 640], replicated
- output 9: float32 [640], replicated
All inputs are finite; a program needn't handle non-finite values.
Results may differ from a plain program's by a relative error of at most 0.0149178.
Values are sent between devices in bfloat16 or wider.
A program may use at most 768 MiB of HBM per device.

v0:
```python
import math
import jax
import jax.numpy as jnp
from jax import lax
from jax.sharding import PartitionSpec as P

LN_EPS = 1e-5
ROW_CAP = 128


def layer_norm_fwd(x_f, ln_gamma, ln_beta):
    tok_mean = jnp.mean(x_f, axis=-1, keepdims=True)
    centered = x_f - tok_mean
    tok_var = jnp.mean(centered * centered, axis=-1, keepdims=True)
    inv_std = lax.rsqrt(tok_var + LN_EPS)
    x_hat = centered * inv_std
    normed = (x_hat * ln_gamma + ln_beta).astype(jnp.bfloat16)
    return normed, x_hat, inv_std


def layer_norm_bwd(d_normed, x_hat, inv_std, ln_gamma):
    d_hat = d_normed * ln_gamma
    mean_one = jnp.mean(d_hat, axis=-1, keepdims=True)
    mean_two = jnp.mean(d_hat * x_hat, axis=-1, keepdims=True)
    return inv_std * (d_hat - mean_one - x_hat * mean_two)


def solution(mesh):
    cp_size = mesh.shape['cp']
    send_pairs = [(source, (source + 1) % cp_size) for source in range(cp_size)]
    act_spec = P('dp', 'cp', None)
    rep_spec = P()

    def device_step(x_in, grad_y, ln_gamma, ln_beta, w_q, w_k, w_v, w_o, b_o):
        batch_loc, tok_loc, chan_count = x_in.shape
        num_heads = w_q.shape[1]
        head_dim = w_q.shape[2]
        row_len = math.gcd(tok_loc, ROW_CAP)
        row_blocks = tok_loc // row_len
        score_scale = head_dim ** -0.5

        x_f = x_in.astype(jnp.float32)
        normed, x_hat, inv_std = layer_norm_fwd(x_f, ln_gamma, ln_beta)
        normed_blk = normed.reshape(batch_loc, row_blocks, row_len, chan_count)
        q_blk = jnp.einsum('bjrc,chd->bjhrd', normed_blk, w_q, preferred_element_type=jnp.float32).astype(jnp.bfloat16)
        w_kv = jnp.stack([w_k, w_v])
        kv_loc = jnp.einsum('bnc,tchd->btnhd', normed, w_kv, preferred_element_type=jnp.float32).astype(jnp.bfloat16)

        def fwd_sample(operands):
            q_sample, max_sample, sum_sample, acc_sample, kv_sample = operands

            def fwd_rows(rows_in):
                q_rows, max_rows, sum_rows, acc_rows = rows_in
                scores = jnp.einsum('hrd,khd->hrk', q_rows, kv_sample[0], preferred_element_type=jnp.float32) * score_scale
                new_max = jnp.maximum(max_rows, jnp.max(scores, axis=-1))
                rescale = jnp.exp(max_rows - new_max)
                prob_rows = jnp.exp(scores - new_max[..., None])
                new_sum = sum_rows * rescale + jnp.sum(prob_rows, axis=-1)
                new_acc = acc_rows * rescale[..., None] + jnp.einsum(
                    'hrk,khd->hrd', prob_rows.astype(jnp.bfloat16), kv_sample[1], preferred_element_type=jnp.float32)
                return new_max, new_sum, new_acc

            return lax.map(fwd_rows, (q_sample, max_sample, sum_sample, acc_sample))

        stat_shape = (batch_loc, row_blocks, num_heads, row_len)
        run_max = jnp.full(stat_shape, -jnp.inf, jnp.float32)
        run_sum = jnp.zeros(stat_shape, jnp.float32)
        run_acc = jnp.zeros(q_blk.shape, jnp.float32)
        kv_cur = kv_loc
        for step_idx in range(cp_size):
            run_max, run_sum, run_acc = lax.map(fwd_sample, (q_blk, run_max, run_sum, run_acc, kv_cur))
            if step_idx < cp_size - 1:
                kv_cur = lax.ppermute(kv_cur, 'cp', send_pairs)

        out_f = run_acc / run_sum[..., None]
        out_blk = out_f.astype(jnp.bfloat16)
        log_norm = run_max + jnp.log(run_sum)
        proj_out = jnp.einsum('bjhrd,hdc->bjrc', out_blk, w_o, preferred_element_type=jnp.float32)
        y_out = (x_f + proj_out.reshape(batch_loc, tok_loc, chan_count) + b_o).astype(jnp.bfloat16)

        dy_blk = grad_y.reshape(batch_loc, row_blocks, row_len, chan_count)
        grad_bo = jnp.sum(grad_y.astype(jnp.float32), axis=(0, 1))
        grad_wo = jnp.einsum('bjhrd,bjrc->hdc', out_blk, dy_blk, preferred_element_type=jnp.float32)
        d_out = jnp.einsum('bjrc,hdc->bjhrd', dy_blk, w_o, preferred_element_type=jnp.float32).astype(jnp.bfloat16)
        row_delta = jnp.sum(d_out.astype(jnp.float32) * out_f, axis=-1)

        def bwd_sample(operands):
            q_sample, do_sample, lse_sample, delta_sample, dq_sample, kv_sample = operands

            def bwd_rows(kv_carry, rows_in):
                dk_acc, dv_acc = kv_carry
                q_rows, do_rows, lse_rows, delta_rows, dq_rows = rows_in
                scores = jnp.einsum('hrd,khd->hrk', q_rows, kv_sample[0], preferred_element_type=jnp.float32) * score_scale
                prob_rows = jnp.exp(scores - lse_rows[..., None])
                d_probs = jnp.einsum('hrd,khd->hrk', do_rows, kv_sample[1], preferred_element_type=jnp.float32)
                d_scores = (prob_rows * (d_probs - delta_rows[..., None])).astype(jnp.bfloat16)
                dq_next = dq_rows + score_scale * jnp.einsum(
                    'hrk,khd->hrd', d_scores, kv_sample[0], preferred_element_type=jnp.float32)
                dk_acc = dk_acc + score_scale * jnp.einsum(
                    'hrk,hrd->khd', d_scores, q_rows, preferred_element_type=jnp.float32)
                dv_acc = dv_acc + jnp.einsum(
                    'hrk,hrd->khd', prob_rows.astype(jnp.bfloat16), do_rows, preferred_element_type=jnp.float32)
                return (dk_acc, dv_acc), dq_next

            zero_kv = jnp.zeros(kv_sample.shape[1:], jnp.float32)
            kv_sums, dq_out = lax.scan(bwd_rows, (zero_kv, zero_kv),
                                       (q_sample, do_sample, lse_sample, delta_sample, dq_sample))
            return dq_out, jnp.stack([kv_sums[0], kv_sums[1]])

        dq_acc = jnp.zeros(q_blk.shape, jnp.float32)
        kv_cur = kv_loc
        dkv_cur = None
        for step_idx in range(cp_size):
            dq_acc, dkv_step = lax.map(bwd_sample, (q_blk, d_out, log_norm, row_delta, dq_acc, kv_cur))
            if step_idx == 0:
                dkv_cur = dkv_step.astype(jnp.bfloat16)
            else:
                dkv_cur = (dkv_cur.astype(jnp.float32) + dkv_step).astype(jnp.bfloat16)
            dkv_cur = lax.ppermute(dkv_cur, 'cp', send_pairs)
            if step_idx < cp_size - 1:
                kv_cur = lax.ppermute(kv_cur, 'cp', send_pairs)

        dq_bf = dq_acc.astype(jnp.bfloat16)
        grad_wq = jnp.einsum('bjrc,bjhrd->chd', normed_blk, dq_bf, preferred_element_type=jnp.float32)
        grad_wkv = jnp.einsum('bnc,btnhd->tchd', normed, dkv_cur, preferred_element_type=jnp.float32)
        d_from_q = jnp.einsum('bjhrd,chd->bjrc', dq_bf, w_q, preferred_element_type=jnp.float32)
        d_from_kv = jnp.einsum('btnhd,tchd->bnc', dkv_cur, w_kv, preferred_element_type=jnp.float32)
        d_normed = (d_from_q.reshape(batch_loc, tok_loc, chan_count) + d_from_kv).astype(jnp.bfloat16).astype(jnp.float32)
        grad_gamma = jnp.sum(d_normed * x_hat, axis=(0, 1))
        grad_beta = jnp.sum(d_normed, axis=(0, 1))
        grad_x = (grad_y.astype(jnp.float32) + layer_norm_bwd(d_normed, x_hat, inv_std, ln_gamma)).astype(jnp.bfloat16)
        summed = lax.psum((grad_gamma, grad_beta, grad_wq, grad_wkv, grad_wo, grad_bo), ('dp', 'cp'))
        return (y_out, grad_x, summed[0], summed[1], summed[2], summed[3][0], summed[3][1], summed[4], summed[5])

    return jax.shard_map(device_step, mesh=mesh,
                         in_specs=(act_spec, act_spec, rep_spec, rep_spec, rep_spec, rep_spec, rep_spec, rep_spec, rep_spec),
                         out_specs=(act_spec, act_spec, rep_spec, rep_spec, rep_spec, rep_spec, rep_spec, rep_spec, rep_spec),
                         check_vma=False)
```

profile of v0, /device:TPU:1, one launch (start us, length us, event | category | flops | bytes accessed | tf_op | source)
XLA Modules:
  0.0 1147.4 jit_solution(11176781041973487002)
XLA Ops:
  24.4 38.7 %while.223 = (s32[]{:T(128)}, f32[2,4,8,128]{3,2,1,0:T(8,128)S(1)}, f32[2,4,8,128]{3,2,1,0:T(8,128)}, f32[2,4,8,128,80]{3,4,2,1,0:T(8,128)}, bf16[2,4,8,128,80]{...) while((s32[]{:T(128)}, f32[2,4,8,128]{3,2,1,0:T(8,128)S(1)}, ...), condition=%wide.region_7.8_spmd, body=%wide.region_2.7_spmd.sunk | while | flops 172051456 | bytes 14760182 | solution.py:71
  80.3 53.0 %while.225 = (s32[]{:T(128)}, f32[2,4,8,128]{3,2,1,0:T(8,128)}, f32[2,4,8,128]{3,2,1,0:T(8,128)}, f32[2,4,8,128,80]{3,4,2,1,0:T(8,128)}, bf16[2,4,8,128,80]{3,4,...) while((s32[]{:T(128)}, f32[2,4,8,128]{3,2,1,0:T(8,128)}, ...), condition=%wide.region_13.14_spmd, body=%wide.region_8.13_spmd.sunk | while | flops 172134400 | bytes 28539296 | solution.py:71
  85.2 17.8 %while.239 = (s32[]{:T(128)}, f32[4,8,128]{2,1,0:T(8,128)S(1)}, f32[4,8,128]{2,1,0:T(8,128)S(1)}, f32[4,8,128,80]{2,3,1,0:T(8,128)}, f32[4,8,128]{2,1,0:T(8,128)...) while((s32[]{:T(128)}, f32[4,8,128]{2,1,0:T(8,128)S(1)}, ...), condition=%wide.region_12.12_spmd, body=%wide.region_9.11_spmd.sunk | while | flops 172134400 | bytes 8483949 | solution.py:63
  111.7 17.8 %while.239 = (s32[]{:T(128)}, f32[4,8,128]{2,1,0:T(8,128)S(1)}, f32[4,8,128]{2,1,0:T(8,128)S(1)}, f32[4,8,128,80]{2,3,1,0:T(8,128)}, f32[4,8,128]{2,1,0:T(8,128)...) while((s32[]{:T(128)}, f32[4,8,128]{2,1,0:T(8,128)S(1)}, ...), condition=%wide.region_12.12_spmd, body=%wide.region_9.11_spmd.sunk | while | flops 172134400 | bytes 8483949 | solution.py:63
  141.5 53.1 %while.227 = (s32[]{:T(128)}, f32[2,4,8,128]{3,2,1,0:T(8,128)}, f32[2,4,8,128]{3,2,1,0:T(8,128)}, f32[2,4,8,128,80]{3,4,2,1,0:T(8,128)}, bf16[2,4,8,128,80]{3,4,...) while((s32[]{:T(128)}, f32[2,4,8,128]{3,2,1,0:T(8,128)}, ...), condition=%wide.region_19.20_spmd, body=%wide.region_14.19_spmd.sunk | while | flops 172134400 | bytes 28539296 | solution.py:71
  173.0 17.8 %while.240 = (s32[]{:T(128)}, f32[4,8,128]{2,1,0:T(8,128)S(1)}, f32[4,8,128]{2,1,0:T(8,128)S(1)}, f32[4,8,128,80]{2,3,1,0:T(8,128)}, f32[4,8,128]{2,1,0:T(8,128)...) while((s32[]{:T(128)}, f32[4,8,128]{2,1,0:T(8,128)S(1)}, ...), condition=%wide.region_18.18_spmd, body=%wide.region_15.17_spmd.sunk | while | flops 172134400 | bytes 8483949 | solution.py:63
  199.3 50.8 %while.229 = (s32[]{:T(128)}, f32[2,4,8,128]{3,2,1,0:T(8,128)}, f32[2,4,8,128]{3,2,1,0:T(8,128)}, f32[2,4,8,128,80]{3,4,1,0,2:T(8,128)}, bf16[2,4,8,128,80]{3,4,...) while((s32[]{:T(128)}, f32[2,4,8,128]{3,2,1,0:T(8,128)}, ...), condition=%wide.region_25.26_spmd, body=%wide.region_20.25_spmd.sunk | while | flops 172134400 | bytes 28800988 | solution.py:71
  203.7 17.9 %while.241 = (s32[]{:T(128)}, f32[4,8,128]{2,1,0:T(8,128)S(1)}, f32[4,8,128]{2,1,0:T(8,128)S(1)}, f32[4,8,128,80]{2,3,1,0:T(8,128)}, f32[4,8,128]{2,1,0:T(8,128)...) while((s32[]{:T(128)}, f32[4,8,128]{2,1,0:T(8,128)S(1)}, ...), condition=%wide.region_24.24_spmd, body=%wide.region_21.23_spmd.sunk | while | flops 172134400 | bytes 8483949 | solution.py:63
  229.1 17.8 %while.241 = (s32[]{:T(128)}, f32[4,8,128]{2,1,0:T(8,128)S(1)}, f32[4,8,128]{2,1,0:T(8,128)S(1)}, f32[4,8,128,80]{2,3,1,0:T(8,128)}, f32[4,8,128]{2,1,0:T(8,128)...) while((s32[]{:T(128)}, f32[4,8,128]{2,1,0:T(8,128)S(1)}, ...), condition=%wide.region_24.24_spmd, body=%wide.region_21.23_spmd.sunk | while | flops 172134400 | bytes 8483949 | solution.py:63
  256.5 111.7 %while.231 = (s32[]{:T(128)}, f32[2,4,8,128,80]{3,4,2,1,0:T(8,128)}, bf16[2,2,512,8,80]{2,4,1,3,0:T(8,128)(2,1)}, bf16[2,4,8,128,80]{3,4,2,1,0:T(8,128)(2,1)S(1)...) while((s32[]{:T(128)}, f32[2,4,8,128,80]{3,4,2,1,0:T(8,128)}, ...), condition=%wide.region_30.31_spmd, body=%wide.region_27.30_spmd.sunk | while | flops 426000384 | bytes 70418464 | solution.py:114
  260.5 46.9 %while.242 = (s32[]{:T(128)}, f32[512,8,80]{0,2,1:T(8,128)}, f32[512,8,80]{0,2,1:T(8,128)}, f32[4,8,128,80]{2,3,1,0:T(8,128)}, bf16[4,8,128,80]{2,3,1,0:T(8,128)...) while((s32[]{:T(128)}, f32[512,8,80]{0,2,1:T(8,128)}, ...), condition=%wide.region_29.29_spmd.clone, body=%wide.region_28.28_spmd.clone.sunk | while | flops 425345024 | bytes 32340688 | solution.py:106
  316.4 46.9 %while.242 = (s32[]{:T(128)}, f32[512,8,80]{0,2,1:T(8,128)}, f32[512,8,80]{0,2,1:T(8,128)}, f32[4,8,128,80]{2,3,1,0:T(8,128)}, bf16[4,8,128,80]{2,3,1,0:T(8,128)...) while((s32[]{:T(128)}, f32[512,8,80]{0,2,1:T(8,128)}, ...), condition=%wide.region_29.29_spmd.clone, body=%wide.region_28.28_spmd.clone.sunk | while | flops 425345024 | bytes 32340688 | solution.py:106
  384.7 125.8 %while.233 = (s32[]{:T(128)}, f32[2,4,8,128,80]{3,4,2,1,0:T(8,128)}, f32[2,2,512,8,80]{2,4,1,3,0:T(8,128)}, bf16[2,4,8,128,80]{3,4,2,1,0:T(8,128)(2,1)S(1)}, bf1...) while((s32[]{:T(128)}, f32[2,4,8,128,80]{3,4,2,1,0:T(8,128)}, ...), condition=%wide.region_34.35_spmd, body=%wide.region_31.34_spmd.sunk | while | flops 426082304 | bytes 74678328 | solution.py:114
  391.2 51.0 %while.243 = (s32[]{:T(128)}, f32[512,8,80]{0,2,1:T(8,128)}, f32[512,8,80]{0,2,1:T(8,128)}, f32[4,8,128,80]{2,3,1,0:T(8,128)}, bf16[4,8,128,80]{2,3,1,0:T(8,128)...) while((s32[]{:T(128)}, f32[512,8,80]{0,2,1:T(8,128)}, ...), condition=%wide.region_33.33_spmd.clone, body=%wide.region_32.32_spmd.clone.sunk | while | flops 425426944 | bytes 32668376 | solution.py:106
  454.0 51.0 %while.243 = (s32[]{:T(128)}, f32[512,8,80]{0,2,1:T(8,128)}, f32[512,8,80]{0,2,1:T(8,128)}, f32[4,8,128,80]{2,3,1,0:T(8,128)}, bf16[4,8,128,80]{2,3,1,0:T(8,128)...) while((s32[]{:T(128)}, f32[512,8,80]{0,2,1:T(8,128)}, ...), condition=%wide.region_33.33_spmd.clone, body=%wide.region_32.32_spmd.clone.sunk | while | flops 425426944 | bytes 32668376 | solution.py:106
  522.0 125.9 %while.235 = (s32[]{:T(128)}, f32[2,4,8,128,80]{3,4,2,1,0:T(8,128)}, f32[2,2,512,8,80]{2,4,1,3,0:T(8,128)}, bf16[2,4,8,128,80]{3,4,2,1,0:T(8,128)(2,1)S(1)}, bf1...) while((s32[]{:T(128)}, f32[2,4,8,128,80]{3,4,2,1,0:T(8,128)}, ...), condition=%wide.region_38.39_spmd, body=%wide.region_35.38_spmd.sunk | while | flops 426082304 | bytes 74678328 | solution.py:114
  528.6 50.9 %while.244 = (s32[]{:T(128)}, f32[512,8,80]{0,2,1:T(8,128)}, f32[512,8,80]{0,2,1:T(8,128)}, f32[4,8,128,80]{2,3,1,0:T(8,128)}, bf16[4,8,128,80]{2,3,1,0:T(8,128)...) while((s32[]{:T(128)}, f32[512,8,80]{0,2,1:T(8,128)}, ...), condition=%wide.region_37.37_spmd.clone, body=%wide.region_36.36_spmd.clone.sunk | while | flops 425426944 | bytes 32668376 | solution.py:106
  591.5 50.9 %while.244 = (s32[]{:T(128)}, f32[512,8,80]{0,2,1:T(8,128)}, f32[512,8,80]{0,2,1:T(8,128)}, f32[4,8,128,80]{2,3,1,0:T(8,128)}, bf16[4,8,128,80]{2,3,1,0:T(8,128)...) while((s32[]{:T(128)}, f32[512,8,80]{0,2,1:T(8,128)}, ...), condition=%wide.region_37.37_spmd.clone, body=%wide.region_36.36_spmd.clone.sunk | while | flops 425426944 | bytes 32668376 | solution.py:106
  657.0 125.9 %while.237 = (s32[]{:T(128)}, bf16[2,4,8,128,80]{3,4,2,1,0:T(8,128)(2,1)}, f32[2,2,512,8,80]{2,4,1,3,0:T(8,128)}, bf16[2,4,8,128,80]{3,4,2,1,0:T(8,128)(2,1)S(1)...) while((s32[]{:T(128)}, ...), condition=%wide.region_42.43_spmd, body=%wide.region_39.42_spmd.sunk | while | flops 426082304 | bytes 86473912 | solution.py:114
  663.5 51.6 %while.245 = (s32[]{:T(128)}, f32[512,8,80]{0,2,1:T(8,128)}, f32[512,8,80]{0,2,1:T(8,128)}, bf16[4,8,128,80]{2,3,1,0:T(8,128)(2,1)}, bf16[4,8,128,80]{2,3,1,0:T(...) while((s32[]{:T(128)}, f32[512,8,80]{0,2,1:T(8,128)}, ...), condition=%wide.region_41.41_spmd.clone, body=%wide.region_40.40_spmd.clone.sunk | while | flops 425426944 | bytes 37910804 | solution.py:106
  726.4 51.6 %while.245 = (s32[]{:T(128)}, f32[512,8,80]{0,2,1:T(8,128)}, f32[512,8,80]{0,2,1:T(8,128)}, bf16[4,8,128,80]{2,3,1,0:T(8,128)(2,1)}, bf16[4,8,128,80]{2,3,1,0:T(...) while((s32[]{:T(128)}, f32[512,8,80]{0,2,1:T(8,128)}, ...), condition=%wide.region_41.41_spmd.clone, body=%wide.region_40.40_spmd.clone.sunk | while | flops 425426944 | bytes 37910804 | solution.py:106
  793.6 49.4 %collective-permute-done.6 = bf16[2,2,512,8,80]{2,4,1,3,0:T(8,128)(2,1)S(1)} collective-permute-done((bf16[2,2,512,8,80]{2,4,1,3,0:T(8,128)(2,1)S(1)}, bf16[2,2,512,8,80]{2,4,1,3,0:T(8,128)(2,1)S(1)}, u32[]{:S(2)}, u32[]{:S(2)}) %collective-permute-start.6) | collective-permute-done | bytes 2621472 | tf_op jit(solution)/shard_map/ppermute | solution.py:119
  859.2 86.7 %all-reduce = (f32[640]{0:T(1024)}, f32[640]{0:T(1024)}, f32[640]{0:T(1024)}) all-reduce(f32[640]{0:T(1024)S(1)} %get-tuple-element.1117, f32[640]{0:T(1024)S(1)} %get-tuple-element.1120, f32[640]{0:T(1024)S(1)} %get-tuple-element.1465), channel_id=1, replica_groups=mesh['dp'=64,'cp'=4] {'dp','cp'}, use_global_device_ids=true, to_apply=%region_46.47 | all-reduce | flops 1920 | bytes 15360 | tf_op jit(solution)/shard_map/psum | solution.py:132
  945.9 187.1 %all-reduce.4.cloned.1.call-done = (f32[640,8,80]{0,2,1:T(8,128)}, f32[2,640,8,80]{1,3,2,0:T(8,128)}, f32[8,80,640]{2,1,0:T(8,128)}) async-done(((f32[640,8,80]{0,2,1:T(8,128)}, f32[2,640,8,80]{1,3,2,0:T(8,128)}, f32[8,80,640]{2,1,0:T(8,128)}), (f32[640,8,80]{0,2,1:T(8,128)}, f32[2,640,8,80]{1,3,2,0:T(8,128)}, f32[8,80,640]{2,1,0:T(8,128)})) %all-reduce.4.cloned.1.call-update) | async-done | bytes 6553616 | tf_op jit(solution)/shard_map/psum | solution.py:132
  (971 shorter events, 852.7 us)
Async XLA Ops:
  7.2 55.9 %copy-start = (bf16[8,80,640]{2,1,0:T(8,128)(2,1)S(1)}, bf16[8,80,640]{2,1,0:T(8,128)(2,1)}, u32[]{:S(2)}) copy-start(bf16[8,80,640]{2,1,0:T(8,128)(2,1)} %param.48) | copy-start | bytes 2457604
  7.2 1125.8 %all-reduce.4.cloned.1.call-start = ((), (), s32[]{:S(2)}) async-start(), calls=%async_computation | async-start | bytes 13107200 | tf_op jit(solution)/shard_map/psum | solution.py:132
  14.1 57.8 %collective-permute-start = (bf16[2,2,512,8,80]{2,4,0,3,1:T(8,128)(2,1)}, bf16[2,2,512,8,80]{2,4,0,3,1:T(8,128)(2,1)}, u32[]{:S(2)}, u32[]{:S(2)}) collective-permute-start(bf16[2,2,512,8,80]{2,4,0,3,1:T(8,128)(2,1)} %convert_bitcast_fusion), channel_id=1, source_target_pairs={{0,1},{1,2},{2,3},{3,0},{4,5},{5,6},{6,7},{7,4},{8,9},{9,10},{10,1... | collective-permute-start | bytes 7864328 | tf_op jit(solution)/shard_map/ppermute | solution.py:73
  75.5 57.8 %collective-permute-start.1 = (bf16[2,2,512,8,80]{2,4,0,3,1:T(8,128)(2,1)}, bf16[2,2,512,8,80]{2,4,0,3,1:T(8,128)(2,1)}, u32[]{:S(2)}, u32[]{:S(2)}) collective-permute-start(bf16[2,2,512,8,80]{2,4,0,3,1:T(8,128)(2,1)} %collective-permute-done), channel_id=1, source_target_pairs={{0,1},{1,2},{2,3},{3,0},{4,5},{5,6},{6,7},{7,4},{8,9},{9,10},{10,1... | collective-permute-start | bytes 7864328 | tf_op jit(solution)/shard_map/ppermute | solution.py:73
  136.8 4.6 copy-start.51
  136.9 57.8 %collective-permute-start.2 = (bf16[2,2,512,8,80]{2,4,0,3,1:T(8,128)(2,1)}, bf16[2,2,512,8,80]{2,4,0,3,1:T(8,128)(2,1)}, u32[]{:S(2)}, u32[]{:S(2)}) collective-permute-start(bf16[2,2,512,8,80]{2,4,0,3,1:T(8,128)(2,1)} %collective-permute-done.1), channel_id=1, source_target_pairs={{0,1},{1,2},{2,3},{3,0},{4,5},{5,6},{6,7},{7,4},{8,9},{9,10},{10,1... | collective-permute-start | bytes 7864328 | tf_op jit(solution)/shard_map/ppermute | solution.py:73
  194.6 4.7 copy-start.54
  256.5 4.0 copy-start.13
  312.4 4.0 copy-start.13
  368.2 142.3 %collective-permute-start.3 = (bf16[2,2,512,8,80]{2,4,1,3,0:T(8,128)(2,1)}, bf16[2,2,512,8,80]{2,4,1,3,0:T(8,128)(2,1)}, u32[]{:S(2)}, u32[]{:S(2)}) collective-permute-start(bf16[2,2,512,8,80]{2,4,1,3,0:T(8,128)(2,1)} %get-tuple-element.848), channel_id=1, source_target_pairs={{0,1},{1,2},{2,3},{3,0},{4,5},{5,6},{6,7},{7,4},{8,9},{9,10},{10,1... | collective-permute-start | bytes 7864328 | tf_op jit(solution)/shard_map/ppermute | solution.py:119
  384.7 3.9 copy-start.15
  447.6 3.9 copy-start.15
  516.4 131.6 %collective-permute-start.4 = (bf16[2,2,512,8,80]{2,4,1,3,0:T(8,128)(2,1)}, bf16[2,2,512,8,80]{2,4,1,3,0:T(8,128)(2,1)}, u32[]{:S(2)}, u32[]{:S(2)}) collective-permute-start(bf16[2,2,512,8,80]{2,4,1,3,0:T(8,128)(2,1)} %add_convert_fusion.2), channel_id=1, source_target_pairs={{0,1},{1,2},{2,3},{3,0},{4,5},{5,6},{6,7},{7,4},{8,9},{9,10},{10,1... | collective-permute-start | bytes 7864328 | tf_op jit(solution)/shard_map/ppermute | solution.py:119
  522.0 4.0 copy-start.17
  585.0 4.0 copy-start.17
  653.8 129.1 %collective-permute-start.5 = (bf16[2,2,512,8,80]{2,4,1,3,0:T(8,128)(2,1)}, bf16[2,2,512,8,80]{2,4,1,3,0:T(8,128)(2,1)}, u32[]{:S(2)}, u32[]{:S(2)}) collective-permute-start(bf16[2,2,512,8,80]{2,4,1,3,0:T(8,128)(2,1)} %add_convert_fusion.1), channel_id=1, source_target_pairs={{0,1},{1,2},{2,3},{3,0},{4,5},{5,6},{6,7},{7,4},{8,9},{9,10},{10,1... | collective-permute-start | bytes 7864328 | tf_op jit(solution)/shard_map/ppermute | solution.py:119
  657.0 4.0 copy-start.19
  715.1 4.8 copy-start.20
  719.9 4.0 copy-start.19
  778.1 4.9 copy-start.20
  782.9 5.9 copy-start.36
  782.9 5.9 copy-start.43
  787.4 55.6 %collective-permute-start.6 = (bf16[2,2,512,8,80]{2,4,1,3,0:T(8,128)(2,1)S(1)}, bf16[2,2,512,8,80]{2,4,1,3,0:T(8,128)(2,1)S(1)}, u32[]{:S(2)}, u32[]{:S(2)}) collective-permute-start(bf16[2,2,512,8,80]{2,4,1,3,0:T(8,128)(2,1)S(1)} %add_convert_fusion), channel_id=1, source_target_pairs={{0,1},{1,2},{2,3},{3,0},{4,5},{5,6},{6,7},{7,4},{8,9},{9,10},{10,1... | collective-permute-start | bytes 7864328 | tf_op jit(solution)/shard_map/ppermute | solution.py:119
  1133.1 4.0 copy-start.42
  (186 other events, 456.9 us)
Sparse Core Ops, SparseCore 0:
  848.8 284.1 all-reduce.3
where the time goes:
time: 1160 us; the launch traced here: 1150 us
  matrix products  528 us (46%)
  waiting for transfers between devices  238 us (21%)
  local copies, waits for them, and re-layouts  182 us (16%)
  blocking collectives  86.7 us (7%)
  other arithmetic  76.1 us (7%)
  starting transfers between devices  20 us (2%)
  between operations  14.8 us (1%)
    psum x1, waiting for transfers between devices, device_step(): lax.psum((grad_gamma, grad_beta, grad_wq, grad_wkv, grad_wo, grad_bo), ('...  187 us
    dot_general x32, matrix products, bwd_rows(): jnp.einsum('hrk,hrd->khd', d_scores, q_rows, preferred_element_type=jnp.f...  101 us
    dot_general x32, matrix products, bwd_rows(): jnp.einsum('hrk,hrd->khd', prob_rows.astype(jnp.bfloat16), do_rows, prefe...  95.3 us
    psum x1, blocking collectives, device_step(): lax.psum((grad_gamma, grad_beta, grad_wq, grad_wkv, grad_wo, grad_bo), ('...  86.7 us
    dot_general x32, matrix products, bwd_rows(): jnp.einsum('hrd,khd->hrk', do_rows, kv_sample[1], preferred_element_type=...  83.6 us
    squeeze x64, local copies, waits for them, and re-layouts, device_step(): lax.map(fwd_sample, (q_blk, run_max, run_sum, run_acc, kv_cur))  77.7 us
    dot_general x32, matrix products, fwd_rows(): jnp.einsum('hrk,khd->hrd', prob_rows.astype(jnp.bfloat16), kv_sample[1],...  67 us
    dot_general x32, matrix products, bwd_rows(): jnp.einsum('hrk,khd->hrd', d_scores, kv_sample[0], preferred_element_type...  56.8 us
  transfers between devices with their start and end apart: 8, of which 3 were waited for; matrix products, arithmetic and copies ran while one was open for 48% of the time, Pallas kernels for 0%

commit v1 on v0

v1 whole, which is shorter than its diff:
```python
import functools
import math
import jax
import jax.numpy as jnp
from jax import lax
from jax.experimental import pallas as pl
from jax.experimental.pallas import tpu as pltpu
from jax.sharding import PartitionSpec as P

LN_EPS = 1e-5
KEY_TILE = 256
BF = jnp.bfloat16
F32 = jnp.float32


def dot_nn(lhs, rhs):
    return lax.dot_general(lhs, rhs, (((1,), (0,)), ((), ())), preferred_element_type=F32)


def dot_nt(lhs, rhs):
    return lax.dot_general(lhs, rhs, (((1,), (1,)), ((), ())), preferred_element_type=F32)


def dot_tn(lhs, rhs):
    return lax.dot_general(lhs, rhs, (((0,), (0,)), ((), ())), preferred_element_type=F32)


def attention_body(scale, qt_ref, kt_ref, vt_ref, do_ref, ot_ref, dq_ref, dk_ref, dv_ref,
                   k_s, v_s, s_s, p_s, ds_s, dk_acc, dv_acc):
    step = pl.program_id(1)
    rows = qt_ref.shape[1]
    tokens = kt_ref.shape[1]
    tiles = tokens // KEY_TILE
    log2_scale = scale * math.log2(math.e)

    @pl.when(step == 0)
    def _():
        k_s[...] = kt_ref[...].T
        v_s[...] = vt_ref[...].T
        dk_acc[...] = jnp.zeros_like(dk_acc)
        dv_acc[...] = jnp.zeros_like(dv_acc)

    q_t = qt_ref[...]
    do_t = do_ref[...]
    top = None
    for tile in range(tiles):
        keys = pl.ds(tile * KEY_TILE, KEY_TILE)
        scores = dot_nn(k_s[keys, :], q_t)
        s_s[keys, :] = scores
        part = jnp.max(scores.reshape(KEY_TILE // 8, 8, rows), axis=0)
        top = part if top is None else jnp.maximum(top, part)
    top = jnp.max(top, axis=0, keepdims=True) * log2_scale
    total = None
    for tile in range(tiles):
        keys = pl.ds(tile * KEY_TILE, KEY_TILE)
        probs = jnp.exp2(s_s[keys, :] * log2_scale - top)
        s_s[keys, :] = probs
        part = jnp.sum(probs.reshape(KEY_TILE // 8, 8, rows), axis=0)
        total = part if total is None else total + part
    recip = 1.0 / jnp.sum(total, axis=0, keepdims=True)
    for tile in range(tiles):
        keys = pl.ds(tile * KEY_TILE, KEY_TILE)
        p_s[keys, :] = (s_s[keys, :] * recip).astype(BF)
    out_t = dot_nn(vt_ref[...], p_s[...])
    ot_ref[...] = out_t.astype(BF)
    delta = jnp.sum(out_t * do_t.astype(F32), axis=0, keepdims=True)
    dv_acc[...] += dot_nt(do_t, p_s[...])
    for tile in range(tiles):
        keys = pl.ds(tile * KEY_TILE, KEY_TILE)
        d_probs = dot_nn(v_s[keys, :], do_t)
        ds_s[keys, :] = ((s_s[keys, :] * recip) * (d_probs - delta)).astype(BF)
    dq_ref[...] = (dot_nn(kt_ref[...], ds_s[...]) * scale).astype(BF)
    dk_acc[...] += dot_nt(q_t, ds_s[...])

    @pl.when(step == pl.num_programs(1) - 1)
    def _():
        dk_ref[...] = (dk_acc[...] * scale).astype(BF)
        dv_ref[...] = dv_acc[...].astype(BF)


def attention(q_t, k_t, v_t, do_t, head_dim, block=256):
    width, tokens = q_t.shape
    heads = width // head_dim
    row_spec = pl.BlockSpec((head_dim, block), lambda h, j: (h, j))
    full_spec = pl.BlockSpec((head_dim, tokens), lambda h, j: (h, 0))
    flops = 12 * heads * tokens * tokens * head_dim
    return pl.pallas_call(
        functools.partial(attention_body, head_dim ** -0.5),
        grid=(heads, tokens // block),
        in_specs=[row_spec, full_spec, full_spec, row_spec],
        out_specs=[row_spec, row_spec, full_spec, full_spec],
        out_shape=[jax.ShapeDtypeStruct((width, tokens), BF)] * 4,
        scratch_shapes=[pltpu.VMEM((tokens, head_dim), BF)] * 2 + [pltpu.VMEM((tokens, block), F32)]
        + [pltpu.VMEM((tokens, block), BF)] * 2 + [pltpu.VMEM((head_dim, tokens), F32)] * 2,
        compiler_params=pltpu.CompilerParams(vmem_limit_bytes=40 * 2 ** 20),
        cost_estimate=pl.CostEstimate(flops=flops, bytes_accessed=16 * width * tokens, transcendentals=heads * tokens * tokens),
        name='attention',
    )(q_t, k_t, v_t, do_t)


def solution(mesh):
    dp_size = mesh.shape['dp']
    cp_size = mesh.shape['cp']
    axes = ('dp', 'cp')
    act_spec = P('dp', 'cp', None)
    rep_spec = P()

    def index_of(dp, cp):
        return dp * cp_size + cp

    send_same, send_cross, swap = [], [], []
    for dp in range(dp_size):
        group, core = dp // 2, dp % 2
        for cp in range(cp_size):
            half, parity = cp // 2, cp % 2
            send_same.append((index_of(dp, cp), index_of(2 * group + half, 2 * core + parity)))
            send_cross.append((index_of(dp, cp), index_of(2 * group + half, 2 * core + 1 - parity)))
            swap.append((index_of(dp, cp), index_of(dp ^ 1, cp)))
    back_same = [(dst, src) for src, dst in send_same]
    back_cross = [(dst, src) for src, dst in send_cross]

    def device_step(x_in, grad_y, ln_gamma, ln_beta, w_q, w_k, w_v, w_o, b_o):
        channels = x_in.shape[2]
        num_heads, head_dim = w_q.shape[1], w_q.shape[2]
        half_heads = num_heads // 2
        width = half_heads * head_dim
        core = lax.rem(lax.axis_index('dp'), 2)
        parity = lax.rem(lax.axis_index('cp'), 2)

        def permute(value, pairs):
            return lax.ppermute(value, axes, pairs)

        def gather_image(band_pair):
            first = lax.dynamic_index_in_dim(band_pair, parity, 0, keepdims=False)
            second = lax.dynamic_index_in_dim(band_pair, 1 - parity, 0, keepdims=False)
            own_a, own_b = permute(first, send_same), permute(second, send_cross)
            return own_a, own_b, permute(own_a, swap), permute(own_b, swap)

        def scatter_image(own):
            half = own.shape[0] // 2
            same, cross = permute(own[:half], back_same), permute(own[half:], back_cross)
            return jnp.where(parity == 0, jnp.stack([same, cross]), jnp.stack([cross, same]))

        def head_slice(weight, which):
            return lax.dynamic_slice_in_dim(weight, which * half_heads, half_heads, 1).reshape(channels, width)

        def out_slice(which):
            return lax.dynamic_slice_in_dim(w_o, which * half_heads, half_heads, 0).reshape(width, channels)

        x_parts = gather_image(x_in)
        dy_parts = gather_image(grad_y)
        x_all = jnp.concatenate(x_parts, axis=0)
        dy_all = jnp.concatenate(dy_parts, axis=0)
        tokens = x_all.shape[0]
        own = tokens // 2

        x_f = x_all.astype(F32)
        mean = jnp.mean(x_f, axis=-1, keepdims=True)
        centered = x_f - mean
        inv_std = lax.rsqrt(jnp.mean(centered * centered, axis=-1, keepdims=True) + LN_EPS)
        normed = (centered * inv_std * ln_gamma + ln_beta).astype(BF)

        wq_mine, wk_mine, wv_mine = (head_slice(w, core) for w in (w_q, w_k, w_v))
        wq_other, wk_other, wv_other = (head_slice(w, 1 - core) for w in (w_q, w_k, w_v))
        wo_mine, wo_other = out_slice(core), out_slice(1 - core)

        def project(weight):
            return lax.dot_general(weight, normed, (((0,), (1,)), ((), ())), preferred_element_type=F32).astype(BF)

        q_t, k_t, v_t = project(wq_mine), project(wk_mine), project(wv_mine)
        do_t = dot_nt(wo_mine, dy_all).astype(BF)
        o_t, dq_t, dk_t, dv_t = attention(q_t, k_t, v_t, do_t, head_dim)

        o_peer = permute(o_t[:, own:], swap)
        y_f = x_all[:own].astype(F32) + (dot_tn(o_t[:, :own], wo_mine) + dot_tn(o_peer, wo_other)) + b_o
        y_out = scatter_image(y_f.astype(BF))

        dqkv_t = jnp.concatenate([dq_t, dk_t, dv_t], axis=0)
        dqkv_peer = permute(dqkv_t[:, own:], swap)
        w_mine = jnp.concatenate([wq_mine, wk_mine, wv_mine], axis=1)
        w_other = jnp.concatenate([wq_other, wk_other, wv_other], axis=1)
        d_normed = (lax.dot_general(dqkv_t[:, :own], w_mine, (((0,), (1,)), ((), ())), preferred_element_type=F32)
                    + lax.dot_general(dqkv_peer, w_other, (((0,), (1,)), ((), ())), preferred_element_type=F32))
        d_normed = d_normed.astype(BF).astype(F32)
        x_hat = centered[:own] * inv_std[:own]
        d_hat = d_normed * ln_gamma
        mean_one = jnp.mean(d_hat, axis=-1, keepdims=True)
        mean_two = jnp.mean(d_hat * x_hat, axis=-1, keepdims=True)
        dx = inv_std[:own] * (d_hat - mean_one - x_hat * mean_two)
        dx = (dy_all[:own].astype(F32) + dx).astype(BF)
        grad_x = scatter_image(dx)

        small = jnp.stack([jnp.sum(d_normed * x_hat, axis=0), jnp.sum(d_normed, axis=0),
                           jnp.sum(dy_all[:own].astype(F32), axis=0)])
        d_w = jnp.concatenate([dot_nn(dqkv_t, normed), dot_nn(o_t, dy_all)], axis=0)
        d_w = d_w.reshape(4, 1, width, channels)
        zero = jnp.zeros_like(d_w)
        both = jnp.where(core == 0, jnp.concatenate([d_w, zero], 1), jnp.concatenate([zero, d_w], 1))
        both, small = lax.psum((both, small), axes)
        both = both.reshape(4, num_heads, head_dim, channels)
        grads = [jnp.transpose(both[i], (2, 0, 1)) for i in range(3)]
        return (y_out, grad_x, small[0], small[1], grads[0], grads[1], grads[2], both[3], small[2])

    return jax.shard_map(device_step, mesh=mesh,
                         in_specs=(act_spec, act_spec) + (rep_spec,) * 7,
                         out_specs=(act_spec, act_spec) + (rep_spec,) * 7,
                         check_vma=False)
```

time: 1160 us -> 440 us (0.38)
  matrix products: 528 us -> 21.6 us
  local copies, waits for them, and re-layouts: 182 us -> 20.1 us
  Pallas kernels: 0 us -> 71.4 us
  waiting for transfers between devices: 238 us -> 181 us
  other arithmetic: 76.1 us -> 24.2 us
    dot_general x233 -> x10, matrix products: 528 us -> 21.6 us  [the longest x2 4.39 us: dot_nn(): lax.dot_general(lhs, rhs, (((1,), (0,)), ((), ())), preferred_element_typ...]
    squeeze x65 -> x2, local copies, waits for them, and re-layouts: 81.7 us -> 3.71 us  [the longest x1 2.55 us: gather_image(): first = lax.dynamic_index_in_dim(band_pair, parity, 0, keepdims=False)]
    pallas_call x0 -> x1, Pallas kernels: none -> 71.4 us  [attention(): pl.pallas_call(functools.partial(attention_body, head_dim ** (-0.5)), gri...]
    while x347 -> x0, local copies, waits for them, and re-layouts: 34.9 us -> none
    psum x1, waiting for transfers between devices: 187 us -> 155 us  [device_step(): both, small = lax.psum((both, small), axes)]
    dynamic_update_slice x24 -> x0, local copies, waits for them, and re-layouts: 31.2 us -> none  [device_step(): lax.map(fwd_sample, (q_blk, run_max, run_sum, run_acc, kv_cur))]
    dynamic_update_slice x40 -> x0, other arithmetic: 28.6 us -> none  [the longest x8 28.1 us: device_step(): lax.map(bwd_sample, (q_blk, d_out, log_norm, row_delta, dq_acc, kv_cur))]
    ppermute x7 -> x14, waiting for transfers between devices: 50.5 us -> 26.6 us  [permute(): return lax.ppermute(value, axes, pairs)]
  transfers between devices with their start and end apart: 8 -> 15, of which waited for: 3 -> 6; matrix products, arithmetic and copies ran while one was open for 48% -> 11% of each run, Pallas kernels for 0% -> 0%
where the time goes in v1:
time: 440 us; the launch traced here: 439 us
  waiting for transfers between devices  181 us (41%)
  blocking collectives  83.9 us (19%)
  Pallas kernels  71.4 us (16%)
  other arithmetic  24.2 us (6%)
  starting transfers between devices  22 us (5%)
  matrix products  21.6 us (5%)
  local copies, waits for them, and re-layouts  20.1 us (5%)
  between operations  14.6 us (3%)
    psum x1, waiting for transfers between devices, device_step(): both, small = lax.psum((both, small), axes)  155 us
    psum x1, blocking collectives, device_step(): both, small = lax.psum((both, small), axes)  83.9 us
    pallas_call x1, Pallas kernels, attention(): pl.pallas_call(functools.partial(attention_body, head_dim ** (-0.5)), gri...  71.4 us
    ppermute x14, waiting for transfers between devices, permute(): return lax.ppermute(value, axes, pairs)  26.6 us
    ppermute x14, starting transfers between devices, permute(): return lax.ppermute(value, axes, pairs)  22 us
  transfers between devices with their start and end apart: 15, of which 6 were waited for; matrix products, arithmetic and copies ran while one was open for 11% of the time, Pallas kernels for 0%

profile of v1, /device:TPU:1, one launch (start us, length us, event | category | flops | bytes accessed | tf_op | source)
XLA Modules:
  0.0 438.9 jit_solution(16605623148068960308)
XLA Ops:
  7.2 2.5 dynamic-slice_bitcast_fusion.3
  9.8 6.0 %collective-permute-start = (bf16[512,640]{1,0:T(8,128)(2,1)}, bf16[512,640]{1,0:T(8,128)(2,1)S(1)}, u32[]{:S(2)}, u32[]{:S(2)}) collective-permute-start(bf16[512,640]{1,0:T(8,128)(2,1)} %get-tuple-element.38), channel_id=1, source_target_pairs={{0,0},{1,1},{2,4},{3,5},{4,2},{5,3},{6,6},{7,7},{8,8},{9,9},{10,12... | collective-permute-start | bytes 1966088 | tf_op jit(solution)/shard_map/ppermute | solution.py:131
  17.7 2.4 collective-permute-start.5
  22.0 9.1 %collective-permute-done = bf16[512,640]{1,0:T(8,128)(2,1)S(1)} collective-permute-done((bf16[512,640]{1,0:T(8,128)(2,1)}, bf16[512,640]{1,0:T(8,128)(2,1)S(1)}, u32[]{:S(2)}, u32[]{:S(2)}) %collective-permute-start) | collective-permute-done | bytes 655392 | tf_op jit(solution)/shard_map/ppermute | solution.py:131
  31.1 3.1 collective-permute-done.1
  38.2 2.6 constant_dynamic-slice_fusion
  40.8 5.9 %collective-permute-done.5 = bf16[512,640]{1,0:T(8,128)(2,1)S(1)} collective-permute-done((bf16[512,640]{1,0:T(8,128)(2,1)}, bf16[512,640]{1,0:T(8,128)(2,1)S(1)}, u32[]{:S(2)}, u32[]{:S(2)}) %collective-permute-start.5) | collective-permute-done | bytes 655392 | tf_op jit(solution)/shard_map/ppermute | solution.py:131
  47.4 3.1 convert_reduce_fusion
  50.5 5.3 %convert_subtract_fusion = (f32[2048,640]{1,0:T(8,128)}, f32[2048]{0:T(1024)S(1)}) fusion(f32[2048]{0:T(1024)S(1)} %broadcast_multiply_fusion, bf16[512,640]{1,0:T(8,128)(2,1)S(1)} %collective-permute-done.3, bf16[512,640]{1,0:T(8,128)(2,1)S(1)} %collective-permute-done.2, bf16[512,640]{1,0:T(8,128)(2,1)S(1)} %collective-permute-done.1, ...), kind=kLoop, calls=%fused_computation.1 | loop fusion | flops 14415872 | bytes 7880704 | tf_op jit(solution)/shard_map/sub | solution.py:159
  55.9 5.1 %add_convert_fusion = bf16[2048,640]{1,0:T(8,128)(2,1)S(1)} fusion(f32[640]{0:T(1024)S(1)} %copy-done.13, f32[640]{0:T(1024)S(1)} %copy-done.12, f32[2048]{0:T(1024)S(1)} %add_rsqrt_fusion, f32[2048]{0:T(1024)S(1)} %broadcast_multiply_fusion, bf16[512,640]{1,0:T(8,128)(2,1)S(1)} %collective-permute-done.3, bf16[512,640]{1,0:T(8,128)(2,1)S(1)} %collective-permute-done.2, ...), kind=kLoop, calls=%fused_computation.3 | loop fusion | flops 17039360 | bytes 5264384 | tf_op jit(solution)/shard_map/convert_element_type | solution.py:161
  66.1 71.4 %attention.1 = (bf16[320,2048]{1,0:T(8,128)(2,1)S(1)}, bf16[320,2048]{1,0:T(8,128)(2,1)S(1)}, bf16[320,2048]{1,0:T(8,128)(2,1)S(1)}, bf16[320,2048]{1,0:T(8,128)(2,1)S(1)}) custom-call(bf16[320,2048]{1,0:T(8,128)(2,1)S(1)} %convolution_convert_fusion.3.qt_ref, bf16[320,2048]{1,0:T(8,128)(2,1)S(1)} %convolution_convert_fusion.2.kt_ref, ...), custom_call_target="tpu_custom_call" | custom-call | flops 16106127360 | bytes 10485760 | tf_op jit(solution)/shard_map/attention/pallas_call | solution.py:87
  139.9 3.2 fusion.27
  145.4 3.2 pad_select_fusion
  150.7 3.8 fusion.8
  154.6 2.2 add_convert_fusion.2
  157.0 3.0 collective-permute-start.9
  162.2 4.2 fusion.7
  168.3 3.2 collective-permute-start.12
  173.1 7.7 %collective-permute-done.9 = bf16[512,640]{1,0:T(8,128)(2,1)} collective-permute-done((bf16[512,640]{1,0:T(8,128)(2,1)S(1)}, bf16[512,640]{1,0:T(8,128)(2,1)}, u32[]{:S(2)}, u32[]{:S(2)}) %collective-permute-start.9) | collective-permute-done | bytes 655392 | tf_op jit(solution)/shard_map/ppermute | solution.py:131
  181.6 3.0 maximum_select_fusion
  184.6 83.9 %psum.14 = f32[3,640]{1,0:T(4,128)S(1)} all-reduce(f32[3,640]{1,0:T(4,128)S(1)} %pad_maximum_fusion.3), channel_id=1, replica_groups=mesh['dp'=64,'cp'=4] {'dp','cp'}, use_global_device_ids=true, to_apply=%region_7.8 | all-reduce | flops 1920 | bytes 15360 | tf_op jit(solution)/shard_map/psum | solution.py:199
  269.1 2.6 maximum_select_fusion.1
  271.7 154.5 %all-reduce.4.cloned.1.call-done = f32[4,2,320,640]{3,2,0,1:T(8,128)} async-done(((f32[4,2,320,640]{3,2,0,1:T(8,128)}), f32[4,2,320,640]{3,2,0,1:T(8,128)}) %all-reduce.4.cloned.1.call-update) | async-done | bytes 6553616 | tf_op jit(solution)/shard_map/psum | solution.py:199
  426.3 5.8 %fusion.24 = (f32[1,2,320,640]{3,2,0,1:T(8,128)}, f32[1,2,320,640]{3,2,0,1:T(8,128)}, f32[1,2,320,640]{3,2,0,1:T(8,128)}, f32[1,2,320,640]{3,2,0,1:T(8,128)}) fusion(f32[4,2,320,640]{3,2,0,1:T(8,128)} %all-reduce.4.cloned.1.call-done), kind=kLoop, calls=%fused_computation.73 | loop fusion | bytes 13107200 | tf_op jit(solution)/shard_map/slice | solution.py:202
  (89 shorter events, 27.4 us)
Async XLA Ops:
  7.2 9.3 %copy-start.5 = (bf16[2,512,640]{2,1,0:T(8,128)(2,1)S(1)}, bf16[2,512,640]{2,1,0:T(8,128)(2,1)}, u32[]{:S(2)}) copy-start(bf16[2,512,640]{2,1,0:T(8,128)(2,1)} %param.10) | copy-start | bytes 3932164
  7.2 419.1 %all-reduce.4.cloned.1.call-start = ((), (), s32[]{:S(2)}) async-start(), calls=%async_computation | async-start | bytes 13107200 | tf_op jit(solution)/shard_map/psum | solution.py:199
  9.8 21.3 %collective-permute-start = (bf16[512,640]{1,0:T(8,128)(2,1)}, bf16[512,640]{1,0:T(8,128)(2,1)S(1)}, u32[]{:S(2)}, u32[]{:S(2)}) collective-permute-start(bf16[512,640]{1,0:T(8,128)(2,1)} %get-tuple-element.38), channel_id=1, source_target_pairs={{0,0},{1,1},{2,4},{3,5},{4,2},{5,3},{6,6},{7,7},{8,8},{9,9},{10,12... | collective-permute-start | bytes 1966088 | tf_op jit(solution)/shard_map/ppermute | solution.py:131
  15.8 18.3 %collective-permute-start.1 = (bf16[512,640]{1,0:T(8,128)(2,1)}, bf16[512,640]{1,0:T(8,128)(2,1)S(1)}, u32[]{:S(2)}, u32[]{:S(2)}) collective-permute-start(bf16[512,640]{1,0:T(8,128)(2,1)} %get-tuple-element.39), channel_id=1, source_target_pairs={{0,1},{1,0},{2,5},{3,4},{4,3},{5,2},{6,7},{7,6},{8,9},{9,8},{10,13... | collective-permute-start | bytes 1966088 | tf_op jit(solution)/shard_map/ppermute | solution.py:131
  17.7 29.0 %collective-permute-start.5 = (bf16[512,640]{1,0:T(8,128)(2,1)}, bf16[512,640]{1,0:T(8,128)(2,1)S(1)}, u32[]{:S(2)}, u32[]{:S(2)}) collective-permute-start(bf16[512,640]{1,0:T(8,128)(2,1)} %get-tuple-element.36), channel_id=1, source_target_pairs={{0,1},{1,0},{2,5},{3,4},{4,3},{5,2},{6,7},{7,6},{8,9},{9,8},{10,13... | collective-permute-start | bytes 1966088 | tf_op jit(solution)/shard_map/ppermute | solution.py:131
  20.0 26.6 %collective-permute-start.4 = (bf16[512,640]{1,0:T(8,128)(2,1)}, bf16[512,640]{1,0:T(8,128)(2,1)S(1)}, u32[]{:S(2)}, u32[]{:S(2)}) collective-permute-start(bf16[512,640]{1,0:T(8,128)(2,1)} %get-tuple-element.37), channel_id=1, source_target_pairs={{0,0},{1,1},{2,4},{3,5},{4,2},{5,3},{6,6},{7,7},{8,8},{9,9},{10,12... | collective-permute-start | bytes 1966088 | tf_op jit(solution)/shard_map/ppermute | solution.py:131
  31.1 16.3 %collective-permute-start.2 = (bf16[512,640]{1,0:T(8,128)(2,1)S(1)}, bf16[512,640]{1,0:T(8,128)(2,1)S(1)}, u32[]{:S(2)}, u32[]{:S(2)}) collective-permute-start(bf16[512,640]{1,0:T(8,128)(2,1)S(1)} %collective-permute-done), channel_id=1, source_target_pairs={{0,4},{1,5},{2,6},{3,7},{4,0},{5,1},{6,2},{7,3},{8,12},{9,13},{10,... | collective-permute-start | bytes 1966088 | tf_op jit(solution)/shard_map/ppermute | solution.py:131
  34.2 13.2 %collective-permute-start.3 = (bf16[512,640]{1,0:T(8,128)(2,1)S(1)}, bf16[512,640]{1,0:T(8,128)(2,1)S(1)}, u32[]{:S(2)}, u32[]{:S(2)}) collective-permute-start(bf16[512,640]{1,0:T(8,128)(2,1)S(1)} %collective-permute-done.1), channel_id=1, source_target_pairs={{0,4},{1,5},{2,6},{3,7},{4,0},{5,1},{6,2},{7,3},{8,12},{9,13},{10,... | collective-permute-start | bytes 1966088 | tf_op jit(solution)/shard_map/ppermute | solution.py:131
  36.1 27.4 %copy-start.11 = (bf16[640,4,80]{0,2,1:T(8,128)(2,1)}, bf16[640,4,80]{0,2,1:T(8,128)(2,1)S(1)}, u32[]{:S(2)}) copy-start(bf16[640,4,80]{0,2,1:T(8,128)(2,1)S(1)} %get-tuple-element.41) | copy-start | bytes 1228804
  38.2 26.7 %copy-start.3 = (bf16[4,80,640]{2,1,0:T(8,128)(2,1)}, bf16[4,80,640]{2,1,0:T(8,128)(2,1)S(1)}, u32[]{:S(2)}) copy-start(bf16[4,80,640]{2,1,0:T(8,128)(2,1)S(1)} %get-tuple-element.47) | copy-start | bytes 1228804
  40.8 20.2 %copy-start.8 = (bf16[640,4,80]{0,2,1:T(8,128)(2,1)}, bf16[640,4,80]{0,2,1:T(8,128)(2,1)S(1)}, u32[]{:S(2)}) copy-start(bf16[640,4,80]{0,2,1:T(8,128)(2,1)S(1)} %get-tuple-element.45) | copy-start | bytes 1228804
  40.8 21.6 %copy-start.9 = (bf16[640,4,80]{0,2,1:T(8,128)(2,1)}, bf16[640,4,80]{0,2,1:T(8,128)(2,1)S(1)}, u32[]{:S(2)}) copy-start(bf16[640,4,80]{0,2,1:T(8,128)(2,1)S(1)} %get-tuple-element.49) | copy-start | bytes 1228804
  46.7 18.1 %collective-permute-start.7 = (bf16[512,640]{1,0:T(8,128)(2,1)S(1)}, bf16[512,640]{1,0:T(8,128)(2,1)S(1)}, u32[]{:S(2)}, u32[]{:S(2)}) collective-permute-start(bf16[512,640]{1,0:T(8,128)(2,1)S(1)} %collective-permute-done.5), channel_id=1, source_target_pairs={{0,4},{1,5},{2,6},{3,7},{4,0},{5,1},{6,2},{7,3},{8,12},{9,13},{10,... | collective-permute-start | bytes 1966088 | tf_op jit(solution)/shard_map/ppermute | solution.py:131
  46.7 15.5 %collective-permute-start.6 = (bf16[512,640]{1,0:T(8,128)(2,1)S(1)}, bf16[512,640]{1,0:T(8,128)(2,1)S(1)}, u32[]{:S(2)}, u32[]{:S(2)}) collective-permute-start(bf16[512,640]{1,0:T(8,128)(2,1)S(1)} %collective-permute-done.4), channel_id=1, source_target_pairs={{0,4},{1,5},{2,6},{3,7},{4,0},{5,1},{6,2},{7,3},{8,12},{9,13},{10,... | collective-permute-start | bytes 1966088 | tf_op jit(solution)/shard_map/ppermute | solution.py:131
  144.6 9.9 %collective-permute-start.8 = (bf16[320,1024]{1,0:T(8,128)(2,1)}, bf16[320,1024]{1,0:T(8,128)(2,1)}, u32[]{:S(2)}, u32[]{:S(2)}) collective-permute-start(bf16[320,1024]{1,0:T(8,128)(2,1)} %slice.63), channel_id=1, source_target_pairs={{0,4},{1,5},{2,6},{3,7},{4,0},{5,1},{6,2},{7,3},{8,12},{9,13},{10,... | collective-permute-start | bytes 1966088 | tf_op jit(solution)/shard_map/ppermute | solution.py:131
  144.9 17.3 %collective-permute-start.11 = (bf16[960,1024]{1,0:T(8,128)(2,1)}, bf16[960,1024]{1,0:T(8,128)(2,1)}, u32[]{:S(2)}, u32[]{:S(2)}) collective-permute-start(bf16[960,1024]{1,0:T(8,128)(2,1)} %slice.83), channel_id=1, source_target_pairs={{0,4},{1,5},{2,6},{3,7},{4,0},{5,1},{6,2},{7,3},{8,12},{9,13},{10,... | collective-permute-start | bytes 5898248 | tf_op jit(solution)/shard_map/ppermute | solution.py:131
  148.6 13.6 %slice-start = ((s8[5242880]{0:T(1024)(128)(4,1)}), s8[4194304]{0:T(1024)(128)(4,1)S(1)}, s32[]{:S(2)}) async-start(s8[5242880]{0:T(1024)(128)(4,1)} %bitcast.48), calls=%async_computation.1 | async-start | bytes 8388608
  150.7 11.5 %slice-start.1 = ((s8[5242880]{0:T(1024)(128)(4,1)}), s8[1048576]{0:T(1024)(128)(4,1)S(1)}, s32[]{:S(2)}) async-start(s8[5242880]{0:T(1024)(128)(4,1)} %bitcast.48), calls=%async_computation.2 | async-start | bytes 2097152
  156.8 5.4 %copy-start.6 = (bf16[640,4,80]{0,2,1:T(8,128)(2,1)S(1)}, bf16[640,4,80]{0,2,1:T(8,128)(2,1)}, u32[]{:S(2)}) copy-start(bf16[640,4,80]{0,2,1:T(8,128)(2,1)} %get-tuple-element.44) | copy-start | bytes 1228804
  156.8 5.4 %copy-start.7 = (bf16[640,4,80]{0,2,1:T(8,128)(2,1)S(1)}, bf16[640,4,80]{0,2,1:T(8,128)(2,1)}, u32[]{:S(2)}) copy-start(bf16[640,4,80]{0,2,1:T(8,128)(2,1)} %get-tuple-element.50) | copy-start | bytes 1228804
  157.0 23.9 %collective-permute-start.9 = (bf16[512,640]{1,0:T(8,128)(2,1)S(1)}, bf16[512,640]{1,0:T(8,128)(2,1)}, u32[]{:S(2)}, u32[]{:S(2)}) collective-permute-start(bf16[512,640]{1,0:T(8,128)(2,1)S(1)} %get-tuple-element.34), channel_id=1, source_target_pairs={{0,0},{1,1},{4,2},{5,3},{2,4},{3,5},{6,6},{7,7},{8,8},{9,9},{12,10... | collective-permute-start | bytes 1966088 | tf_op jit(solution)/shard_map/ppermute | solution.py:131
  160.0 21.6 %collective-permute-start.10 = (bf16[512,640]{1,0:T(8,128)(2,1)S(1)}, bf16[512,640]{1,0:T(8,128)(2,1)}, u32[]{:S(2)}, u32[]{:S(2)}) collective-permute-start(bf16[512,640]{1,0:T(8,128)(2,1)S(1)} %get-tuple-element.35), channel_id=1, source_target_pairs={{1,0},{0,1},{5,2},{4,3},{3,4},{2,5},{7,6},{6,7},{9,8},{8,9},{13,10... | collective-permute-start | bytes 1966088 | tf_op jit(solution)/shard_map/ppermute | solution.py:131
  168.3 100.8 %collective-permute-start.12 = (bf16[512,640]{1,0:T(8,128)(2,1)S(1)}, bf16[512,640]{1,0:T(8,128)(2,1)S(1)}, u32[]{:S(2)}, u32[]{:S(2)}) collective-permute-start(bf16[512,640]{1,0:T(8,128)(2,1)S(1)} %get-tuple-element.32), channel_id=1, source_target_pairs={{0,0},{1,1},{4,2},{5,3},{2,4},{3,5},{6,6},{7,7},{8,8},{9,9},{12,10... | collective-permute-start | bytes 1966088 | tf_op jit(solution)/shard_map/ppermute | solution.py:131
  171.6 97.5 %collective-permute-start.13 = (bf16[512,640]{1,0:T(8,128)(2,1)S(1)}, bf16[512,640]{1,0:T(8,128)(2,1)}, u32[]{:S(2)}, u32[]{:S(2)}) collective-permute-start(bf16[512,640]{1,0:T(8,128)(2,1)S(1)} %get-tuple-element.33), channel_id=1, source_target_pairs={{1,0},{0,1},{5,2},{4,3},{3,4},{2,5},{7,6},{6,7},{9,8},{8,9},{13,10... | collective-permute-start | bytes 1966088 | tf_op jit(solution)/shard_map/ppermute | solution.py:131
  (8 other events, 35.1 us)
Sparse Core Ops, SparseCore 0:
  148.7 277.5 all-reduce.3

commit v2 on v1

--- a/solution.py
+++ b/solution.py
@@ -98,6 +98,194 @@
     )(q_t, k_t, v_t, do_t)
 
 
+MESH = pl.DeviceIdType.MESH
+RING = 4
+
+
+def ring_copies(src, relay, fin, sems, axis_pos, device_of, split, rows):
+    send, recv = sems
+    right, left, across = (lax.rem(axis_pos + k, RING) for k in (1, RING - 1, 2))
+    low, high = pl.ds(0, split), pl.ds(split, rows - split)
+
+    def copy(k, source, target, where):
+        return pltpu.make_async_remote_copy(src_ref=source, dst_ref=target, send_sem=send.at[k], recv_sem=recv.at[k],
+                                            device_id=device_of(where), device_id_type=MESH)
+
+    return [copy(0, src.at[across, low], relay.at[low], right),
+            copy(1, src.at[across, high], relay.at[high], left),
+            copy(2, src.at[right, high], fin.at[0, high], right),
+            copy(3, src.at[left, low], fin.at[1, low], left),
+            copy(4, relay.at[low], fin.at[0, low], right),
+            copy(5, relay.at[high], fin.at[1, high], left)]
+
+
+def gather_copies(out, first, stride, rows, sems, axis_pos, device_of, split):
+    send, recv = sems
+    right, left = lax.rem(axis_pos + 1, RING), lax.rem(axis_pos + RING - 1, RING)
+
+    def copy(k, block, begin, size, where):
+        part = out.at[pl.ds(pl.multiple_of(first + block * stride + begin, 8), size)]
+        return pltpu.make_async_remote_copy(src_ref=part, dst_ref=part, send_sem=send.at[k], recv_sem=recv.at[k],
+                                            device_id=device_of(where), device_id_type=MESH)
+
+    return [copy(0, axis_pos, 0, rows, right), copy(1, axis_pos, 0, rows, left),
+            copy(2, left, 0, split, right), copy(3, right, split, rows - split, left)]
+
+
+def all_reduce_body(depth, gp_ref, gq_ref, out_ref,
+                    p_relay, p_fin, q_relay, q_fin, p2, q2, p2_relay, p2_fin, q2_relay, q2_fin,
+                    z_src, z_recv, z_out, ring_sems, ag_sems, z_sems, swap_sems):
+    dp, x = lax.axis_index('dp'), lax.axis_index('cp')
+    core = lax.rem(dp, 2)
+    y = lax.rem(dp // 2, RING)
+    z = dp // (2 * RING)
+
+    def at(zz, yy, cc):
+        return (zz * RING + yy) * 2 + cc
+
+    def on_x(pos):
+        return (dp, pos)
+
+    def on_y(pos):
+        return (at(z, pos, core), x)
+
+    def on_z(pos):
+        return (at(pos, y, core), x)
+
+    peer = (at(z, y, 1 - core), x)
+    barrier = pltpu.get_barrier_semaphore()
+    peers = [on_x(lax.rem(x + 1, RING)), on_x(lax.rem(x + RING - 1, RING)),
+             on_y(lax.rem(y + 1, RING)), on_y(lax.rem(y + RING - 1, RING)), peer]
+    peers += [on_z(lax.rem(z + d, depth)) for d in range(1, depth)]
+    for device in peers:
+        pl.semaphore_signal(barrier, inc=1, device_id=device, device_id_type=MESH)
+    pl.semaphore_wait(barrier, len(peers))
+
+    def sems(pool, k):
+        return pool.at[0, k], pool.at[1, k]
+
+    def two_rings(first, second):
+        plans = [ring_copies(src, relay, fin, sm, pos, dev, split, rows)
+                 for src, relay, fin, pos, dev, split, rows, sm in (first, second)]
+        for k in range(4):
+            for plan in plans:
+                plan[k].start()
+        for way, k in ((0, 4), (1, 5)):
+            for plan, (src, relay, fin, pos, dev, split, rows, sm) in zip(plans, (first, second)):
+                part = pl.ds(0, split) if way == 0 else pl.ds(split, rows - split)
+                owner = lax.rem(pos + (1 if way == 0 else RING - 1), RING)
+                plan[way].wait_recv()
+                relay[part] = src[owner, part] + relay[part]
+                plan[k].start()
+        for k in (2, 3, 4, 5):
+            for plan in plans:
+                plan[k].wait_recv()
+        for plan in plans:
+            for copy in plan:
+                copy.wait_send()
+
+    two_rings((gp_ref, p_relay, p_fin, y, on_y, 88, 168, sems(ring_sems, 0)),
+              (gq_ref, q_relay, q_fin, x, on_x, 80, 160, sems(ring_sems, 1)))
+    tail = pl.ds(160, 8)
+    for block in range(RING):
+        rows = pl.ds(block * 40, 40)
+        p2[block, pl.ds(0, 40)] = gp_ref[y, rows] + (p_fin[0, rows] + p_fin[1, rows])
+        p2[block, pl.ds(40, 8)] = gp_ref[y, tail] + (p_fin[0, tail] + p_fin[1, tail])
+        q2[block] = gq_ref[x, rows] + (q_fin[0, rows] + q_fin[1, rows])
+    two_rings((p2, p2_relay, p2_fin, x, on_x, 24, 48, sems(ring_sems, 2)),
+              (q2, q2_relay, q2_fin, y, on_y, 24, 40, sems(ring_sems, 3)))
+    count = 0
+    for src, fin, pos, rows in ((p2, p2_fin, x, 48), (q2, q2_fin, y, 40)):
+        for i in range(rows // 8):
+            r = pl.ds(i * 8, 8)
+            for j in range(5):
+                c = pl.ds(j * 128, 128)
+                z_src[count] = src[pos, r, c] + (fin[0, r, c] + fin[1, r, c])
+                count += 1
+    z_src[count] = jnp.zeros((8, 128), F32)
+    each = 56 // depth
+
+    def z_copy(k, source, target, d):
+        return pltpu.make_async_remote_copy(src_ref=source, dst_ref=target, send_sem=z_sems.at[0, k, d - 1],
+                                            recv_sem=z_sems.at[1, k, d - 1], device_id=on_z(lax.rem(z + d, depth)),
+                                            device_id_type=MESH)
+
+    mine = pl.ds(z * each, each)
+    copies = [z_copy(0, z_src.at[pl.ds(lax.rem(z + d, depth) * each, each)], z_recv.at[d - 1], d)
+              for d in range(1, depth)]
+    for copy in copies:
+        copy.start()
+    total = z_src[mine]
+    for d, copy in enumerate(copies):
+        copy.wait_recv()
+        total = total + z_recv[d]
+    z_out[mine] = total
+    for copy in copies:
+        copy.wait_send()
+    copies = [z_copy(1, z_out.at[mine], z_out.at[mine], d) for d in range(1, depth)]
+    for copy in copies:
+        copy.start()
+    for copy in copies:
+        copy.wait_recv()
+    for copy in copies:
+        copy.wait_send()
+
+    out = out_ref.at[core]
+    p_first, q_first = y * 160, 640 + x * 160
+    count = 0
+    for first, rows in ((p_first + x * 40, 48), (q_first + y * 40, 40)):
+        for i in range(rows // 8):
+            for j in range(5):
+                c = pl.ds(j * 128, 128)
+                if i < 5:
+                    out[pl.ds(pl.multiple_of(first + i * 8, 8), 8), c] = z_out[count]
+                else:
+                    out[pl.ds(1280, 8), c] = z_out[count]
+                count += 1
+
+    def two_gathers(first, second):
+        plans = [gather_copies(out, base, stride, rows, sm, pos, dev, split)
+                 for base, stride, rows, pos, dev, split, sm in (first, second)]
+        for k in (0, 1):
+            for plan in plans:
+                plan[k].start()
+        for k in (0, 1):
+            for plan in plans:
+                plan[k].wait_recv()
+                plan[k + 2].start()
+        for k in (2, 3):
+            for plan in plans:
+                plan[k].wait_recv()
+        for plan in plans:
+            for copy in plan:
+                copy.wait_send()
+
+    two_gathers((p_first, 40, 40, x, on_x, 24, sems(ag_sems, 0)), (q_first, 40, 40, y, on_y, 24, sems(ag_sems, 1)))
+    two_gathers((0, 160, 160, y, on_y, 80, sems(ag_sems, 2)), (640, 160, 160, x, on_x, 80, sems(ag_sems, 3)))
+    swap = pltpu.make_async_remote_copy(src_ref=out, dst_ref=out, send_sem=swap_sems.at[0], recv_sem=swap_sems.at[1],
+                                        device_id=peer, device_id_type=MESH)
+    swap.start()
+    swap.wait()
+
+
+def all_reduce(grad_p, grad_q, depth):
+    channels = grad_p.shape[2]
+    vm = lambda *shape: pltpu.VMEM(shape, F32)
+    in_vmem = pl.BlockSpec(memory_space=pltpu.VMEM)
+    dma = pltpu.SemaphoreType.DMA
+    return pl.pallas_call(
+        functools.partial(all_reduce_body, depth),
+        in_specs=[in_vmem, in_vmem], out_specs=in_vmem,
+        out_shape=jax.ShapeDtypeStruct((2, 1288, channels), F32),
+        scratch_shapes=[vm(168, channels), vm(2, 168, channels), vm(160, channels), vm(2, 160, channels),
+                        vm(RING, 48, channels), vm(RING, 40, channels), vm(48, channels), vm(2, 48, channels),
+                        vm(40, channels), vm(2, 40, channels), vm(56, 8, 128), vm(max(depth - 1, 1), 56 // depth, 8, 128),
+                        vm(56, 8, 128), dma((2, 4, 6)), dma((2, 4, 4)), dma((2, 2, max(depth - 1, 1))), dma((2,))],
+        compiler_params=pltpu.CompilerParams(collective_id=0, has_side_effects=True, vmem_limit_bytes=40 * 2 ** 20),
+        name='grad_all_reduce',
+    )(grad_p, grad_q)
+
+
 def solution(mesh):
     dp_size = mesh.shape['dp']
     cp_size = mesh.shape['cp']
@@ -193,10 +381,11 @@
         small = jnp.stack([jnp.sum(d_normed * x_hat, axis=0), jnp.sum(d_normed, axis=0),
                            jnp.sum(dy_all[:own].astype(F32), axis=0)])
         d_w = jnp.concatenate([dot_nn(dqkv_t, normed), dot_nn(o_t, dy_all)], axis=0)
-        d_w = d_w.reshape(4, 1, width, channels)
-        zero = jnp.zeros_like(d_w)
-        both = jnp.where(core == 0, jnp.concatenate([d_w, zero], 1), jnp.concatenate([zero, d_w], 1))
-        both, small = lax.psum((both, small), axes)
+        grad_p = jnp.concatenate([d_w[:640].reshape(4, 160, channels),
+                                  jnp.broadcast_to(jnp.pad(small, ((0, 5), (0, 0))), (4, 8, channels))], axis=1)
+        both = all_reduce(grad_p, d_w[640:].reshape(4, 160, channels), dp_size // 8)
+        small = both[0, 1280:] + both[1, 1280:]
+        both = jnp.transpose(both[:, :1280].reshape(2, 4, half_heads, head_dim, channels), (1, 0, 2, 3, 4))
         both = both.reshape(4, num_heads, head_dim, channels)
         grads = [jnp.transpose(both[i], (2, 0, 1)) for i in range(3)]
         return (y_out, grad_x, small[0], small[1], grads[0], grads[1], grads[2], both[3], small[2])

time: 440 us -> 264 us (0.60)
  waiting for transfers between devices: 181 us -> 35.8 us
  Pallas kernels: 71.4 us -> 159 us
  blocking collectives: 83.9 us -> 0 us
  between operations: 14.6 us -> 1.18 us
  other arithmetic: 24.2 us -> 16.8 us
  local copies, waits for them, and re-layouts: 20.1 us -> 13.1 us
  matrix products: 21.6 us -> 15.6 us
    psum x1 -> x0, waiting for transfers between devices: 155 us -> none  [device_step(): both, small = lax.psum((both, small), axes)]
    pallas_call x0 -> x1, Pallas kernels: none -> 88 us  [all_reduce(): pl.pallas_call(functools.partial(all_reduce_body, depth), in_specs=[in_vm...]
    psum x1 -> x0, blocking collectives: 83.9 us -> none  [device_step(): both, small = lax.psum((both, small), axes)]
    ppermute x14, waiting for transfers between devices: 26.6 us -> 35.8 us  [permute(): return lax.ppermute(value, axes, pairs)]
  transfers between devices with their start and end apart: 15 -> 14, of which waited for: 6 -> 5; matrix products, arithmetic and copies ran while one was open for 11% -> 12% of each run, Pallas kernels for 0% -> 33%
where the time goes in v2:
time: 264 us
  Pallas kernels  159 us (60%)
  waiting for transfers between devices  35.8 us (14%)
  starting transfers between devices  21.9 us (8%)
  other arithmetic  16.8 us (6%)
  matrix products  15.6 us (6%)
  local copies, waits for them, and re-layouts  13.1 us (5%)
    pallas_call x1, Pallas kernels, all_reduce(): pl.pallas_call(functools.partial(all_reduce_body, depth), in_specs=[in_vm...  88 us
    pallas_call x1, Pallas kernels, attention(): pl.pallas_call(functools.partial(attention_body, head_dim ** (-0.5)), gri...  71.4 us
    ppermute x14, waiting for transfers between devices, permute(): return lax.ppermute(value, axes, pairs)  35.8 us
    ppermute x14, starting transfers between devices, permute(): return lax.ppermute(value, axes, pairs)  21.9 us
  transfers between devices with their start and end apart: 14, of which 5 were waited for; matrix products, arithmetic and copies ran while one was open for 12% of the time, Pallas kernels for 33%

profile of v2, /device:TPU:1, one launch (start us, length us, event | category | flops | bytes accessed | tf_op | source)
XLA Modules:
  0.0 263.7 jit_solution(11667560545609925765)
XLA Ops:
  0.7 2.6 dynamic-slice_bitcast_fusion.3
  3.2 6.0 %collective-permute-start = (bf16[512,640]{1,0:T(8,128)(2,1)}, bf16[512,640]{1,0:T(8,128)(2,1)S(1)}, u32[]{:S(2)}, u32[]{:S(2)}) collective-permute-start(bf16[512,640]{1,0:T(8,128)(2,1)} %get-tuple-element.40), channel_id=1, source_target_pairs={{0,0},{1,1},{2,4},{3,5},{4,2},{5,3},{6,6},{7,7},{8,8},{9,9},{10,12... | collective-permute-start | bytes 1966088 | tf_op jit(solution)/shard_map/ppermute | solution.py:319
  11.1 2.4 collective-permute-start.5
  13.5 1.9 collective-permute-start.4
  15.4 9.1 %collective-permute-done = bf16[512,640]{1,0:T(8,128)(2,1)S(1)} collective-permute-done((bf16[512,640]{1,0:T(8,128)(2,1)}, bf16[512,640]{1,0:T(8,128)(2,1)S(1)}, u32[]{:S(2)}, u32[]{:S(2)}) %collective-permute-start) | collective-permute-done | bytes 655392 | tf_op jit(solution)/shard_map/ppermute | solution.py:319
  24.5 3.1 %collective-permute-done.1 = bf16[512,640]{1,0:T(8,128)(2,1)S(1)} collective-permute-done((bf16[512,640]{1,0:T(8,128)(2,1)}, bf16[512,640]{1,0:T(8,128)(2,1)S(1)}, u32[]{:S(2)}, u32[]{:S(2)}) %collective-permute-start.1) | collective-permute-done | bytes 655392 | tf_op jit(solution)/shard_map/ppermute | solution.py:319
  30.3 9.8 %collective-permute-done.5 = bf16[512,640]{1,0:T(8,128)(2,1)S(1)} collective-permute-done((bf16[512,640]{1,0:T(8,128)(2,1)}, bf16[512,640]{1,0:T(8,128)(2,1)S(1)}, u32[]{:S(2)}, u32[]{:S(2)}) %collective-permute-start.5) | collective-permute-done | bytes 655392 | tf_op jit(solution)/shard_map/ppermute | solution.py:319
  40.8 3.1 %convert_reduce_fusion = f32[2048]{0:T(1024)S(1)} fusion(bf16[512,640]{1,0:T(8,128)(2,1)S(1)} %collective-permute-done.3, bf16[512,640]{1,0:T(8,128)(2,1)S(1)} %collective-permute-done.2, bf16[512,640]{1,0:T(8,128)(2,1)S(1)} %collective-permute-done.1, bf16[512,640]{1,0:T(8,128)(2,1)S(1)} %collective-permute-done), kind=kLoop, calls=%fused_computation.1 | loop fusion | flops 11794432 | bytes 2629632 | tf_op jit(solution)/shard_map/reduce_sum | solution.py:346
  44.0 3.9 %convert_subtract_fusion = (f32[2048,640]{1,0:T(8,128)S(1)}, f32[2048]{0:T(1024)S(1)}) fusion(f32[2048]{0:T(1024)S(1)} %broadcast_multiply_fusion, bf16[512,640]{1,0:T(8,128)(2,1)S(1)} %collective-permute-done.3, bf16[512,640]{1,0:T(8,128)(2,1)S(1)} %collective-permute-done.2, bf16[512,640]{1,0:T(8,128)(2,1)S(1)} %collective-permute-done.1, ...), kind=kLoop, calls=%fused_computation | loop fusion | flops 14415872 | bytes 7880704 | tf_op jit(solution)/shard_map/sub | solution.py:347
  47.9 5.1 %add_convert_fusion = bf16[2048,640]{1,0:T(8,128)(2,1)S(1)} fusion(f32[640]{0:T(1024)S(1)} %copy-done.8, f32[640]{0:T(1024)S(1)} %copy-done.7, f32[2048]{0:T(1024)S(1)} %add_rsqrt_fusion, f32[2048]{0:T(1024)S(1)} %broadcast_multiply_fusion, bf16[512,640]{1,0:T(8,128)(2,1)S(1)} %collective-permute-done.3, bf16[512,640]{1,0:T(8,128)(2,1)S(1)} %collective-permute-done.2, ...), kind=kLoop, calls=%fused_computation.2 | loop fusion | flops 17039360 | bytes 5264384 | tf_op jit(solution)/shard_map/convert_element_type | solution.py:349
  56.9 1.5 copy-done.5
  59.6 71.4 %attention.1 = (bf16[320,2048]{1,0:T(8,128)(2,1)S(1)}, bf16[320,2048]{1,0:T(8,128)(2,1)S(1)}, bf16[320,2048]{1,0:T(8,128)(2,1)S(1)}, bf16[320,2048]{1,0:T(8,128)(2,1)S(1)}) custom-call(bf16[320,2048]{1,0:T(8,128)(2,1)S(1)} %convolution_convert_fusion.3.qt_ref, bf16[320,2048]{1,0:T(8,128)(2,1)S(1)} %convolution_convert_fusion.2.kt_ref, ...), custom_call_target="tpu_custom_call" | custom-call | flops 16106127360 | bytes 10485760 | tf_op jit(solution)/shard_map/attention/pallas_call | solution.py:87
  131.3 3.2 %fusion.27 = f32[960,640]{1,0:T(8,128)S(1)} fusion(bf16[960,2048]{1,0:T(8,128)(2,1)S(1)} %constant_dynamic-update-slice_fusion.4, bf16[2048,640]{1,0:T(8,128)(2,1)S(1)} %add_convert_fusion), kind=kOutput, calls=%fused_computation.79 | convolution fusion | flops 2516582400 | bytes 9011200 | tf_op jit(solution)/shard_map/dot_general | solution.py:17
  138.9 2.9 %collective-permute-start.9 = (bf16[512,640]{1,0:T(8,128)(2,1)S(1)}, bf16[512,640]{1,0:T(8,128)(2,1)S(1)}, u32[]{:S(2)}, u32[]{:S(2)}) collective-permute-start(bf16[512,640]{1,0:T(8,128)(2,1)S(1)} %get-tuple-element.36), channel_id=1, source_target_pairs={{0,0},{1,1},{4,2},{5,3},{2,4},{3,5},{6,6},{7,7},{8,8},{9,9},{12,10... | collective-permute-start | bytes 1966088 | tf_op jit(solution)/shard_map/ppermute | solution.py:319
  141.8 2.2 collective-permute-start.10
  144.2 1.8 fusion.8
  146.0 11.2 %collective-permute-done.9 = bf16[512,640]{1,0:T(8,128)(2,1)S(1)} collective-permute-done((bf16[512,640]{1,0:T(8,128)(2,1)S(1)}, bf16[512,640]{1,0:T(8,128)(2,1)S(1)}, u32[]{:S(2)}, u32[]{:S(2)}) %collective-permute-start.9) | collective-permute-done | bytes 655392 | tf_op jit(solution)/shard_map/ppermute | solution.py:319
  157.3 2.6 collective-permute-done.10
  161.2 2.5 fusion.7
  163.7 1.7 convert_reduce_fusion.2
  165.6 2.9 %collective-permute-start.12 = (bf16[512,640]{1,0:T(8,128)(2,1)S(1)}, bf16[512,640]{1,0:T(8,128)(2,1)S(1)}, u32[]{:S(2)}, u32[]{:S(2)}) collective-permute-start(bf16[512,640]{1,0:T(8,128)(2,1)S(1)} %get-tuple-element.34), channel_id=1, source_target_pairs={{0,0},{1,1},{4,2},{5,3},{2,4},{3,5},{6,6},{7,7},{8,8},{9,9},{12,10... | collective-permute-start | bytes 1966088 | tf_op jit(solution)/shard_map/ppermute | solution.py:319
  168.5 1.8 collective-permute-start.13
  170.5 88.0 %grad_all_reduce.1 = f32[2,1288,640]{2,1,0:T(8,128)S(1)} custom-call(f32[4,168,640]{2,1,0:T(8,128)S(1)} %pad_maximum_fusion.1.gp_ref, f32[4,160,640]{2,1,0:T(8,128)S(1)} %bitcast.51), custom_call_target="tpu_custom_call" | custom-call | tf_op jit(solution)/shard_map/grad_all_reduce/pallas_call | solution.py:276
  259.6 2.9 %fusion.24 = (f32[1,2,4,80,640]{4,3,2,0,1:T(8,128)}, f32[1,2,4,80,640]{4,3,2,0,1:T(8,128)}, f32[1,2,4,80,640]{4,3,2,0,1:T(8,128)}, f32[1,2,4,80,640]{4,3,2,0,1:T(8,128)}) fusion(f32[4,2,4,80,640]{4,3,2,0,1:T(8,128)S(1)} %bitcast.52), kind=kLoop, calls=%fused_computation.76 | loop fusion | bytes 13107200 | tf_op jit(solution)/shard_map/slice | solution.py:391
  (74 shorter events, 19.0 us)
Async XLA Ops:
  0.6 9.3 %copy-start = (bf16[2,512,640]{2,1,0:T(8,128)(2,1)S(1)}, bf16[2,512,640]{2,1,0:T(8,128)(2,1)}, u32[]{:S(2)}) copy-start(bf16[2,512,640]{2,1,0:T(8,128)(2,1)} %param.10) | copy-start | bytes 3932164
  3.2 21.3 %collective-permute-start = (bf16[512,640]{1,0:T(8,128)(2,1)}, bf16[512,640]{1,0:T(8,128)(2,1)S(1)}, u32[]{:S(2)}, u32[]{:S(2)}) collective-permute-start(bf16[512,640]{1,0:T(8,128)(2,1)} %get-tuple-element.40), channel_id=1, source_target_pairs={{0,0},{1,1},{2,4},{3,5},{4,2},{5,3},{6,6},{7,7},{8,8},{9,9},{10,12... | collective-permute-start | bytes 1966088 | tf_op jit(solution)/shard_map/ppermute | solution.py:319
  9.3 20.9 %copy-start.1 = (bf16[640,8,80]{0,2,1:T(8,128)(2,1)S(1)}, bf16[640,8,80]{0,2,1:T(8,128)(2,1)}, u32[]{:S(2)}) copy-start(bf16[640,8,80]{0,2,1:T(8,128)(2,1)} %param.15) | copy-start | bytes 2457604
  9.3 18.3 %collective-permute-start.1 = (bf16[512,640]{1,0:T(8,128)(2,1)}, bf16[512,640]{1,0:T(8,128)(2,1)S(1)}, u32[]{:S(2)}, u32[]{:S(2)}) collective-permute-start(bf16[512,640]{1,0:T(8,128)(2,1)} %get-tuple-element.41), channel_id=1, source_target_pairs={{0,1},{1,0},{2,5},{3,4},{4,3},{5,2},{6,7},{7,6},{8,9},{9,8},{10,13... | collective-permute-start | bytes 1966088 | tf_op jit(solution)/shard_map/ppermute | solution.py:319
  11.1 29.0 %collective-permute-start.5 = (bf16[512,640]{1,0:T(8,128)(2,1)}, bf16[512,640]{1,0:T(8,128)(2,1)S(1)}, u32[]{:S(2)}, u32[]{:S(2)}) collective-permute-start(bf16[512,640]{1,0:T(8,128)(2,1)} %get-tuple-element.38), channel_id=1, source_target_pairs={{0,1},{1,0},{2,5},{3,4},{4,3},{5,2},{6,7},{7,6},{8,9},{9,8},{10,13... | collective-permute-start | bytes 1966088 | tf_op jit(solution)/shard_map/ppermute | solution.py:319
  13.5 26.6 %collective-permute-start.4 = (bf16[512,640]{1,0:T(8,128)(2,1)}, bf16[512,640]{1,0:T(8,128)(2,1)S(1)}, u32[]{:S(2)}, u32[]{:S(2)}) collective-permute-start(bf16[512,640]{1,0:T(8,128)(2,1)} %get-tuple-element.39), channel_id=1, source_target_pairs={{0,0},{1,1},{2,4},{3,5},{4,2},{5,3},{6,6},{7,7},{8,8},{9,9},{10,12... | collective-permute-start | bytes 1966088 | tf_op jit(solution)/shard_map/ppermute | solution.py:319
  15.4 14.8 %copy-start.2 = (bf16[640,8,80]{0,2,1:T(8,128)(2,1)S(1)}, bf16[640,8,80]{0,2,1:T(8,128)(2,1)}, u32[]{:S(2)}) copy-start(bf16[640,8,80]{0,2,1:T(8,128)(2,1)} %param.14) | copy-start | bytes 2457604
  24.5 16.3 %collective-permute-start.2 = (bf16[512,640]{1,0:T(8,128)(2,1)S(1)}, bf16[512,640]{1,0:T(8,128)(2,1)S(1)}, u32[]{:S(2)}, u32[]{:S(2)}) collective-permute-start(bf16[512,640]{1,0:T(8,128)(2,1)S(1)} %collective-permute-done), channel_id=1, source_target_pairs={{0,4},{1,5},{2,6},{3,7},{4,0},{5,1},{6,2},{7,3},{8,12},{9,13},{10,... | collective-permute-start | bytes 1966088 | tf_op jit(solution)/shard_map/ppermute | solution.py:319
  27.6 13.2 %collective-permute-start.3 = (bf16[512,640]{1,0:T(8,128)(2,1)S(1)}, bf16[512,640]{1,0:T(8,128)(2,1)S(1)}, u32[]{:S(2)}, u32[]{:S(2)}) collective-permute-start(bf16[512,640]{1,0:T(8,128)(2,1)S(1)} %collective-permute-done.1), channel_id=1, source_target_pairs={{0,4},{1,5},{2,6},{3,7},{4,0},{5,1},{6,2},{7,3},{8,12},{9,13},{10,... | collective-permute-start | bytes 1966088 | tf_op jit(solution)/shard_map/ppermute | solution.py:319
  28.8 26.8 %copy-start.3 = (bf16[640,4,80]{0,2,1:T(8,128)(2,1)}, bf16[640,4,80]{0,2,1:T(8,128)(2,1)S(1)}, u32[]{:S(2)}) copy-start(bf16[640,4,80]{0,2,1:T(8,128)(2,1)S(1)} %get-tuple-element.43) | copy-start | bytes 1228804
  40.1 16.7 %collective-permute-start.7 = (bf16[512,640]{1,0:T(8,128)(2,1)S(1)}, bf16[512,640]{1,0:T(8,128)(2,1)S(1)}, u32[]{:S(2)}, u32[]{:S(2)}) collective-permute-start(bf16[512,640]{1,0:T(8,128)(2,1)S(1)} %collective-permute-done.5), channel_id=1, source_target_pairs={{0,4},{1,5},{2,6},{3,7},{4,0},{5,1},{6,2},{7,3},{8,12},{9,13},{10,... | collective-permute-start | bytes 1966088 | tf_op jit(solution)/shard_map/ppermute | solution.py:319
  40.1 14.1 %collective-permute-start.6 = (bf16[512,640]{1,0:T(8,128)(2,1)S(1)}, bf16[512,640]{1,0:T(8,128)(2,1)S(1)}, u32[]{:S(2)}, u32[]{:S(2)}) collective-permute-start(bf16[512,640]{1,0:T(8,128)(2,1)S(1)} %collective-permute-done.4), channel_id=1, source_target_pairs={{0,4},{1,5},{2,6},{3,7},{4,0},{5,1},{6,2},{7,3},{8,12},{9,13},{10,... | collective-permute-start | bytes 1966088 | tf_op jit(solution)/shard_map/ppermute | solution.py:319
  43.9 4.0 %copy-start.7 = (f32[640]{0:T(1024)S(1)}, f32[640]{0:T(1024)}, u32[]{:S(2)}) copy-start(f32[640]{0:T(1024)} %param.11) | copy-start | bytes 7684
  44.0 4.0 %copy-start.8 = (f32[640]{0:T(1024)S(1)}, f32[640]{0:T(1024)}, u32[]{:S(2)}) copy-start(f32[640]{0:T(1024)} %param.12) | copy-start | bytes 7684
  56.9 1.5 copy-start.5
  134.7 1.7 copy-start.6
  134.8 2.9 %collective-permute-start.8 = (bf16[320,1024]{1,0:T(8,128)(2,1)S(1)}, bf16[320,1024]{1,0:T(8,128)(2,1)S(1)}, u32[]{:S(2)}, u32[]{:S(2)}) collective-permute-start(bf16[320,1024]{1,0:T(8,128)(2,1)S(1)} %slice.81), channel_id=1, source_target_pairs={{0,4},{1,5},{2,6},{3,7},{4,0},{5,1},{6,2},{7,3},{8,12},{9,13},{10,... | collective-permute-start | bytes 1966088 | tf_op jit(solution)/shard_map/ppermute | solution.py:319
  134.9 26.3 %collective-permute-start.11 = (bf16[960,1024]{1,0:T(8,128)(2,1)S(1)}, bf16[960,1024]{1,0:T(8,128)(2,1)S(1)}, u32[]{:S(2)}, u32[]{:S(2)}) collective-permute-start(bf16[960,1024]{1,0:T(8,128)(2,1)S(1)} %slice.106), channel_id=1, source_target_pairs={{0,4},{1,5},{2,6},{3,7},{4,0},{5,1},{6,2},{7,3},{8,12},{9,13},{10,... | collective-permute-start | bytes 5898248 | tf_op jit(solution)/shard_map/ppermute | solution.py:319
  136.5 1.2 copy-start.9
  138.9 18.4 %collective-permute-start.9 = (bf16[512,640]{1,0:T(8,128)(2,1)S(1)}, bf16[512,640]{1,0:T(8,128)(2,1)S(1)}, u32[]{:S(2)}, u32[]{:S(2)}) collective-permute-start(bf16[512,640]{1,0:T(8,128)(2,1)S(1)} %get-tuple-element.36), channel_id=1, source_target_pairs={{0,0},{1,1},{4,2},{5,3},{2,4},{3,5},{6,6},{7,7},{8,8},{9,9},{12,10... | collective-permute-start | bytes 1966088 | tf_op jit(solution)/shard_map/ppermute | solution.py:319
  141.8 2.4 copy-start.4
  141.8 18.1 %collective-permute-start.10 = (bf16[512,640]{1,0:T(8,128)(2,1)S(1)}, bf16[512,640]{1,0:T(8,128)(2,1)S(1)}, u32[]{:S(2)}, u32[]{:S(2)}) collective-permute-start(bf16[512,640]{1,0:T(8,128)(2,1)S(1)} %get-tuple-element.37), channel_id=1, source_target_pairs={{1,0},{0,1},{5,2},{4,3},{3,4},{2,5},{7,6},{6,7},{9,8},{8,9},{13,10... | collective-permute-start | bytes 1966088 | tf_op jit(solution)/shard_map/ppermute | solution.py:319
  165.6 96.9 %collective-permute-start.12 = (bf16[512,640]{1,0:T(8,128)(2,1)S(1)}, bf16[512,640]{1,0:T(8,128)(2,1)S(1)}, u32[]{:S(2)}, u32[]{:S(2)}) collective-permute-start(bf16[512,640]{1,0:T(8,128)(2,1)S(1)} %get-tuple-element.34), channel_id=1, source_target_pairs={{0,0},{1,1},{4,2},{5,3},{2,4},{3,5},{6,6},{7,7},{8,8},{9,9},{12,10... | collective-permute-start | bytes 1966088 | tf_op jit(solution)/shard_map/ppermute | solution.py:319
  168.5 93.9 %collective-permute-start.13 = (bf16[512,640]{1,0:T(8,128)(2,1)S(1)}, bf16[512,640]{1,0:T(8,128)(2,1)S(1)}, u32[]{:S(2)}, u32[]{:S(2)}) collective-permute-start(bf16[512,640]{1,0:T(8,128)(2,1)S(1)} %get-tuple-element.35), channel_id=1, source_target_pairs={{1,0},{0,1},{5,2},{4,3},{3,4},{2,5},{7,6},{6,7},{9,8},{8,9},{13,10... | collective-permute-start | bytes 1966088 | tf_op jit(solution)/shard_map/ppermute | solution.py:319

commit v3 on v2

--- a/solution.py
+++ b/solution.py
@@ -7,8 +7,12 @@
 from jax.experimental.pallas import tpu as pltpu
 from jax.sharding import PartitionSpec as P
 
+
 LN_EPS = 1e-5
 KEY_TILE = 256
+Q_BLOCK = 256
+FOLD = 16
+AUG = 96
 BF = jnp.bfloat16
 F32 = jnp.float32
 
@@ -25,77 +29,156 @@
     return lax.dot_general(lhs, rhs, (((0,), (0,)), ((), ())), preferred_element_type=F32)
 
 
-def attention_body(scale, qt_ref, kt_ref, vt_ref, do_ref, ot_ref, dq_ref, dk_ref, dv_ref,
-                   k_s, v_s, s_s, p_s, ds_s, dk_acc, dv_acc):
+def split_parts(value):
+    high = value.astype(BF)
+    rest = value - high.astype(F32)
+    mid = rest.astype(BF)
+    return high, mid, (rest - mid.astype(F32)).astype(BF)
+
+
+def fold_rows(value, op):
+    groups = value.reshape(value.shape[0] // FOLD, FOLD, value.shape[1])
+    out = groups[0]
+    for i in range(1, groups.shape[0]):
+        out = op(out, groups[i])
+    return out
+
+
+def forward_body(scale, group, qt_ref, kt_ref, vt_ref, ot_ref, of_ref, lse_ref, k_s, v_s, *bufs):
     step = pl.program_id(1)
-    rows = qt_ref.shape[1]
-    tokens = kt_ref.shape[1]
+    zero = jnp.minimum(step, 0)
+    dim, tokens = kt_ref.shape
     tiles = tokens // KEY_TILE
     log2_scale = scale * math.log2(math.e)
 
     @pl.when(step == 0)
     def _():
-        k_s[...] = kt_ref[...].T
-        v_s[...] = vt_ref[...].T
+        k_t = kt_ref[...]
+        k_s[...] = jnp.concatenate([k_t, k_t, k_t], axis=0).T
+        v_s[0:dim, :] = vt_ref[...]
+        v_s[dim:, :] = jnp.concatenate([jnp.ones((1, tokens), F32), jnp.zeros((AUG - dim - 1, tokens), F32)], axis=0).astype(BF)
+
+    def rows(tile, base=None):
+        return pl.ds(tile * KEY_TILE if base is None else pl.multiple_of(base + tile * KEY_TILE, KEY_TILE), KEY_TILE)
+
+    def block(i):
+        return pl.ds(pl.multiple_of((step * group + i) * Q_BLOCK, Q_BLOCK), Q_BLOCK)
+
+    total = tiles * group
+    lag = tiles + 1
+    query, part, top, probs, out = {}, {}, {}, {}, {}
+    for g in range(total + lag + 2):
+        if g < total:
+            i, t = divmod(g, tiles)
+            if t == 0:
+                query[i] = jnp.concatenate(split_parts(qt_ref[:, block(i)].astype(F32) * log2_scale), axis=0)
+            scores = dot_nn(k_s[rows(t), :], query[i])
+            bufs[i % len(bufs)][rows(t), :] = scores
+            folded = fold_rows(scores, jnp.maximum)
+            part[i] = folded if t == 0 else jnp.maximum(part[i], folded)
+            if t == tiles - 1:
+                top[i] = jnp.max(part[i], axis=0, keepdims=True)
+        if lag <= g < total + lag:
+            i, t = divmod(g - lag, tiles)
+            probs[g - lag] = jnp.exp2(bufs[i % len(bufs)][rows(t, zero), :] - top[i]).astype(BF)
+        if g >= lag + 2:
+            i, t = divmod(g - lag - 2, tiles)
+            part_out = dot_nn(v_s[:, rows(t)], probs[g - lag - 2])
+            out[i] = part_out if t == 0 else out[i] + part_out
+            if t == tiles - 1:
+                denom = out[i][dim:dim + 1]
+                normed = out[i][:dim] * (1.0 / denom)
+                ot_ref[:, block(i)] = normed.astype(BF)
+                of_ref[:, block(i)] = normed
+                lse = (top[i] + jnp.log2(denom)) * (1.0 / log2_scale)
+                lse_ref[:, block(i)] = jnp.concatenate([p.astype(F32) for p in split_parts(lse)] + [jnp.zeros((13, Q_BLOCK), F32)], axis=0).astype(BF)
+
+
+def attention_forward(q_t, k_t, v_t, head_dim, group=4):
+    width, tokens = q_t.shape
+    heads = width // head_dim
+    full = pl.BlockSpec((head_dim, tokens), lambda h, j: (h, 0))
+    stat = pl.BlockSpec((16, tokens), lambda h, j: (h, 0))
+    return pl.pallas_call(
+        functools.partial(forward_body, head_dim ** -0.5, group),
+        grid=(heads, tokens // (Q_BLOCK * group)),
+        in_specs=[full] * 3, out_specs=[full, full, stat],
+        out_shape=[jax.ShapeDtypeStruct((width, tokens), BF), jax.ShapeDtypeStruct((width, tokens), F32),
+                   jax.ShapeDtypeStruct((heads * 16, tokens), BF)],
+        scratch_shapes=[pltpu.VMEM((tokens, 3 * head_dim), BF), pltpu.VMEM((AUG, tokens), BF)]
+        + [pltpu.VMEM((tokens, Q_BLOCK), F32)] * 3,
+        compiler_params=pltpu.CompilerParams(vmem_limit_bytes=40 * 2 ** 20),
+        cost_estimate=pl.CostEstimate(flops=4 * heads * tokens * tokens * head_dim, bytes_accessed=12 * width * tokens,
+                                      transcendentals=heads * tokens * tokens),
+        name='attention_forward',
+    )(q_t, k_t, v_t)
+
+
+def backward_body(scale, group, qt_ref, kt_ref, vt_ref, do_ref, lse_ref, delta_ref, grad_ref, k_s, v_s, dk_acc, dv_acc):
+    step = pl.program_id(1)
+    dim, tokens = kt_ref.shape
+    tiles = tokens // KEY_TILE
+    log2_scale = scale * math.log2(math.e)
+
+    @pl.when(step == 0)
+    def _():
+        minus = jnp.concatenate([jnp.full((3, tokens), -1.0, F32), jnp.zeros((AUG - dim - 3, tokens), F32)], axis=0).astype(BF)
+        k_s[...] = jnp.concatenate([kt_ref[...], minus], axis=0).T
+        v_s[...] = jnp.concatenate([vt_ref[...], minus], axis=0).T
         dk_acc[...] = jnp.zeros_like(dk_acc)
         dv_acc[...] = jnp.zeros_like(dv_acc)
 
-    q_t = qt_ref[...]
-    do_t = do_ref[...]
-    top = None
-    for tile in range(tiles):
-        keys = pl.ds(tile * KEY_TILE, KEY_TILE)
-        scores = dot_nn(k_s[keys, :], q_t)
-        s_s[keys, :] = scores
-        part = jnp.max(scores.reshape(KEY_TILE // 8, 8, rows), axis=0)
-        top = part if top is None else jnp.maximum(top, part)
-    top = jnp.max(top, axis=0, keepdims=True) * log2_scale
-    total = None
-    for tile in range(tiles):
-        keys = pl.ds(tile * KEY_TILE, KEY_TILE)
-        probs = jnp.exp2(s_s[keys, :] * log2_scale - top)
-        s_s[keys, :] = probs
-        part = jnp.sum(probs.reshape(KEY_TILE // 8, 8, rows), axis=0)
-        total = part if total is None else total + part
-    recip = 1.0 / jnp.sum(total, axis=0, keepdims=True)
-    for tile in range(tiles):
-        keys = pl.ds(tile * KEY_TILE, KEY_TILE)
-        p_s[keys, :] = (s_s[keys, :] * recip).astype(BF)
-    out_t = dot_nn(vt_ref[...], p_s[...])
-    ot_ref[...] = out_t.astype(BF)
-    delta = jnp.sum(out_t * do_t.astype(F32), axis=0, keepdims=True)
-    dv_acc[...] += dot_nt(do_t, p_s[...])
-    for tile in range(tiles):
-        keys = pl.ds(tile * KEY_TILE, KEY_TILE)
-        d_probs = dot_nn(v_s[keys, :], do_t)
-        ds_s[keys, :] = ((s_s[keys, :] * recip) * (d_probs - delta)).astype(BF)
-    dq_ref[...] = (dot_nn(kt_ref[...], ds_s[...]) * scale).astype(BF)
-    dk_acc[...] += dot_nt(q_t, ds_s[...])
+    def rows(tile):
+        return pl.ds(tile * KEY_TILE, KEY_TILE)
+
+    total = tiles * group
+    ops, probs, d_scores, dq = {}, {}, {}, {}
+    for g in range(total + 2):
+        if g < total:
+            i, t = divmod(g, tiles)
+            if t == 0:
+                cols = pl.ds(pl.multiple_of((step * group + i) * Q_BLOCK, Q_BLOCK), Q_BLOCK)
+                q_t, do_t = qt_ref[:, cols], do_ref[:, cols]
+                ops[i] = (cols, q_t, do_t, jnp.concatenate([q_t, lse_ref[:, cols]], axis=0),
+                          jnp.concatenate([do_t, delta_ref[:, cols]], axis=0))
+            scores = dot_nn(k_s[rows(t), :], ops[i][3])
+            d_probs = dot_nn(v_s[rows(t), :], ops[i][4])
+            prob = jnp.exp2(scores * log2_scale)
+            probs[g] = prob.astype(BF)
+            d_scores[g] = (prob * d_probs).astype(BF)
+        if g >= 2:
+            i, t = divmod(g - 2, tiles)
+            cols, q_t, do_t = ops[i][:3]
+            dv_acc[:, rows(t)] += dot_nt(do_t, probs[g - 2])
+            part = dot_nn(kt_ref[:, rows(t)], d_scores[g - 2])
+            dq[i] = part if t == 0 else dq[i] + part
+            if t == tiles - 1:
+                grad_ref[0, :, cols] = (dq[i] * scale).astype(BF)
+            dk_acc[:, rows(t)] += dot_nt(q_t, d_scores[g - 2])
 
     @pl.when(step == pl.num_programs(1) - 1)
     def _():
-        dk_ref[...] = (dk_acc[...] * scale).astype(BF)
-        dv_ref[...] = dv_acc[...].astype(BF)
-
-
-def attention(q_t, k_t, v_t, do_t, head_dim, block=256):
+        grad_ref[1] = (dk_acc[...] * scale).astype(BF)
+        grad_ref[2] = dv_acc[...].astype(BF)
+
+
+def attention_backward(q_t, k_t, v_t, do_t, lse, delta, head_dim, group=4):
     width, tokens = q_t.shape
     heads = width // head_dim
-    row_spec = pl.BlockSpec((head_dim, block), lambda h, j: (h, j))
-    full_spec = pl.BlockSpec((head_dim, tokens), lambda h, j: (h, 0))
-    flops = 12 * heads * tokens * tokens * head_dim
+    full = pl.BlockSpec((head_dim, tokens), lambda h, j: (h, 0))
+    stat = pl.BlockSpec((16, tokens), lambda h, j: (h, 0))
     return pl.pallas_call(
-        functools.partial(attention_body, head_dim ** -0.5),
-        grid=(heads, tokens // block),
-        in_specs=[row_spec, full_spec, full_spec, row_spec],
-        out_specs=[row_spec, row_spec, full_spec, full_spec],
-        out_shape=[jax.ShapeDtypeStruct((width, tokens), BF)] * 4,
-        scratch_shapes=[pltpu.VMEM((tokens, head_dim), BF)] * 2 + [pltpu.VMEM((tokens, block), F32)]
-        + [pltpu.VMEM((tokens, block), BF)] * 2 + [pltpu.VMEM((head_dim, tokens), F32)] * 2,
+        functools.partial(backward_body, head_dim ** -0.5, group),
+        grid=(heads, tokens // (Q_BLOCK * group)),
+        in_specs=[full] * 4 + [stat] * 2,
+        out_specs=pl.BlockSpec((3, head_dim, tokens), lambda h, j: (0, h, 0)),
+        out_shape=jax.ShapeDtypeStruct((3, width, tokens), BF),
+        scratch_shapes=[pltpu.VMEM((tokens, AUG), BF)] * 2 + [pltpu.VMEM((head_dim, tokens), F32)] * 2,
         compiler_params=pltpu.CompilerParams(vmem_limit_bytes=40 * 2 ** 20),
-        cost_estimate=pl.CostEstimate(flops=flops, bytes_accessed=16 * width * tokens, transcendentals=heads * tokens * tokens),
-        name='attention',
-    )(q_t, k_t, v_t, do_t)
+        cost_estimate=pl.CostEstimate(flops=10 * heads * tokens * tokens * head_dim, bytes_accessed=16 * width * tokens,
+                                      transcendentals=heads * tokens * tokens),
+        name='attention_backward',
+    )(q_t, k_t, v_t, do_t, lse, delta)
 
 
 MESH = pl.DeviceIdType.MESH
@@ -356,14 +439,18 @@
             return lax.dot_general(weight, normed, (((0,), (1,)), ((), ())), preferred_element_type=F32).astype(BF)
 
         q_t, k_t, v_t = project(wq_mine), project(wk_mine), project(wv_mine)
+        o_t, o_f, lse = attention_forward(q_t, k_t, v_t, head_dim)
+        o_peer = permute(o_t[:, own:], swap)
         do_t = dot_nt(wo_mine, dy_all).astype(BF)
-        o_t, dq_t, dk_t, dv_t = attention(q_t, k_t, v_t, do_t, head_dim)
-
-        o_peer = permute(o_t[:, own:], swap)
+        delta = jnp.sum((o_f * do_t.astype(F32)).reshape(half_heads, head_dim, tokens), axis=1)
+        delta = jnp.pad(jnp.stack(split_parts(delta), axis=1), ((0, 0), (0, 13), (0, 0))).reshape(half_heads * 16, tokens)
         y_f = x_all[:own].astype(F32) + (dot_tn(o_t[:, :own], wo_mine) + dot_tn(o_peer, wo_other)) + b_o
-        y_out = scatter_image(y_f.astype(BF))
-
-        dqkv_t = jnp.concatenate([dq_t, dk_t, dv_t], axis=0)
+        y_own, delta = lax.optimization_barrier((y_f.astype(BF), delta))
+        y_same = permute(y_own[:own // 2], back_same)
+        y_cross = permute(y_own[own // 2:], back_cross)
+        dqkv_t = attention_backward(q_t, k_t, v_t, do_t, lse, delta, head_dim)
+        y_out = jnp.where(parity == 0, jnp.stack([y_same, y_cross]), jnp.stack([y_cross, y_same]))
+        dqkv_t = dqkv_t.reshape(3 * width, tokens)
         dqkv_peer = permute(dqkv_t[:, own:], swap)
         w_mine = jnp.concatenate([wq_mine, wk_mine, wv_mine], axis=1)
         w_other = jnp.concatenate([wq_other, wk_other, wv_other], axis=1)

time: 264 us -> 260 us (0.985); the launches traced: 264 us -> 255 us
  Pallas kernels: 159 us -> 140 us
  waiting for transfers between devices: 35.8 us -> 27.6 us
  other arithmetic: 16.8 us -> 24.8 us
  local copies, waits for them, and re-layouts: 13.1 us -> 20.6 us
    pallas_call x1 -> x2, Pallas kernels: 71.4 us -> 53.1 us  [the longest x1 34.2 us: attention_backward(): pl.pallas_call(functools.partial(backward_body, head_dim ** (-0.5), group...]
    ppermute x14, waiting for transfers between devices: 35.8 us -> 27.6 us  [permute(): return lax.ppermute(value, axes, pairs)]
    dynamic_slice x2, local copies, waits for them, and re-layouts: 1.35 us -> 4.78 us  [head_slice(): lax.dynamic_slice_in_dim(weight, which * half_heads, half_heads, 1)]
  transfers between devices with their start and end apart: 14 -> 14, of which waited for: 5 -> 5; matrix products, arithmetic and copies ran while one was open for 12% -> 19% of each run, Pallas kernels for 33% -> 42%
where the time goes in v3:
time: 260 us; the launch traced here: 255 us
  Pallas kernels  140 us (54%)
  waiting for transfers between devices  27.6 us (11%)
  other arithmetic  24.8 us (10%)
  starting transfers between devices  22.5 us (9%)
  local copies, waits for them, and re-layouts  20.6 us (8%)
  matrix products  17.8 us (7%)
    pallas_call x1, Pallas kernels, all_reduce(): pl.pallas_call(functools.partial(all_reduce_body, depth), in_specs=[in_vm...  87.3 us
    pallas_call x1, Pallas kernels, attention_backward(): pl.pallas_call(functools.partial(backward_body, head_dim ** (-0.5), group...  34.2 us
    ppermute x14, waiting for transfers between devices, permute(): return lax.ppermute(value, axes, pairs)  27.6 us
    ppermute x14, starting transfers between devices, permute(): return lax.ppermute(value, axes, pairs)  22.5 us
    pallas_call x1, Pallas kernels, attention_forward(): pl.pallas_call(functools.partial(forward_body, head_dim ** (-0.5), group)...  18.9 us
    sub x1, other arithmetic, device_step(): centered = x_f - mean  5.35 us
  transfers between devices with their start and end apart: 14, of which 5 were waited for; matrix products, arithmetic and copies ran while one was open for 19% of the time, Pallas kernels for 42%

profile of v3, /device:TPU:1, one launch (start us, length us, event | category | flops | bytes accessed | tf_op | source)
XLA Modules:
  0.0 255.2 jit_solution(13557317938599890908)
XLA Ops:
  0.7 2.6 %dynamic-slice_bitcast_fusion.3 = (bf16[512,640]{1,0:T(8,128)(2,1)}, bf16[512,640]{1,0:T(8,128)(2,1)}) fusion(bf16[2,512,640]{2,1,0:T(8,128)(2,1)} %param.9, s32[]{:T(128)S(6)} %select_n.34, s32[]{:T(128)S(6)} %select_n.35), kind=kLoop, calls=%fused_computation.48 | loop fusion | bytes 2621448 | tf_op jit(solution)/shard_map/jit(dynamic_index_in_dim)/squeeze | solution.py:405
  3.2 6.0 %collective-permute-start = (bf16[512,640]{1,0:T(8,128)(2,1)}, bf16[512,640]{1,0:T(8,128)(2,1)S(1)}, u32[]{:S(2)}, u32[]{:S(2)}) collective-permute-start(bf16[512,640]{1,0:T(8,128)(2,1)} %get-tuple-element.42), channel_id=1, source_target_pairs={{0,0},{1,1},{2,4},{3,5},{4,2},{5,3},{6,6},{7,7},{8,8},{9,9},{10,12... | collective-permute-start | bytes 1966088 | tf_op jit(solution)/shard_map/ppermute | solution.py:402
  11.1 2.4 collective-permute-start.6
  15.4 9.3 %collective-permute-done = bf16[512,640]{1,0:T(8,128)(2,1)S(1)} collective-permute-done((bf16[512,640]{1,0:T(8,128)(2,1)}, bf16[512,640]{1,0:T(8,128)(2,1)S(1)}, u32[]{:S(2)}, u32[]{:S(2)}) %collective-permute-start) | collective-permute-done | bytes 655392 | tf_op jit(solution)/shard_map/ppermute | solution.py:402
  24.7 3.0 %collective-permute-done.1 = bf16[512,640]{1,0:T(8,128)(2,1)S(1)} collective-permute-done((bf16[512,640]{1,0:T(8,128)(2,1)}, bf16[512,640]{1,0:T(8,128)(2,1)S(1)}, u32[]{:S(2)}, u32[]{:S(2)}) %collective-permute-start.1) | collective-permute-done | bytes 655392 | tf_op jit(solution)/shard_map/ppermute | solution.py:402
  27.8 2.2 constant_dynamic-slice_fusion.2
  32.1 2.6 %constant_dynamic-slice_fusion = (bf16[640,4,80]{0,2,1:T(8,128)(2,1)}, bf16[640,4,80]{0,2,1:T(8,128)(2,1)S(1)}, bf16[640,4,80]{0,2,1:T(8,128)(2,1)S(1)}, bf16[640,4,80]{0,2,1:T(8,128)(2,1)}) fusion(bf16[640,8,80]{0,2,1:T(8,128)(2,1)} %param.15, s32[]{:T(128)S(6)} %select_n.37, s32[]{:T(128)S(6)} %select_n.36, bf16[640,8,80]{0,2,1:T(8,128)(2,1)} %param.14), kind=kLoop, calls=%fused_computation.68 | loop fusion | bytes 3276808 | tf_op jit(solution)/shard_map/dynamic_slice | solution.py:416
  34.7 5.6 %collective-permute-done.6 = bf16[512,640]{1,0:T(8,128)(2,1)S(1)} collective-permute-done((bf16[512,640]{1,0:T(8,128)(2,1)}, bf16[512,640]{1,0:T(8,128)(2,1)S(1)}, u32[]{:S(2)}, u32[]{:S(2)}) %collective-permute-start.6) | collective-permute-done | bytes 655392 | tf_op jit(solution)/shard_map/ppermute | solution.py:402
  42.5 3.1 %convert_reduce_fusion = f32[2048]{0:T(1024)S(1)} fusion(bf16[512,640]{1,0:T(8,128)(2,1)S(1)} %collective-permute-done.3, bf16[512,640]{1,0:T(8,128)(2,1)S(1)} %collective-permute-done.2, bf16[512,640]{1,0:T(8,128)(2,1)S(1)} %collective-permute-done.1, bf16[512,640]{1,0:T(8,128)(2,1)S(1)} %collective-permute-done), kind=kLoop, calls=%fused_computation.1 | loop fusion | flops 11794432 | bytes 2629632 | tf_op jit(solution)/shard_map/reduce_sum | solution.py:429
  45.7 5.3 %convert_subtract_fusion = (f32[2048,640]{1,0:T(8,128)}, f32[2048]{0:T(1024)S(1)}) fusion(f32[2048]{0:T(1024)S(1)} %broadcast_multiply_fusion, bf16[512,640]{1,0:T(8,128)(2,1)S(1)} %collective-permute-done.3, bf16[512,640]{1,0:T(8,128)(2,1)S(1)} %collective-permute-done.2, bf16[512,640]{1,0:T(8,128)(2,1)S(1)} %collective-permute-done.1, ...), kind=kLoop, calls=%fused_computation | loop fusion | flops 14415872 | bytes 7880704 | tf_op jit(solution)/shard_map/sub | solution.py:430
  51.1 5.1 %add_convert_fusion = bf16[2048,640]{1,0:T(8,128)(2,1)S(1)} fusion(f32[640]{0:T(1024)S(1)} %copy-done.27, f32[640]{0:T(1024)S(1)} %copy-done.26, f32[2048]{0:T(1024)S(1)} %add_rsqrt_fusion, f32[2048]{0:T(1024)S(1)} %broadcast_multiply_fusion, bf16[512,640]{1,0:T(8,128)(2,1)S(1)} %collective-permute-done.3, bf16[512,640]{1,0:T(8,128)(2,1)S(1)} %collective-permute-done.2, ...), kind=kLoop, calls=%fused_computation.2 | loop fusion | flops 17039360 | bytes 5264384 | tf_op jit(solution)/shard_map/convert_element_type | solution.py:432
  59.9 18.9 %attention_forward.1 = (bf16[320,2048]{1,0:T(8,128)(2,1)S(1)}, f32[320,2048]{1,0:T(8,128)S(1)}, bf16[64,2048]{1,0:T(8,128)(2,1)S(1)}) custom-call(bf16[320,2048]{1,0:T(8,128)(2,1)S(1)} %convolution_convert_fusion.3.qt_ref, bf16[320,2048]{1,0:T(8,128)(2,1)S(1)} %convolution_convert_fusion.2.kt_ref, bf16[320,2048]{1,0:T(8,128)(2,1)S(1)} %convolution_convert_fusion.1.vt_ref), custom_call_target="tpu_custom_call" | custom-call | flops 5368709120 | bytes 7864320 | tf_op jit(solution)/shard_map/attention_forward/pallas_call | solution.py:102
  83.8 2.6 %reduce_sum.76 = f32[4,2048]{1,0:T(4,128)} reduce(f32[4,80,2048]{2,1,0:T(8,128)} %bitcast.62, f32[]{:T(128)} %constant.45.clone.1), dimensions={1}, to_apply=%region_2.3 | reduce | flops 647168 | bytes 2654212 | tf_op jit(solution)/shard_map/reduce_sum | solution.py:445
  90.3 2.3 add_convert_fusion.2
  92.6 34.2 %attention_backward.1 = bf16[3,320,2048]{2,1,0:T(8,128)(2,1)S(1)} custom-call(bf16[320,2048]{1,0:T(8,128)(2,1)S(1)} %copy-done.5, bf16[320,2048]{1,0:T(8,128)(2,1)S(1)} %copy-done.3, bf16[320,2048]{1,0:T(8,128)(2,1)S(1)} %copy-done.1, bf16[320,2048]{1,0:T(8,128)(2,1)S(1)} %convolution_convert_fusion.do_ref, bf16[64,2048]{1,0:T(8,128)(2,1)S(1)} %get-tuple-element.17.lse_ref, ...), custom_call_target="tpu_custom_call" | custom-call | flops 13421772800 | bytes 10485760 | tf_op jit(solution)/shard_map/attention_backward/pallas_call | solution.py:170
  129.8 3.0 %collective-permute-start.9 = (bf16[512,640]{1,0:T(8,128)(2,1)S(1)}, bf16[512,640]{1,0:T(8,128)(2,1)S(1)}, u32[]{:S(2)}, u32[]{:S(2)}) collective-permute-start(bf16[512,640]{1,0:T(8,128)(2,1)S(1)} %get-tuple-element.38), channel_id=1, source_target_pairs={{0,0},{1,1},{4,2},{5,3},{2,4},{3,5},{6,6},{7,7},{8,8},{9,9},{12,10... | collective-permute-start | bytes 1966088 | tf_op jit(solution)/shard_map/ppermute | solution.py:402
  132.8 2.1 collective-permute-start.10
  135.0 3.2 %fusion.33 = f32[960,640]{1,0:T(8,128)S(1)} fusion(bf16[960,2048]{1,0:T(8,128)(2,1)S(1)} %bitcast.56, bf16[2048,640]{1,0:T(8,128)(2,1)S(1)} %copy-done.9), kind=kOutput, calls=%fused_computation.87 | convolution fusion | flops 2516582400 | bytes 9011200 | tf_op jit(solution)/shard_map/dot_general | solution.py:21
  141.3 7.4 %collective-permute-done.9 = bf16[512,640]{1,0:T(8,128)(2,1)S(1)} collective-permute-done((bf16[512,640]{1,0:T(8,128)(2,1)S(1)}, bf16[512,640]{1,0:T(8,128)(2,1)S(1)}, u32[]{:S(2)}, u32[]{:S(2)}) %collective-permute-start.9) | collective-permute-done | bytes 655392 | tf_op jit(solution)/shard_map/ppermute | solution.py:402
  152.2 2.5 fusion.7
  154.8 2.7 %convert_reduce_fusion.2 = (f32[640]{0:T(1024)S(1)}, bf16[1024,640]{1,0:T(8,128)(2,1)S(1)}) fusion(bf16[512,640]{1,0:T(8,128)(2,1)S(1)} %copy-done.11, bf16[512,640]{1,0:T(8,128)(2,1)} %collective-permute-done.5, f32[1024]{0:T(1024)S(1)} %broadcast_multiply_fusion.1, f32[2048,640]{1,0:T(8,128)S(1)} %bitcast.61, f32[1024]{0:T(1024)S(1)} %broadcast_multiply_fusion.2, ...), kind=kLoop, calls=%fused_computation.10 | loop fusion | flops 9174400 | bytes 6571008 | tf_op jit(solution)/shard_map/reduce_sum | solution.py:469
  157.6 2.9 %collective-permute-start.12 = (bf16[512,640]{1,0:T(8,128)(2,1)S(1)}, bf16[512,640]{1,0:T(8,128)(2,1)S(1)}, u32[]{:S(2)}, u32[]{:S(2)}) collective-permute-start(bf16[512,640]{1,0:T(8,128)(2,1)S(1)} %get-tuple-element.36), channel_id=1, source_target_pairs={{0,0},{1,1},{4,2},{5,3},{2,4},{3,5},{6,6},{7,7},{8,8},{9,9},{12,10... | collective-permute-start | bytes 1966088 | tf_op jit(solution)/shard_map/ppermute | solution.py:402
  162.5 87.3 %grad_all_reduce.1 = f32[2,1288,640]{2,1,0:T(8,128)S(1)} custom-call(f32[4,168,640]{2,1,0:T(8,128)S(1)} %pad_maximum_fusion.1.gp_ref, f32[4,160,640]{2,1,0:T(8,128)S(1)} %bitcast.54), custom_call_target="tpu_custom_call" | custom-call | tf_op jit(solution)/shard_map/grad_all_reduce/pallas_call | solution.py:359
  250.8 2.9 %fusion.30 = (f32[1,2,4,80,640]{4,3,2,0,1:T(8,128)}, f32[1,2,4,80,640]{4,3,2,0,1:T(8,128)}, f32[1,2,4,80,640]{4,3,2,0,1:T(8,128)}, f32[1,2,4,80,640]{4,3,2,0,1:T(8,128)}) fusion(f32[4,2,4,80,640]{4,3,2,0,1:T(8,128)S(1)} %bitcast.59), kind=kLoop, calls=%fused_computation.84 | loop fusion | bytes 13107200 | tf_op jit(solution)/shard_map/slice | solution.py:478
  (120 shorter events, 34.4 us)
Async XLA Ops:
  3.2 21.5 %collective-permute-start = (bf16[512,640]{1,0:T(8,128)(2,1)}, bf16[512,640]{1,0:T(8,128)(2,1)S(1)}, u32[]{:S(2)}, u32[]{:S(2)}) collective-permute-start(bf16[512,640]{1,0:T(8,128)(2,1)} %get-tuple-element.42), channel_id=1, source_target_pairs={{0,0},{1,1},{2,4},{3,5},{4,2},{5,3},{6,6},{7,7},{8,8},{9,9},{10,12... | collective-permute-start | bytes 1966088 | tf_op jit(solution)/shard_map/ppermute | solution.py:402
  9.2 18.5 %collective-permute-start.1 = (bf16[512,640]{1,0:T(8,128)(2,1)}, bf16[512,640]{1,0:T(8,128)(2,1)S(1)}, u32[]{:S(2)}, u32[]{:S(2)}) collective-permute-start(bf16[512,640]{1,0:T(8,128)(2,1)} %get-tuple-element.43), channel_id=1, source_target_pairs={{0,1},{1,0},{2,5},{3,4},{4,3},{5,2},{6,7},{7,6},{8,9},{9,8},{10,13... | collective-permute-start | bytes 1966088 | tf_op jit(solution)/shard_map/ppermute | solution.py:402
  11.1 29.2 %collective-permute-start.6 = (bf16[512,640]{1,0:T(8,128)(2,1)}, bf16[512,640]{1,0:T(8,128)(2,1)S(1)}, u32[]{:S(2)}, u32[]{:S(2)}) collective-permute-start(bf16[512,640]{1,0:T(8,128)(2,1)} %get-tuple-element.40), channel_id=1, source_target_pairs={{0,1},{1,0},{2,5},{3,4},{4,3},{5,2},{6,7},{7,6},{8,9},{9,8},{10,13... | collective-permute-start | bytes 1966088 | tf_op jit(solution)/shard_map/ppermute | solution.py:402
  13.5 26.9 %collective-permute-start.5 = (bf16[512,640]{1,0:T(8,128)(2,1)}, bf16[512,640]{1,0:T(8,128)(2,1)}, u32[]{:S(2)}, u32[]{:S(2)}) collective-permute-start(bf16[512,640]{1,0:T(8,128)(2,1)} %get-tuple-element.41), channel_id=1, source_target_pairs={{0,0},{1,1},{2,4},{3,5},{4,2},{5,3},{6,6},{7,7},{8,8},{9,9},{10,12... | collective-permute-start | bytes 1966088 | tf_op jit(solution)/shard_map/ppermute | solution.py:402
  24.7 17.8 %collective-permute-start.2 = (bf16[512,640]{1,0:T(8,128)(2,1)S(1)}, bf16[512,640]{1,0:T(8,128)(2,1)S(1)}, u32[]{:S(2)}, u32[]{:S(2)}) collective-permute-start(bf16[512,640]{1,0:T(8,128)(2,1)S(1)} %collective-permute-done), channel_id=1, source_target_pairs={{0,4},{1,5},{2,6},{3,7},{4,0},{5,1},{6,2},{7,3},{8,12},{9,13},{10,... | collective-permute-start | bytes 1966088 | tf_op jit(solution)/shard_map/ppermute | solution.py:402
  27.8 23.3 %copy-start.6 = (bf16[512,640]{1,0:T(8,128)(2,1)}, bf16[512,640]{1,0:T(8,128)(2,1)S(1)}, u32[]{:S(2)}) copy-start(bf16[512,640]{1,0:T(8,128)(2,1)S(1)} %collective-permute-done.1) | copy-start | bytes 1966084
  27.8 14.7 %collective-permute-start.3 = (bf16[512,640]{1,0:T(8,128)(2,1)S(1)}, bf16[512,640]{1,0:T(8,128)(2,1)S(1)}, u32[]{:S(2)}, u32[]{:S(2)}) collective-permute-start(bf16[512,640]{1,0:T(8,128)(2,1)S(1)} %collective-permute-done.1), channel_id=1, source_target_pairs={{0,4},{1,5},{2,6},{3,7},{4,0},{5,1},{6,2},{7,3},{8,12},{9,13},{10,... | collective-permute-start | bytes 1966088 | tf_op jit(solution)/shard_map/ppermute | solution.py:402
  30.0 28.7 %copy-start.22 = (bf16[640,4,80]{0,2,1:T(8,128)(2,1)}, bf16[640,4,80]{0,2,1:T(8,128)(2,1)S(1)}, u32[]{:S(2)}) copy-start(bf16[640,4,80]{0,2,1:T(8,128)(2,1)S(1)} %get-tuple-element.45) | copy-start | bytes 1228804
  32.1 48.2 %copy-start.12 = (bf16[4,80,640]{2,1,0:T(8,128)(2,1)}, bf16[4,80,640]{2,1,0:T(8,128)(2,1)S(1)}, u32[]{:S(2)}) copy-start(bf16[4,80,640]{2,1,0:T(8,128)(2,1)S(1)} %get-tuple-element.51) | copy-start | bytes 1228804
  34.7 21.5 %copy-start.17 = (bf16[640,4,80]{0,2,1:T(8,128)(2,1)}, bf16[640,4,80]{0,2,1:T(8,128)(2,1)S(1)}, u32[]{:S(2)}) copy-start(bf16[640,4,80]{0,2,1:T(8,128)(2,1)S(1)} %get-tuple-element.49) | copy-start | bytes 1228804
  34.7 22.7 %copy-start.19 = (bf16[640,4,80]{0,2,1:T(8,128)(2,1)}, bf16[640,4,80]{0,2,1:T(8,128)(2,1)S(1)}, u32[]{:S(2)}) copy-start(bf16[640,4,80]{0,2,1:T(8,128)(2,1)S(1)} %get-tuple-element.55) | copy-start | bytes 1228804
  40.3 39.8 %collective-permute-start.8 = (bf16[512,640]{1,0:T(8,128)(2,1)S(1)}, bf16[512,640]{1,0:T(8,128)(2,1)S(1)}, u32[]{:S(2)}, u32[]{:S(2)}) collective-permute-start(bf16[512,640]{1,0:T(8,128)(2,1)S(1)} %collective-permute-done.6), channel_id=1, source_target_pairs={{0,4},{1,5},{2,6},{3,7},{4,0},{5,1},{6,2},{7,3},{8,12},{9,13},{10,... | collective-permute-start | bytes 1966088 | tf_op jit(solution)/shard_map/ppermute | solution.py:402
  40.3 39.7 %collective-permute-start.7 = (bf16[512,640]{1,0:T(8,128)(2,1)}, bf16[512,640]{1,0:T(8,128)(2,1)S(1)}, u32[]{:S(2)}, u32[]{:S(2)}) collective-permute-start(bf16[512,640]{1,0:T(8,128)(2,1)} %collective-permute-done.5), channel_id=1, source_target_pairs={{0,4},{1,5},{2,6},{3,7},{4,0},{5,1},{6,2},{7,3},{8,12},{9,13},{10,... | collective-permute-start | bytes 1966088 | tf_op jit(solution)/shard_map/ppermute | solution.py:402
  59.9 18.9 %copy-start.4 = (bf16[320,2048]{1,0:T(8,128)(2,1)}, bf16[320,2048]{1,0:T(8,128)(2,1)S(1)}, u32[]{:S(2)}) copy-start(bf16[320,2048]{1,0:T(8,128)(2,1)S(1)} %convolution_convert_fusion.3.qt_ref) | copy-start | bytes 3932164
  79.8 10.4 %collective-permute-start.4 = (bf16[320,1024]{1,0:T(8,128)(2,1)}, bf16[320,1024]{1,0:T(8,128)(2,1)}, u32[]{:S(2)}, u32[]{:S(2)}) collective-permute-start(bf16[320,1024]{1,0:T(8,128)(2,1)} %slice.81), channel_id=1, source_target_pairs={{0,4},{1,5},{2,6},{3,7},{4,0},{5,1},{6,2},{7,3},{8,12},{9,13},{10,... | collective-permute-start | bytes 1966088 | tf_op jit(solution)/shard_map/ppermute | solution.py:402
  127.0 25.2 %collective-permute-start.11 = (bf16[960,1024]{1,0:T(8,128)(2,1)S(1)}, bf16[960,1024]{1,0:T(8,128)(2,1)S(1)}, u32[]{:S(2)}, u32[]{:S(2)}) collective-permute-start(bf16[960,1024]{1,0:T(8,128)(2,1)S(1)} %slice.104), channel_id=1, source_target_pairs={{0,4},{1,5},{2,6},{3,7},{4,0},{5,1},{6,2},{7,3},{8,12},{9,13},{10,... | collective-permute-start | bytes 5898248 | tf_op jit(solution)/shard_map/ppermute | solution.py:402
  129.8 18.9 %collective-permute-start.9 = (bf16[512,640]{1,0:T(8,128)(2,1)S(1)}, bf16[512,640]{1,0:T(8,128)(2,1)S(1)}, u32[]{:S(2)}, u32[]{:S(2)}) collective-permute-start(bf16[512,640]{1,0:T(8,128)(2,1)S(1)} %get-tuple-element.38), channel_id=1, source_target_pairs={{0,0},{1,1},{4,2},{5,3},{2,4},{3,5},{6,6},{7,7},{8,8},{9,9},{12,10... | collective-permute-start | bytes 1966088 | tf_op jit(solution)/shard_map/ppermute | solution.py:402
  132.8 18.1 %collective-permute-start.10 = (bf16[512,640]{1,0:T(8,128)(2,1)S(1)}, bf16[512,640]{1,0:T(8,128)(2,1)S(1)}, u32[]{:S(2)}, u32[]{:S(2)}) collective-permute-start(bf16[512,640]{1,0:T(8,128)(2,1)S(1)} %get-tuple-element.39), channel_id=1, source_target_pairs={{1,0},{0,1},{5,2},{4,3},{3,4},{2,5},{7,6},{6,7},{9,8},{8,9},{13,10... | collective-permute-start | bytes 1966088 | tf_op jit(solution)/shard_map/ppermute | solution.py:402
  138.2 14.0 %slice-start = ((s8[5242880]{0:T(1024)(128)(4,1)}), s8[4194304]{0:T(1024)(128)(4,1)S(1)}, s32[]{:S(2)}) async-start(s8[5242880]{0:T(1024)(128)(4,1)} %bitcast.60), calls=%async_computation | async-start | bytes 8388608
  139.4 12.7 %slice-start.1 = ((s8[5242880]{0:T(1024)(128)(4,1)}), s8[1048576]{0:T(1024)(128)(4,1)S(1)}, s32[]{:S(2)}) async-start(s8[5242880]{0:T(1024)(128)(4,1)} %bitcast.60), calls=%async_computation.1 | async-start | bytes 2097152
  141.3 10.9 %copy-start.15 = (bf16[640,4,80]{0,2,1:T(8,128)(2,1)S(1)}, bf16[640,4,80]{0,2,1:T(8,128)(2,1)}, u32[]{:S(2)}) copy-start(bf16[640,4,80]{0,2,1:T(8,128)(2,1)} %get-tuple-element.48) | copy-start | bytes 1228804
  141.3 10.9 %copy-start.16 = (bf16[640,4,80]{0,2,1:T(8,128)(2,1)S(1)}, bf16[640,4,80]{0,2,1:T(8,128)(2,1)}, u32[]{:S(2)}) copy-start(bf16[640,4,80]{0,2,1:T(8,128)(2,1)} %get-tuple-element.56) | copy-start | bytes 1228804
  157.6 96.1 %collective-permute-start.12 = (bf16[512,640]{1,0:T(8,128)(2,1)S(1)}, bf16[512,640]{1,0:T(8,128)(2,1)S(1)}, u32[]{:S(2)}, u32[]{:S(2)}) collective-permute-start(bf16[512,640]{1,0:T(8,128)(2,1)S(1)} %get-tuple-element.36), channel_id=1, source_target_pairs={{0,0},{1,1},{4,2},{5,3},{2,4},{3,5},{6,6},{7,7},{8,8},{9,9},{12,10... | collective-permute-start | bytes 1966088 | tf_op jit(solution)/shard_map/ppermute | solution.py:402
  160.6 93.2 %collective-permute-start.13 = (bf16[512,640]{1,0:T(8,128)(2,1)S(1)}, bf16[512,640]{1,0:T(8,128)(2,1)S(1)}, u32[]{:S(2)}, u32[]{:S(2)}) collective-permute-start(bf16[512,640]{1,0:T(8,128)(2,1)S(1)} %get-tuple-element.37), channel_id=1, source_target_pairs={{1,0},{0,1},{5,2},{4,3},{3,4},{2,5},{7,6},{6,7},{9,8},{8,9},{13,10... | collective-permute-start | bytes 1966088 | tf_op jit(solution)/shard_map/ppermute | solution.py:402
  (21 other events, 75.5 us)

commit v4 on v1

v4 whole, which is shorter than its diff:
```python
import functools
import math
import jax
import jax.numpy as jnp
from jax import lax
from jax.experimental import pallas as pl
from jax.experimental.pallas import tpu as pltpu
from jax.sharding import PartitionSpec as P


LN_EPS = 1e-5
KEY_TILE = 256
Q_BLOCK = 256
FOLD = 16
AUG = 96
BF = jnp.bfloat16
F32 = jnp.float32


def dot_nn(lhs, rhs):
    return lax.dot_general(lhs, rhs, (((1,), (0,)), ((), ())), preferred_element_type=F32)


def dot_nt(lhs, rhs):
    return lax.dot_general(lhs, rhs, (((1,), (1,)), ((), ())), preferred_element_type=F32)


def dot_tn(lhs, rhs):
    return lax.dot_general(lhs, rhs, (((0,), (0,)), ((), ())), preferred_element_type=F32)


def split_parts(value):
    high = value.astype(BF)
    rest = value - high.astype(F32)
    mid = rest.astype(BF)
    return high, mid, (rest - mid.astype(F32)).astype(BF)


def fold_rows(value, op):
    groups = value.reshape(value.shape[0] // FOLD, FOLD, value.shape[1])
    out = groups[0]
    for i in range(1, groups.shape[0]):
        out = op(out, groups[i])
    return out


def forward_body(scale, group, qt_ref, kt_ref, vt_ref, ot_ref, of_ref, lse_ref, k_s, v_s, *bufs):
    step = pl.program_id(1)
    zero = jnp.minimum(step, 0)
    dim, tokens = kt_ref.shape
    tiles = tokens // KEY_TILE
    log2_scale = scale * math.log2(math.e)

    @pl.when(step == 0)
    def _():
        k_t = kt_ref[...]
        k_s[...] = jnp.concatenate([k_t, k_t, k_t], axis=0).T
        v_s[0:dim, :] = vt_ref[...]
        v_s[dim:, :] = jnp.concatenate([jnp.ones((1, tokens), F32), jnp.zeros((AUG - dim - 1, tokens), F32)], axis=0).astype(BF)

    def rows(tile, base=None):
        return pl.ds(tile * KEY_TILE if base is None else pl.multiple_of(base + tile * KEY_TILE, KEY_TILE), KEY_TILE)

    def block(i):
        return pl.ds(pl.multiple_of((step * group + i) * Q_BLOCK, Q_BLOCK), Q_BLOCK)

    total = tiles * group
    lag = tiles + 1
    query, part, top, probs, out = {}, {}, {}, {}, {}
    for g in range(total + lag + 2):
        if g < total:
            i, t = divmod(g, tiles)
            if t == 0:
                query[i] = jnp.concatenate(split_parts(qt_ref[:, block(i)].astype(F32) * log2_scale), axis=0)
            scores = dot_nn(k_s[rows(t), :], query[i])
            bufs[i % len(bufs)][rows(t), :] = scores
            folded = fold_rows(scores, jnp.maximum)
            part[i] = folded if t == 0 else jnp.maximum(part[i], folded)
            if t == tiles - 1:
                top[i] = jnp.max(part[i], axis=0, keepdims=True)
        if lag <= g < total + lag:
            i, t = divmod(g - lag, tiles)
            probs[g - lag] = jnp.exp2(bufs[i % len(bufs)][rows(t, zero), :] - top[i]).astype(BF)
        if g >= lag + 2:
            i, t = divmod(g - lag - 2, tiles)
            part_out = dot_nn(v_s[:, rows(t)], probs[g - lag - 2])
            out[i] = part_out if t == 0 else out[i] + part_out
            if t == tiles - 1:
                denom = out[i][dim:dim + 1]
                normed = out[i][:dim] * (1.0 / denom)
                ot_ref[:, block(i)] = normed.astype(BF)
                of_ref[:, block(i)] = normed
                lse = (top[i] + jnp.log2(denom)) * (1.0 / log2_scale)
                lse_ref[:, block(i)] = jnp.concatenate([p.astype(F32) for p in split_parts(lse)] + [jnp.zeros((13, Q_BLOCK), F32)], axis=0).astype(BF)


def attention_forward(q_t, k_t, v_t, head_dim, group=4):
    width, tokens = q_t.shape
    heads = width // head_dim
    full = pl.BlockSpec((head_dim, tokens), lambda h, j: (h, 0))
    stat = pl.BlockSpec((16, tokens), lambda h, j: (h, 0))
    return pl.pallas_call(
        functools.partial(forward_body, head_dim ** -0.5, group),
        grid=(heads, tokens // (Q_BLOCK * group)),
        in_specs=[full] * 3, out_specs=[full, full, stat],
        out_shape=[jax.ShapeDtypeStruct((width, tokens), BF), jax.ShapeDtypeStruct((width, tokens), F32),
                   jax.ShapeDtypeStruct((heads * 16, tokens), BF)],
        scratch_shapes=[pltpu.VMEM((tokens, 3 * head_dim), BF), pltpu.VMEM((AUG, tokens), BF)]
        + [pltpu.VMEM((tokens, Q_BLOCK), F32)] * 3,
        compiler_params=pltpu.CompilerParams(vmem_limit_bytes=40 * 2 ** 20),
        cost_estimate=pl.CostEstimate(flops=4 * heads * tokens * tokens * head_dim, bytes_accessed=12 * width * tokens,
                                      transcendentals=heads * tokens * tokens),
        name='attention_forward',
    )(q_t, k_t, v_t)


MESH = pl.DeviceIdType.MESH
RING = 4
ROUNDS = 5
ROUND_ROWS = 256
SPLIT = 384
ORDER = (('y', 'x'), ('y', 'x'), ('y', 'x'), ('y', 'y'), ('y', 'x'))


class Links:
    def __init__(self, depth):
        dp, self.x = lax.axis_index('dp'), lax.axis_index('cp')
        self.core = lax.rem(dp, 2)
        self.y = lax.rem(dp // 2, RING)
        self.z = dp // (2 * RING)
        self.depth = depth
        self.pos = {'x': self.x, 'y': self.y, 'z': self.z}
        self.size = {'x': RING, 'y': RING, 'z': depth}
        self.peer = self.at(core=1 - self.core)
        pair, odd = self.x // 2, lax.rem(self.x, 2)
        self.owners = [(pair, 2 * self.core + odd), (pair, 2 * self.core + 1 - odd)]
        self.workers = [(pair, 2 * self.core), (pair, 2 * self.core + 1)]

    def at(self, x=None, y=None, z=None, core=None):
        pick = lambda value, own: own if value is None else value
        return ((pick(z, self.z) * RING + pick(y, self.y)) * 2 + pick(core, self.core), pick(x, self.x))

    def step(self, axis, d):
        return self.at(**{axis: lax.rem(self.pos[axis] + d, self.size[axis])})

    def is_self(self, place):
        return jnp.logical_and(place[0] == self.core, place[1] == self.x)


def remote(source, target, send, recv, device):
    return pltpu.make_async_remote_copy(src_ref=source, dst_ref=target, send_sem=send, recv_sem=recv,
                                        device_id=device, device_id_type=MESH)


class GradReduce:
    def __init__(self, links, grad, out, result, bufs, sems):
        self.result = result
        self.links, self.grad, self.both, self.out = links, grad, out, out.at[links.core]
        (self.relay1, self.fin1, self.mid, self.relay2, self.fin2, self.z_src, self.z_recv, self.z_out) = bufs
        self.rs_sems, self.ag_sems, self.z_sems, self.swap_sems, self.store_sems = sems

    def axes(self, rnd, unit):
        first = ORDER[rnd][unit]
        return first, ('x' if first == 'y' else 'y')

    def scatter(self, rnd, unit, phase):
        links = self.links
        axis = self.axes(rnd, unit)[phase]
        pos = links.pos[axis]
        right, left, across = (lax.rem(pos + k, RING) for k in (1, RING - 1, 2))
        to_right, to_left = links.step(axis, 1), links.step(axis, RING - 1)
        low, high = pl.ds(0, SPLIT), pl.ds(SPLIT, 640 - SPLIT)
        if phase == 0:
            rows, relay, fin = 32, self.relay1.at[rnd, unit], self.fin1.at[rnd, unit]
            first = rnd * ROUND_ROWS + unit * 128
            src = lambda owner: self.grad.at[pl.ds(pl.multiple_of(first + owner * 32, 8), 32)]
        else:
            rows, relay, fin = 8, self.relay2.at[rnd, unit], self.fin2.at[rnd, unit]
            src = lambda owner: self.mid.at[rnd, unit, pl.ds(pl.multiple_of(owner * 8, 8), 8)]
        every = pl.ds(0, rows)
        send = lambda k: self.rs_sems.at[0, rnd, unit, phase, k]
        recv = lambda k: self.rs_sems.at[1, rnd, unit, phase, k]
        copies = [remote(src(across).at[every, low], relay.at[every, low], send(0), recv(0), to_right),
                  remote(src(across).at[every, high], relay.at[every, high], send(1), recv(1), to_left),
                  remote(src(right).at[every, high], fin.at[0, every, high], send(2), recv(2), to_right),
                  remote(src(left).at[every, low], fin.at[1, every, low], send(3), recv(3), to_left),
                  remote(relay.at[every, low], fin.at[0, every, low], send(4), recv(4), to_right),
                  remote(relay.at[every, high], fin.at[1, every, high], send(5), recv(5), to_left)]
        return copies, src, relay, fin, pos, right, left, low, high

    def scatter_start(self, rnd, unit, phase):
        copies = self.scatter(rnd, unit, phase)[0]
        for copy in copies[:4]:
            copy.start()

    def scatter_relay(self, rnd, unit, phase):
        copies, src, relay, _, _, right, left, low, high = self.scatter(rnd, unit, phase)
        for k, owner, cols in ((0, right, low), (1, left, high)):
            copies[k].wait_recv()
            relay[:, cols] = relay[:, cols] + src(owner)[:, cols]
            copies[4 + k].start()

    def scatter_end(self, rnd, unit, phase):
        copies, src, _, fin, pos = self.scatter(rnd, unit, phase)[:5]
        for k in (2, 3, 4, 5):
            copies[k].wait_recv()
        for copy in copies:
            copy.wait_send()
        return src(pos)[...] + (fin[0] + fin[1])

    def gather(self, rnd, unit, phase):
        links = self.links
        order = self.axes(rnd, unit)
        axis = order[phase]
        pos = links.pos[axis]
        rows = 32 if phase == 0 else 8
        first = rnd * ROUND_ROWS + unit * 128
        if phase == 1:
            first = first + links.pos[order[0]] * 32
        right, left = lax.rem(pos + 1, RING), lax.rem(pos + RING - 1, RING)
        to_right, to_left = links.step(axis, 1), links.step(axis, RING - 1)
        low, high, every = pl.ds(0, SPLIT), pl.ds(SPLIT, 640 - SPLIT), pl.ds(0, 640)

        def copy(k, block, cols, device):
            part = self.out.at[pl.ds(pl.multiple_of(first + block * rows, 8), rows), cols]
            return remote(part, part, self.ag_sems.at[0, rnd, unit, phase, k], self.ag_sems.at[1, rnd, unit, phase, k], device)

        return [copy(0, pos, every, to_right), copy(1, pos, every, to_left),
                copy(2, left, low, to_right), copy(3, right, high, to_left)]

    def gather_start(self, rnd, unit, phase):
        for copy in self.gather(rnd, unit, phase)[:2]:
            copy.start()

    def gather_relay(self, rnd, unit, phase):
        copies = self.gather(rnd, unit, phase)
        for k in (0, 1):
            copies[k].wait_recv()
            copies[k + 2].start()

    def gather_end(self, rnd, unit, phase):
        copies = self.gather(rnd, unit, phase)
        for k in (2, 3):
            copies[k].wait_recv()
        for copy in copies:
            copy.wait_send()

    def z_copies(self, rnd, way):
        links = self.links
        each = 16 // links.depth
        send, recv = self.z_sems.at[0, rnd, way], self.z_sems.at[1, rnd, way]
        mine = pl.ds(links.z * each, each)
        copies = []
        for d in range(1, links.depth):
            far = lax.rem(links.z + d, links.depth)
            if way == 0:
                source, target = self.z_src.at[rnd, pl.ds(far * each, each)], self.z_recv.at[rnd, d - 1]
            else:
                source = target = self.z_out.at[rnd, mine]
            copies.append(remote(source, target, send, recv, links.step('z', d)))
        return copies, mine

    def z_wait(self, rnd, way):
        if self.links.depth > 1:
            whole = self.z_recv.at[rnd]
            all_of = remote(whole, whole, self.z_sems.at[0, rnd, way], self.z_sems.at[1, rnd, way], self.links.step('z', 1))
            all_of.wait_recv()
            all_of.wait_send()

    def swap(self, rnd):
        part = self.out.at[pl.ds(rnd * ROUND_ROWS, ROUND_ROWS)]
        return remote(part, part, self.swap_sems.at[0, rnd], self.swap_sems.at[1, rnd], self.links.peer)

    def stage(self, rnd, k):
        units = (0, 1)
        if k == 0:
            for u in units:
                self.scatter_start(rnd, u, 0)
        elif k == 1:
            for u in units:
                self.scatter_relay(rnd, u, 0)
        elif k == 2:
            for u in units:
                self.mid[rnd, u] = self.scatter_end(rnd, u, 0)
                self.scatter_start(rnd, u, 1)
        elif k == 3:
            for u in units:
                self.scatter_relay(rnd, u, 1)
        elif k == 4:
            for u in units:
                total = self.scatter_end(rnd, u, 1)
                for j in range(5):
                    self.z_src[rnd, u * 5 + j] = total[:, j * 128:(j + 1) * 128]
            self.z_src[rnd, pl.ds(10, 6)] = jnp.zeros((6, 8, 128), F32)
            for copy in self.z_copies(rnd, 0)[0]:
                copy.start()
        elif k == 5:
            self.z_wait(rnd, 0)
            copies, mine = self.z_copies(rnd, 1)
            total = self.z_src[rnd, mine]
            for d in range(self.links.depth - 1):
                total = total + self.z_recv[rnd, d]
            self.z_out[rnd, mine] = total
            for copy in copies:
                copy.start()
        elif k == 6:
            self.z_wait(rnd, 1)
            for u in units:
                order = self.axes(rnd, u)
                first = rnd * ROUND_ROWS + u * 128 + self.links.pos[order[0]] * 32 + self.links.pos[order[1]] * 8
                for j in range(5):
                    self.out[pl.ds(pl.multiple_of(first, 8), 8), pl.ds(j * 128, 128)] = self.z_out[rnd, u * 5 + j]
                self.gather_start(rnd, u, 1)
        elif k == 7:
            for u in units:
                self.gather_relay(rnd, u, 1)
        elif k == 8:
            for u in units:
                self.gather_end(rnd, u, 1)
                self.gather_start(rnd, u, 0)
        elif k == 9:
            for u in units:
                self.gather_relay(rnd, u, 0)
        elif k == 10:
            for u in units:
                self.gather_end(rnd, u, 0)
            self.swap(rnd).start()
        else:
            self.swap(rnd).wait()
            self.store(rnd).start()

    def store(self, rnd):
        rows = pl.ds(rnd * ROUND_ROWS, ROUND_ROWS)
        return pltpu.make_async_copy(self.both.at[:, rows], self.result.at[:, rows], self.store_sems.at[rnd])


def backward_body(scale, group, depth, qt_ref, kt_ref, vt_ref, do_ref, lse_ref, delta_ref,
                  normed_ref, dy_ref, ot_ref, x_ref, wt_ref, gamma_ref, gx_ref, out_ref, small_ref,
                  k_s, v_s, dk_acc, dv_acc, grads, grads_peer, d_w, d_w_all, dx_s,
                  relay1, fin1, mid, relay2, fin2, z_src, z_recv, z_out, small_s, small_recv,
                  rs_sems, ag_sems, z_sems, swap_sems, store_sems, grad_sems, gx_send, gx_recv, small_sems):
    head, step = pl.program_id(0), pl.program_id(1)
    heads, steps = 4, kt_ref.shape[1] // (Q_BLOCK * group)
    now = head * steps + step
    dim, tokens = kt_ref.shape
    own = tokens // 2
    width = heads * dim
    tiles = tokens // KEY_TILE
    log2_scale = scale * math.log2(math.e)
    links = Links(depth)
    reduce = GradReduce(links, d_w, d_w_all, out_ref, (relay1, fin1, mid, relay2, fin2, z_src, z_recv, z_out),
                        (rs_sems, ag_sems, z_sems, swap_sems, store_sems))
    head_rows = pl.ds(pl.multiple_of(head * dim, 16), dim)

    def swap_grads(h):
        rows = pl.ds(pl.multiple_of(h * dim, 16), dim)
        return remote(grads.at[:, rows, pl.ds(own, own)], grads_peer.at[:, rows], grad_sems.at[0, h], grad_sems.at[1, h], links.peer)

    @pl.when(now == 0)
    def _():
        barrier = pltpu.get_barrier_semaphore()
        fixed = [links.peer]
        fixed += [links.step(axis, d) for axis in ('x', 'y') for d in (1, 2, 3)]
        fixed += [links.step('z', d) for d in range(1, depth)]
        for device in fixed:
            pl.semaphore_signal(barrier, inc=1, device_id=device, device_id_type=MESH)
        count = len(fixed)
        for place in links.owners + links.workers:
            other = jnp.logical_not(links.is_self(place))
            count = count + other.astype(jnp.int32)

            @pl.when(other)
            def _():
                pl.semaphore_signal(barrier, inc=1, device_id=links.at(core=place[0], x=place[1]), device_id_type=MESH)
        pl.semaphore_wait(barrier, count)
        d_w[pl.ds(0, width)] = dot_nn(ot_ref[...], dy_ref[...])

    for at in range(heads * steps):
        todo = [(rnd, at - rnd * steps) for rnd in range(ROUNDS - 1) if 0 <= at - rnd * steps <= 11]
        if todo:
            @pl.when(now == at)
            def _():
                for rnd, k in todo:
                    reduce.stage(rnd, k)

    @pl.when(step == 0)
    def _():
        minus = jnp.concatenate([jnp.full((3, tokens), -1.0, F32), jnp.zeros((AUG - dim - 3, tokens), F32)], axis=0).astype(BF)
        k_s[...] = jnp.concatenate([kt_ref[...], minus], axis=0).T
        v_s[...] = jnp.concatenate([vt_ref[...], minus], axis=0).T
        dk_acc[...] = jnp.zeros_like(dk_acc)
        dv_acc[...] = jnp.zeros_like(dv_acc)

    def rows_of(tile):
        return pl.ds(tile * KEY_TILE, KEY_TILE)

    total = tiles * group
    ops, probs, d_scores, dq = {}, {}, {}, {}
    for g in range(total + 2):
        if g < total:
            i, t = divmod(g, tiles)
            if t == 0:
                cols = pl.ds(pl.multiple_of((step * group + i) * Q_BLOCK, Q_BLOCK), Q_BLOCK)
                q_t, do_t = qt_ref[:, cols], do_ref[:, cols]
                ops[i] = (cols, q_t, do_t, jnp.concatenate([q_t, lse_ref[:, cols]], axis=0),
                          jnp.concatenate([do_t, delta_ref[:, cols]], axis=0))
            scores = dot_nn(k_s[rows_of(t), :], ops[i][3])
            d_probs = dot_nn(v_s[rows_of(t), :], ops[i][4])
            prob = jnp.exp2(scores * log2_scale)
            probs[g] = prob.astype(BF)
            d_scores[g] = (prob * d_probs).astype(BF)
        if g >= 2:
            i, t = divmod(g - 2, tiles)
            cols, q_t, do_t = ops[i][:3]
            dv_acc[:, rows_of(t)] += dot_nt(do_t, probs[g - 2])
            part = dot_nn(kt_ref[:, rows_of(t)], d_scores[g - 2])
            dq[i] = part if t == 0 else dq[i] + part
            if t == tiles - 1:
                grads[0, head_rows, cols] = (dq[i] * scale).astype(BF)
            dk_acc[:, rows_of(t)] += dot_nt(q_t, d_scores[g - 2])

    @pl.when(step == steps - 1)
    def _():
        grads[1, head_rows] = (dk_acc[...] * scale).astype(BF)
        grads[2, head_rows] = dv_acc[...].astype(BF)
        stacked = jnp.concatenate([grads[0, head_rows], grads[1, head_rows], grads[2, head_rows]], axis=0)
        d_w[pl.ds(pl.multiple_of(width + head * (3 * dim), 8), 3 * dim)] = dot_nn(stacked, normed_ref[...])
        swap_grads(head).start()

    @pl.when(now == heads * steps - 1)
    def _():
        def tail(slot):
            last = heads * steps + slot
            for rnd in range(ROUNDS):
                if 0 <= last - rnd * steps <= 11:
                    reduce.stage(rnd, last - rnd * steps)

        tail(0)
        for h in range(heads):
            swap_grads(h).wait()
        gamma = gamma_ref[...]
        sums = [jnp.zeros((1, 640), F32)] * 3
        band = own // 2
        piece = band // 2
        odd = lax.rem(links.x, 2)

        def send_dx(i, start):
            core, x = links.owners[i // 2]
            source = dx_s.at[pl.ds(i * piece, piece)]
            target = gx_ref.at[odd, pl.ds((i % 2) * piece, piece)]
            far = remote(source, target, gx_send.at[i], gx_recv.at[odd, i % 2], links.at(core=core, x=x))
            near = pltpu.make_async_copy(source, target, gx_recv.at[odd, i % 2])
            here = links.is_self((core, x))

            @pl.when(jnp.logical_not(here))
            def _():
                far.start() if start else far.wait_send()

            if start:
                @pl.when(here)
                def _():
                    near.start()

        for i in range(4):
            toks = pl.ds(i * piece, piece)
            mine = jnp.concatenate([grads[k, :, toks] for k in range(3)], axis=0)
            theirs = jnp.concatenate([grads_peer[k, :, toks] for k in range(3)], axis=0)
            d_normed = (dot_tn(mine, wt_ref[0]) + dot_tn(theirs, wt_ref[1])).astype(BF).astype(F32)
            x_f = x_ref[toks].astype(F32)
            centered = x_f - jnp.mean(x_f, axis=-1, keepdims=True)
            inv_std = lax.rsqrt(jnp.mean(centered * centered, axis=-1, keepdims=True) + LN_EPS)
            x_hat = centered * inv_std
            d_hat = d_normed * gamma
            mean_one = jnp.mean(d_hat, axis=-1, keepdims=True)
            mean_two = jnp.mean(d_hat * x_hat, axis=-1, keepdims=True)
            dy_f = dy_ref[toks].astype(F32)
            dx_s[toks] = (dy_f + inv_std * (d_hat - mean_one - x_hat * mean_two)).astype(BF)
            send_dx(i, True)
            for k, term in enumerate((d_normed * x_hat, d_normed, dy_f)):
                sums[k] = sums[k] + jnp.sum(term, axis=0, keepdims=True)
            tail(1 + i)

        for k in range(3):
            for j in range(5):
                small_s[0, pl.ds(k * 5 + j, 1)] = sums[k][:, j * 128:(j + 1) * 128]
        small_s[0, pl.ds(15, 1)] = jnp.zeros((1, 128), F32)
        first = 0
        for hop, axis in enumerate(('x', 'y', 'z', 'core')):
            far = [links.peer] if axis == 'core' else [links.step(axis, d) for d in range(1, links.size[axis])]
            copies = [remote(small_s.at[hop], small_recv.at[first + d], small_sems.at[0, first + d], small_sems.at[1, first + d], device)
                      for d, device in enumerate(far)]
            for copy in copies:
                copy.start()
            tail(5 + hop)
            acc = small_s[hop]
            for d, copy in enumerate(copies):
                copy.wait_recv()
                acc = acc + small_recv[first + d]
            for copy in copies:
                copy.wait_send()
            if hop < 3:
                small_s[hop + 1] = acc
            else:
                small_ref[...] = acc
            first += len(far)
        for slot in range(9, 12):
            tail(slot)
        for rnd in range(ROUNDS):
            reduce.store(rnd).wait()
        for i in range(4):
            send_dx(i, False)
        for m in range(2):
            for i in range(2):
                part = gx_ref.at[m, pl.ds(i * piece, piece)]
                pltpu.make_async_copy(part, part, gx_recv.at[m, i]).wait()


def attention_backward(q_t, k_t, v_t, do_t, lse, delta, normed, dy, o_t, x_own, w_t, gamma, head_dim, depth, group=2):
    width, tokens = q_t.shape
    heads = width // head_dim
    channels = normed.shape[1]
    own = tokens // 2
    full = pl.BlockSpec((head_dim, tokens), lambda h, j: (h, 0))
    stat = pl.BlockSpec((16, tokens), lambda h, j: (h, 0))

    def whole(shape):
        return pl.BlockSpec(shape, lambda h, j: (0,) * len(shape), pipeline_mode=pl.Buffered(1))

    vm = lambda *shape: pltpu.VMEM(shape, F32)
    dma = pltpu.SemaphoreType.DMA
    far = max(depth - 1, 1)
    return pl.pallas_call(
        functools.partial(backward_body, head_dim ** -0.5, group, depth),
        grid=(heads, tokens // (Q_BLOCK * group)),
        in_specs=[full] * 4 + [stat] * 2 + [whole(a.shape) for a in (normed, dy, o_t, x_own, w_t, gamma)],
        out_specs=[pl.BlockSpec(memory_space=pl.ANY)] * 2 + [whole((16, 128))],
        out_shape=[jax.ShapeDtypeStruct((2, own // 2, channels), BF), jax.ShapeDtypeStruct((2, 1280, channels), F32),
                   jax.ShapeDtypeStruct((16, 128), F32)],
        scratch_shapes=[pltpu.VMEM((tokens, AUG), BF)] * 2 + [vm(head_dim, tokens)] * 2
        + [pltpu.VMEM((3, width, tokens), BF), pltpu.VMEM((3, width, own), BF), vm(1280, channels), vm(2, 1280, channels), pltpu.VMEM((own, channels), BF),
           vm(ROUNDS, 2, 32, channels), vm(ROUNDS, 2, 2, 32, channels), vm(ROUNDS, 2, 32, channels),
           vm(ROUNDS, 2, 8, channels), vm(ROUNDS, 2, 2, 8, channels), vm(ROUNDS, 16, 8, 128),
           vm(ROUNDS, far, 16 // depth, 8, 128), vm(ROUNDS, 16, 8, 128), vm(4, 16, 128), vm(7 + far, 16, 128),
           dma((2, ROUNDS, 2, 2, 6)), dma((2, ROUNDS, 2, 2, 4)), dma((2, ROUNDS, 2)), dma((2, ROUNDS)), dma((ROUNDS,)), dma((2, 4)),
           dma((4,)), dma((2, 2)), dma((2, 7 + far))],
        compiler_params=pltpu.CompilerParams(collective_id=0, has_side_effects=True, vmem_limit_bytes=60 * 2 ** 20),
        cost_estimate=pl.CostEstimate(flops=10 * heads * tokens * tokens * head_dim, bytes_accessed=16 * width * tokens,
                                      transcendentals=heads * tokens * tokens),
        name='attention_backward',
    )(q_t, k_t, v_t, do_t, lse, delta, normed, dy, o_t, x_own, w_t, gamma)


def solution(mesh):
    dp_size = mesh.shape['dp']
    cp_size = mesh.shape['cp']
    axes = ('dp', 'cp')
    act_spec = P('dp', 'cp', None)
    rep_spec = P()

    def index_of(dp, cp):
        return dp * cp_size + cp

    send_same, send_cross, swap = [], [], []
    for dp in range(dp_size):
        group, core = dp // 2, dp % 2
        for cp in range(cp_size):
            half, parity = cp // 2, cp % 2
            send_same.append((index_of(dp, cp), index_of(2 * group + half, 2 * core + parity)))
            send_cross.append((index_of(dp, cp), index_of(2 * group + half, 2 * core + 1 - parity)))
            swap.append((index_of(dp, cp), index_of(dp ^ 1, cp)))
    back_same = [(dst, src) for src, dst in send_same]
    back_cross = [(dst, src) for src, dst in send_cross]

    def device_step(x_in, grad_y, ln_gamma, ln_beta, w_q, w_k, w_v, w_o, b_o):
        channels = x_in.shape[2]
        num_heads, head_dim = w_q.shape[1], w_q.shape[2]
        half_heads = num_heads // 2
        width = half_heads * head_dim
        core = lax.rem(lax.axis_index('dp'), 2)
        parity = lax.rem(lax.axis_index('cp'), 2)

        def permute(value, pairs):
            return lax.ppermute(value, axes, pairs)

        def gather_image(band_pair):
            first = lax.dynamic_index_in_dim(band_pair, parity, 0, keepdims=False)
            second = lax.dynamic_index_in_dim(band_pair, 1 - parity, 0, keepdims=False)
            own_a, own_b = permute(first, send_same), permute(second, send_cross)
            return own_a, own_b, permute(own_a, swap), permute(own_b, swap)

        def head_slice(weight, which):
            return lax.dynamic_slice_in_dim(weight, which * half_heads, half_heads, 1).reshape(channels, width)

        def out_slice(which):
            return lax.dynamic_slice_in_dim(w_o, which * half_heads, half_heads, 0).reshape(width, channels)

        x_parts = gather_image(x_in)
        dy_parts = gather_image(grad_y)
        x_all = jnp.concatenate(x_parts, axis=0)
        dy_all = jnp.concatenate(dy_parts, axis=0)
        tokens = x_all.shape[0]
        own = tokens // 2

        x_f = x_all.astype(F32)
        mean = jnp.mean(x_f, axis=-1, keepdims=True)
        centered = x_f - mean
        inv_std = lax.rsqrt(jnp.mean(centered * centered, axis=-1, keepdims=True) + LN_EPS)
        normed = (centered * inv_std * ln_gamma + ln_beta).astype(BF)

        wq_mine, wk_mine, wv_mine = (head_slice(w, core) for w in (w_q, w_k, w_v))
        wq_other, wk_other, wv_other = (head_slice(w, 1 - core) for w in (w_q, w_k, w_v))
        wo_mine, wo_other = out_slice(core), out_slice(1 - core)

        w_t = jnp.stack([jnp.concatenate([wq_mine, wk_mine, wv_mine], axis=1).T,
                         jnp.concatenate([wq_other, wk_other, wv_other], axis=1).T])

        def project(weight):
            return lax.dot_general(weight, normed, (((0,), (1,)), ((), ())), preferred_element_type=F32).astype(BF)

        q_t, k_t, v_t = project(wq_mine), project(wk_mine), project(wv_mine)
        o_t, o_f, lse = attention_forward(q_t, k_t, v_t, head_dim)
        o_peer = permute(o_t[:, own:], swap)
        do_t = dot_nt(wo_mine, dy_all).astype(BF)
        delta = jnp.sum((o_f * do_t.astype(F32)).reshape(half_heads, head_dim, tokens), axis=1)
        delta = jnp.pad(jnp.stack(split_parts(delta), axis=1), ((0, 0), (0, 13), (0, 0))).reshape(half_heads * 16, tokens)
        y_f = x_all[:own].astype(F32) + (dot_tn(o_t[:, :own], wo_mine) + dot_tn(o_peer, wo_other)) + b_o
        y_own, delta = lax.optimization_barrier((y_f.astype(BF), delta))
        y_same = permute(y_own[:own // 2], back_same)
        y_cross = permute(y_own[own // 2:], back_cross)
        grad_x, both, small = attention_backward(q_t, k_t, v_t, do_t, lse, delta, normed, dy_all, o_t, x_all[:own], w_t,
                                                 ln_gamma.reshape(1, channels), head_dim, dp_size // 8)
        y_out = jnp.where(parity == 0, jnp.stack([y_same, y_cross]), jnp.stack([y_cross, y_same]))
        small = small[:15].reshape(3, channels)
        grad_wo = both[:, :width].reshape(num_heads, head_dim, channels)
        both = both[:, width:].reshape(num_heads, 3, head_dim, channels)
        grads = [jnp.transpose(both[:, i], (2, 0, 1)) for i in range(3)]
        return (y_out, grad_x, small[0], small[1], grads[0], grads[1], grads[2], grad_wo, small[2])

    return jax.shard_map(device_step, mesh=mesh,
                         in_specs=(act_spec, act_spec) + (rep_spec,) * 7,
                         out_specs=(act_spec, act_spec) + (rep_spec,) * 7,
                         check_vma=False)
```

time: 440 us -> 239 us (0.54)
  waiting for transfers between devices: 181 us -> 11.7 us
  blocking collectives: 83.9 us -> 0 us
  Pallas kernels: 71.4 us -> 155 us
  matrix products: 21.6 us -> 6.95 us
  between operations: 14.6 us -> 1.19 us
    psum x1 -> x0, waiting for transfers between devices: 155 us -> none  [device_step(): both, small = lax.psum((both, small), axes)]
    psum x1 -> x0, blocking collectives: 83.9 us -> none  [device_step(): both, small = lax.psum((both, small), axes)]
    pallas_call x1 -> x2, Pallas kernels: 71.4 us -> 155 us  [the longest x1 136 us: attention_backward(): pl.pallas_call(functools.partial(backward_body, head_dim ** (-0.5), group...]
    ppermute x14 -> x11, waiting for transfers between devices: 26.6 us -> 11.7 us  [permute(): return lax.ppermute(value, axes, pairs)]
    dot_general x4 -> x0, matrix products: 12.4 us -> none  [the longest x2 4.39 us: dot_nn(): lax.dot_general(lhs, rhs, (((1,), (0,)), ((), ())), preferred_element_typ...]
    select_n x3 -> x1, other arithmetic: 8.72 us -> 1.29 us  [device_step(): jnp.where(parity == 0, jnp.stack([y_same, y_cross]), jnp.stack([y_cross,...]
    sub x1 -> x0, other arithmetic: 5.32 us -> none  [device_step(): centered = x_f - mean]
    reduce_sum x1 -> x2, other arithmetic: 1.71 us -> 6.16 us  [the longest x1 4.15 us: device_step(): jnp.mean(centered * centered, axis=-1, keepdims=True) + LN_EPS]
  transfers between devices with their start and end apart: 15 -> 11, of which waited for: 6 -> 4; matrix products, arithmetic and copies ran while one was open for 11% -> 18% of each run, Pallas kernels for 0% -> 65%
where the time goes in v4:
time: 239 us; the launch traced here: 238 us
  Pallas kernels  155 us (65%)
  local copies, waits for them, and re-layouts  22.2 us (9%)
  starting transfers between devices  20.4 us (9%)
  other arithmetic  20.4 us (9%)
  waiting for transfers between devices  11.7 us (5%)
  matrix products  6.95 us (3%)
    pallas_call x1, Pallas kernels, attention_backward(): pl.pallas_call(functools.partial(backward_body, head_dim ** (-0.5), group...  136 us
    ppermute x11, starting transfers between devices, permute(): return lax.ppermute(value, axes, pairs)  20.4 us
    pallas_call x1, Pallas kernels, attention_forward(): pl.pallas_call(functools.partial(forward_body, head_dim ** (-0.5), group)...  18.9 us
    ppermute x11, waiting for transfers between devices, permute(): return lax.ppermute(value, axes, pairs)  11.7 us
    convert_element_type x1, other arithmetic, device_step(): normed = (centered * inv_std * ln_gamma + ln_beta).astype(BF)  5.09 us
  transfers between devices with their start and end apart: 11, of which 4 were waited for; matrix products, arithmetic and copies ran while one was open for 18% of the time, Pallas kernels for 65%

profile of v4, /device:TPU:1, one launch (start us, length us, event | category | flops | bytes accessed | tf_op | source)
XLA Modules:
  0.0 237.8 jit_solution(6535116068603526494)
XLA Ops:
  0.7 2.6 %dynamic-slice_bitcast_fusion.3 = (bf16[512,640]{1,0:T(8,128)(2,1)}, bf16[512,640]{1,0:T(8,128)(2,1)}) fusion(bf16[2,512,640]{2,1,0:T(8,128)(2,1)} %param.9, s32[]{:T(128)S(6)} %select_n.30, s32[]{:T(128)S(6)} %select_n.31), kind=kLoop, calls=%fused_computation.27 | loop fusion | bytes 2621448 | tf_op jit(solution)/shard_map/jit(dynamic_index_in_dim)/squeeze | solution.py:586
  3.3 3.9 %collective-permute-start.1 = (bf16[512,640]{1,0:T(8,128)(2,1)}, bf16[512,640]{1,0:T(8,128)(2,1)S(1)}, u32[]{:S(2)}, u32[]{:S(2)}) collective-permute-start(bf16[512,640]{1,0:T(8,128)(2,1)} %get-tuple-element.33), channel_id=1, source_target_pairs={{0,1},{1,0},{2,5},{3,4},{4,3},{5,2},{6,7},{7,6},{8,9},{9,8},{10,13... | collective-permute-start | bytes 1966088 | tf_op jit(solution)/shard_map/ppermute | solution.py:583
  7.1 2.2 collective-permute-start
  10.5 4.9 %collective-permute-start.5 = (bf16[512,640]{1,0:T(8,128)(2,1)}, bf16[512,640]{1,0:T(8,128)(2,1)}, u32[]{:S(2)}, u32[]{:S(2)}) collective-permute-start(bf16[512,640]{1,0:T(8,128)(2,1)} %get-tuple-element.31), channel_id=1, source_target_pairs={{0,0},{1,1},{2,4},{3,5},{4,2},{5,3},{6,6},{7,7},{8,8},{9,9},{10,12... | collective-permute-start | bytes 1966088 | tf_op jit(solution)/shard_map/ppermute | solution.py:583
  18.2 1.4 collective-permute-done.1
  19.7 3.4 %collective-permute-start.3 = (bf16[512,640]{1,0:T(8,128)(2,1)S(1)}, bf16[512,640]{1,0:T(8,128)(2,1)S(1)}, u32[]{:S(2)}, u32[]{:S(2)}) collective-permute-start(bf16[512,640]{1,0:T(8,128)(2,1)S(1)} %collective-permute-done.1), channel_id=1, source_target_pairs={{0,4},{1,5},{2,6},{3,7},{4,0},{5,1},{6,2},{7,3},{8,12},{9,13},{10,... | collective-permute-start | bytes 1966088 | tf_op jit(solution)/shard_map/ppermute | solution.py:583
  23.1 3.9 %collective-permute-done = bf16[512,640]{1,0:T(8,128)(2,1)S(1)} collective-permute-done((bf16[512,640]{1,0:T(8,128)(2,1)}, bf16[512,640]{1,0:T(8,128)(2,1)S(1)}, u32[]{:S(2)}, u32[]{:S(2)}) %collective-permute-start) | collective-permute-done | bytes 655392 | tf_op jit(solution)/shard_map/ppermute | solution.py:583
  27.1 1.7 pad_maximum_fusion.1.wt_ref
  29.4 1.9 constant_dynamic-slice_fusion.3
  31.3 5.9 %collective-permute-done.5 = bf16[512,640]{1,0:T(8,128)(2,1)} collective-permute-done((bf16[512,640]{1,0:T(8,128)(2,1)}, bf16[512,640]{1,0:T(8,128)(2,1)}, u32[]{:S(2)}, u32[]{:S(2)}) %collective-permute-start.5) | collective-permute-done | bytes 655392 | tf_op jit(solution)/shard_map/ppermute | solution.py:583
  39.0 1.7 constant_dynamic-update-slice_fusion.4
  40.7 3.1 %convert_reduce_fusion = f32[2048]{0:T(1024)S(1)} fusion(bf16[512,640]{1,0:T(8,128)(2,1)S(1)} %collective-permute-done.3, bf16[512,640]{1,0:T(8,128)(2,1)S(1)} %collective-permute-done.2, bf16[512,640]{1,0:T(8,128)(2,1)S(1)} %collective-permute-done.1, bf16[512,640]{1,0:T(8,128)(2,1)S(1)} %collective-permute-done), kind=kLoop, calls=%fused_computation.1 | loop fusion | flops 11794432 | bytes 2629632 | tf_op jit(solution)/shard_map/reduce_sum | solution.py:605
  43.9 4.2 %fusion.2 = f32[2048]{0:T(1024)S(1)} fusion(f32[2048]{0:T(1024)S(1)} %broadcast_multiply_fusion, bf16[512,640]{1,0:T(8,128)(2,1)S(1)} %collective-permute-done.3, bf16[512,640]{1,0:T(8,128)(2,1)S(1)} %collective-permute-done.2, bf16[512,640]{1,0:T(8,128)(2,1)S(1)} %collective-permute-done.1, bf16[512,640]{1,0:T(8,128)(2,1)S(1)} %collective-permute-done), kind=kLoop, calls=%fused_computation.4 | loop fusion | flops 14415872 | bytes 2637824 | tf_op jit(solution)/shard_map/reduce_sum | solution.py:607
  48.1 5.1 %fusion.5.normed_ref = bf16[2048,640]{1,0:T(8,128)(2,1)S(1)} fusion(f32[640]{0:T(1024)S(1)} %copy-done.20, f32[640]{0:T(1024)S(1)} %copy-done.19, f32[2048]{0:T(1024)S(1)} %add_rsqrt_fusion, f32[2048]{0:T(1024)S(1)} %broadcast_multiply_fusion, bf16[512,640]{1,0:T(8,128)(2,1)S(1)} %collective-permute-done.3, bf16[512,640]{1,0:T(8,128)(2,1)S(1)} %collective-permute-done.2, ...), kind=kLoop, calls=%fused_computation.7 | loop fusion | flops 17039360 | bytes 5264384 | tf_op jit(solution)/shard_map/convert_element_type | solution.py:608
  56.9 18.9 %attention_forward.1 = (bf16[320,2048]{1,0:T(8,128)(2,1)S(1)}, f32[320,2048]{1,0:T(8,128)S(1)}, bf16[64,2048]{1,0:T(8,128)(2,1)S(1)}) custom-call(bf16[320,2048]{1,0:T(8,128)(2,1)S(1)} %convolution_convert_fusion.3.qt_ref, bf16[320,2048]{1,0:T(8,128)(2,1)S(1)} %convolution_convert_fusion.2.kt_ref, bf16[320,2048]{1,0:T(8,128)(2,1)S(1)} %convolution_convert_fusion.1.vt_ref), custom_call_target="tpu_custom_call" | custom-call | flops 5368709120 | bytes 7864320 | tf_op jit(solution)/shard_map/attention_forward/pallas_call | solution.py:102
  78.4 1.9 convert_multiply_fusion
  80.3 2.0 reduce_sum.31
  85.5 3.2 %collective-permute-start.10 = (bf16[512,640]{1,0:T(8,128)(2,1)S(1)}, bf16[512,640]{1,0:T(8,128)(2,1)S(1)}, u32[]{:S(2)}, u32[]{:S(2)}) collective-permute-start(bf16[512,640]{1,0:T(8,128)(2,1)S(1)} %get-tuple-element.29), channel_id=1, source_target_pairs={{1,0},{0,1},{5,2},{4,3},{3,4},{2,5},{7,6},{6,7},{9,8},{8,9},{13,10... | collective-permute-start | bytes 1966088 | tf_op jit(solution)/shard_map/ppermute | solution.py:583
  88.7 1.9 collective-permute-start.9
  90.7 136.1 %attention_backward.1 = (bf16[2,512,640]{2,1,0:T(8,128)(2,1)}, f32[2,1280,640]{2,1,0:T(8,128)}, f32[16,128]{1,0:T(8,128)}) custom-call(bf16[320,2048]{1,0:T(8,128)(2,1)} %copy-done.1, bf16[320,2048]{1,0:T(8,128)(2,1)} %copy-done.2, bf16[320,2048]{1,0:T(8,128)(2,1)} %copy-done.3, bf16[320,2048]{1,0:T(8,128)(2,1)} %copy-done.15, bf16[64,2048]{1,0:T(8,128)(2,1)} %copy-done.4, ...), custom_call_target="tpu_custom_call" | custom-call | flops 13421772800 | bytes 10485760 | tf_op jit(solution)/shard_map/attention_backward/pallas_call | solution.py:532
  226.7 2.7 %slice.52 = f32[2,960,640]{2,1,0:T(8,128)S(1)} slice(f32[2,1280,640]{2,1,0:T(8,128)} %get-tuple-element.24), slice={[0:2], [320:1280], [0:640]} | slice | bytes 9830400 | tf_op jit(solution)/shard_map/slice | solution.py:635
  229.4 2.7 %slice.56 = f32[2,320,640]{2,1,0:T(8,128)} slice(f32[2,1280,640]{2,1,0:T(8,128)} %get-tuple-element.24), slice={[0:2], [0:320], [0:640]} | slice | bytes 3276800 | tf_op jit(solution)/shard_map/slice | solution.py:634
  232.8 2.3 slice_bitcast_fusion
  235.1 1.3 maximum_select_fusion
  (83 shorter events, 17.6 us)
Async XLA Ops:
  0.6 8.7 %copy-start.13 = (bf16[2,512,640]{2,1,0:T(8,128)(2,1)S(1)}, bf16[2,512,640]{2,1,0:T(8,128)(2,1)}, u32[]{:S(2)}) copy-start(bf16[2,512,640]{2,1,0:T(8,128)(2,1)} %param.10) | copy-start | bytes 3932164
  0.7 14.8 %copy-start.16 = (bf16[640,8,80]{0,2,1:T(8,128)(2,1)S(1)}, bf16[640,8,80]{0,2,1:T(8,128)(2,1)}, u32[]{:S(2)}) copy-start(bf16[640,8,80]{0,2,1:T(8,128)(2,1)} %param.15) | copy-start | bytes 2457604
  3.3 16.4 %collective-permute-start.1 = (bf16[512,640]{1,0:T(8,128)(2,1)}, bf16[512,640]{1,0:T(8,128)(2,1)S(1)}, u32[]{:S(2)}, u32[]{:S(2)}) collective-permute-start(bf16[512,640]{1,0:T(8,128)(2,1)} %get-tuple-element.33), channel_id=1, source_target_pairs={{0,1},{1,0},{2,5},{3,4},{4,3},{5,2},{6,7},{7,6},{8,9},{9,8},{10,13... | collective-permute-start | bytes 1966088 | tf_op jit(solution)/shard_map/ppermute | solution.py:583
  7.1 19.9 %collective-permute-start = (bf16[512,640]{1,0:T(8,128)(2,1)}, bf16[512,640]{1,0:T(8,128)(2,1)S(1)}, u32[]{:S(2)}, u32[]{:S(2)}) collective-permute-start(bf16[512,640]{1,0:T(8,128)(2,1)} %get-tuple-element.32), channel_id=1, source_target_pairs={{0,0},{1,1},{2,4},{3,5},{4,2},{5,3},{6,6},{7,7},{8,8},{9,9},{10,12... | collective-permute-start | bytes 1966088 | tf_op jit(solution)/shard_map/ppermute | solution.py:583
  10.5 26.7 %collective-permute-start.5 = (bf16[512,640]{1,0:T(8,128)(2,1)}, bf16[512,640]{1,0:T(8,128)(2,1)}, u32[]{:S(2)}, u32[]{:S(2)}) collective-permute-start(bf16[512,640]{1,0:T(8,128)(2,1)} %get-tuple-element.31), channel_id=1, source_target_pairs={{0,0},{1,1},{2,4},{3,5},{4,2},{5,3},{6,6},{7,7},{8,8},{9,9},{10,12... | collective-permute-start | bytes 1966088 | tf_op jit(solution)/shard_map/ppermute | solution.py:583
  15.4 22.2 %collective-permute-start.6 = (bf16[512,640]{1,0:T(8,128)(2,1)}, bf16[512,640]{1,0:T(8,128)(2,1)}, u32[]{:S(2)}, u32[]{:S(2)}) collective-permute-start(bf16[512,640]{1,0:T(8,128)(2,1)} %get-tuple-element.30), channel_id=1, source_target_pairs={{0,1},{1,0},{2,5},{3,4},{4,3},{5,2},{6,7},{7,6},{8,9},{9,8},{10,13... | collective-permute-start | bytes 1966088 | tf_op jit(solution)/shard_map/ppermute | solution.py:583
  18.0 5.1 %copy-start.10 = (bf16[640,4,80]{0,2,1:T(8,128)(2,1)}, bf16[640,4,80]{0,2,1:T(8,128)(2,1)S(1)}, u32[]{:S(2)}) copy-start(bf16[640,4,80]{0,2,1:T(8,128)(2,1)S(1)} %get-tuple-element.35) | copy-start | bytes 1228804
  18.2 10.6 %copy-start.19 = (f32[640]{0:T(1024)S(1)}, f32[640]{0:T(1024)}, u32[]{:S(2)}) copy-start(f32[640]{0:T(1024)} %param.11) | copy-start | bytes 7684
  19.7 21.0 %collective-permute-start.3 = (bf16[512,640]{1,0:T(8,128)(2,1)S(1)}, bf16[512,640]{1,0:T(8,128)(2,1)S(1)}, u32[]{:S(2)}, u32[]{:S(2)}) collective-permute-start(bf16[512,640]{1,0:T(8,128)(2,1)S(1)} %collective-permute-done.1), channel_id=1, source_target_pairs={{0,4},{1,5},{2,6},{3,7},{4,0},{5,1},{6,2},{7,3},{8,12},{9,13},{10,... | collective-permute-start | bytes 1966088 | tf_op jit(solution)/shard_map/ppermute | solution.py:583
  27.0 13.7 %collective-permute-start.2 = (bf16[512,640]{1,0:T(8,128)(2,1)S(1)}, bf16[512,640]{1,0:T(8,128)(2,1)S(1)}, u32[]{:S(2)}, u32[]{:S(2)}) collective-permute-start(bf16[512,640]{1,0:T(8,128)(2,1)S(1)} %collective-permute-done), channel_id=1, source_target_pairs={{0,4},{1,5},{2,6},{3,7},{4,0},{5,1},{6,2},{7,3},{8,12},{9,13},{10,... | collective-permute-start | bytes 1966088 | tf_op jit(solution)/shard_map/ppermute | solution.py:583
  31.3 45.6 %copy-start.8 = (bf16[4,80,640]{2,1,0:T(8,128)(2,1)}, bf16[4,80,640]{2,1,0:T(8,128)(2,1)S(1)}, u32[]{:S(2)}) copy-start(bf16[4,80,640]{2,1,0:T(8,128)(2,1)S(1)} %get-tuple-element.41) | copy-start | bytes 1228804
  37.2 39.5 %collective-permute-start.7 = (bf16[512,640]{1,0:T(8,128)(2,1)}, bf16[512,640]{1,0:T(8,128)(2,1)S(1)}, u32[]{:S(2)}, u32[]{:S(2)}) collective-permute-start(bf16[512,640]{1,0:T(8,128)(2,1)} %collective-permute-done.5), channel_id=1, source_target_pairs={{0,4},{1,5},{2,6},{3,7},{4,0},{5,1},{6,2},{7,3},{8,12},{9,13},{10,... | collective-permute-start | bytes 1966088 | tf_op jit(solution)/shard_map/ppermute | solution.py:583
  37.6 39.2 %collective-permute-start.8 = (bf16[512,640]{1,0:T(8,128)(2,1)}, bf16[512,640]{1,0:T(8,128)(2,1)S(1)}, u32[]{:S(2)}, u32[]{:S(2)}) collective-permute-start(bf16[512,640]{1,0:T(8,128)(2,1)} %collective-permute-done.6), channel_id=1, source_target_pairs={{0,4},{1,5},{2,6},{3,7},{4,0},{5,1},{6,2},{7,3},{8,12},{9,13},{10,... | collective-permute-start | bytes 1966088 | tf_op jit(solution)/shard_map/ppermute | solution.py:583
  40.7 7.3 %copy-start.20 = (f32[640]{0:T(1024)S(1)}, f32[640]{0:T(1024)}, u32[]{:S(2)}) copy-start(f32[640]{0:T(1024)} %param.12) | copy-start | bytes 7684
  48.1 5.1 %copy-start.11 = (bf16[640,4,80]{0,2,1:T(8,128)(2,1)S(1)}, bf16[640,4,80]{0,2,1:T(8,128)(2,1)}, u32[]{:S(2)}) copy-start(bf16[640,4,80]{0,2,1:T(8,128)(2,1)} %copy-done.10) | copy-start | bytes 1228804
  53.2 2.5 %copy-start.7 = (bf16[2048,640]{1,0:T(8,128)(2,1)}, bf16[2048,640]{1,0:T(8,128)(2,1)S(1)}, u32[]{:S(2)}) copy-start(bf16[2048,640]{1,0:T(8,128)(2,1)S(1)} %fusion.5.normed_ref) | copy-start | bytes 7864324
  54.4 2.5 %copy-start.1 = (bf16[320,2048]{1,0:T(8,128)(2,1)}, bf16[320,2048]{1,0:T(8,128)(2,1)S(1)}, u32[]{:S(2)}) copy-start(bf16[320,2048]{1,0:T(8,128)(2,1)S(1)} %convolution_convert_fusion.3.qt_ref) | copy-start | bytes 3932164
  56.9 19.0 %copy-start.3 = (bf16[320,2048]{1,0:T(8,128)(2,1)}, bf16[320,2048]{1,0:T(8,128)(2,1)S(1)}, u32[]{:S(2)}) copy-start(bf16[320,2048]{1,0:T(8,128)(2,1)S(1)} %convolution_convert_fusion.1.vt_ref) | copy-start | bytes 3932164
  75.9 7.3 %copy-start = (bf16[320,2048]{1,0:T(8,128)(2,1)}, bf16[320,2048]{1,0:T(8,128)(2,1)S(1)}, u32[]{:S(2)}) copy-start(bf16[320,2048]{1,0:T(8,128)(2,1)S(1)} %get-tuple-element.17.ot_ref) | copy-start | bytes 3932164
  76.0 8.2 %collective-permute-start.4 = (bf16[320,1024]{1,0:T(8,128)(2,1)S(1)}, bf16[320,1024]{1,0:T(8,128)(2,1)S(1)}, u32[]{:S(2)}, u32[]{:S(2)}) collective-permute-start(bf16[320,1024]{1,0:T(8,128)(2,1)S(1)} %slice.47), channel_id=1, source_target_pairs={{0,4},{1,5},{2,6},{3,7},{4,0},{5,1},{6,2},{7,3},{8,12},{9,13},{10,... | collective-permute-start | bytes 1966088 | tf_op jit(solution)/shard_map/ppermute | solution.py:583
  80.3 3.0 %copy-start.9 = (bf16[4,80,640]{2,1,0:T(8,128)(2,1)S(1)}, bf16[4,80,640]{2,1,0:T(8,128)(2,1)}, u32[]{:S(2)}) copy-start(bf16[4,80,640]{2,1,0:T(8,128)(2,1)} %copy-done.8) | copy-start | bytes 1228804
  85.5 149.6 %collective-permute-start.10 = (bf16[512,640]{1,0:T(8,128)(2,1)S(1)}, bf16[512,640]{1,0:T(8,128)(2,1)S(1)}, u32[]{:S(2)}, u32[]{:S(2)}) collective-permute-start(bf16[512,640]{1,0:T(8,128)(2,1)S(1)} %get-tuple-element.29), channel_id=1, source_target_pairs={{1,0},{0,1},{5,2},{4,3},{3,4},{2,5},{7,6},{6,7},{9,8},{8,9},{13,10... | collective-permute-start | bytes 1966088 | tf_op jit(solution)/shard_map/ppermute | solution.py:583
  88.7 146.4 %collective-permute-start.9 = (bf16[512,640]{1,0:T(8,128)(2,1)S(1)}, bf16[512,640]{1,0:T(8,128)(2,1)S(1)}, u32[]{:S(2)}, u32[]{:S(2)}) collective-permute-start(bf16[512,640]{1,0:T(8,128)(2,1)S(1)} %get-tuple-element.28), channel_id=1, source_target_pairs={{0,0},{1,1},{4,2},{5,3},{2,4},{3,5},{6,6},{7,7},{8,8},{9,9},{12,10... | collective-permute-start | bytes 1966088 | tf_op jit(solution)/shard_map/ppermute | solution.py:583
  229.4 2.7 %copy-start.18 = (f32[16,128]{1,0:T(8,128)S(1)}, f32[16,128]{1,0:T(8,128)}, u32[]{:S(2)}) copy-start(f32[16,128]{1,0:T(8,128)} %get-tuple-element.23) | copy-start | bytes 24580
  (9 other events, 16.0 us)

commit v5 on v4

--- a/solution.py
+++ b/solution.py
@@ -118,7 +118,7 @@
 RING = 4
 ROUNDS = 5
 ROUND_ROWS = 256
-SPLIT = 384
+STAGES = 8
 ORDER = (('y', 'x'), ('y', 'x'), ('y', 'x'), ('y', 'y'), ('y', 'x'))
 
 
@@ -154,96 +154,55 @@
 
 class GradReduce:
     def __init__(self, links, grad, out, result, bufs, sems):
-        self.result = result
-        self.links, self.grad, self.both, self.out = links, grad, out, out.at[links.core]
-        (self.relay1, self.fin1, self.mid, self.relay2, self.fin2, self.z_src, self.z_recv, self.z_out) = bufs
+        self.links, self.grad, self.both, self.out, self.result = links, grad, out, out.at[links.core], result
+        self.recv1, self.recv2, self.mid, self.z_src, self.z_recv, self.z_out = bufs
         self.rs_sems, self.ag_sems, self.z_sems, self.swap_sems, self.store_sems = sems
 
     def axes(self, rnd, unit):
         first = ORDER[rnd][unit]
         return first, ('x' if first == 'y' else 'y')
 
-    def scatter(self, rnd, unit, phase):
-        links = self.links
+    def block(self, rnd, unit, phase):
+        first = rnd * ROUND_ROWS + unit * 128
+        if phase == 0:
+            return first, 32
+        return first + self.links.pos[self.axes(rnd, unit)[0]] * 32, 8
+
+    def landing(self, rnd, unit, phase):
+        return (self.recv1 if phase == 0 else self.recv2).at[rnd, unit]
+
+    def wait_all(self, rnd, unit, phase, sems):
+        whole = self.landing(rnd, unit, phase)
+        every = remote(whole, whole, sems.at[0, rnd, unit, phase], sems.at[1, rnd, unit, phase], self.links.peer)
+        every.wait_recv()
+        every.wait_send()
+
+    def source(self, rnd, unit, phase, owner):
+        if phase == 0:
+            first, rows = self.block(rnd, unit, 0)
+            return self.grad.at[pl.ds(pl.multiple_of(first + owner * rows, 8), rows)]
+        return self.mid.at[rnd, unit, pl.ds(pl.multiple_of(owner * 8, 8), 8)]
+
+    def scatter_start(self, rnd, unit, phase):
         axis = self.axes(rnd, unit)[phase]
-        pos = links.pos[axis]
-        right, left, across = (lax.rem(pos + k, RING) for k in (1, RING - 1, 2))
-        to_right, to_left = links.step(axis, 1), links.step(axis, RING - 1)
-        low, high = pl.ds(0, SPLIT), pl.ds(SPLIT, 640 - SPLIT)
-        if phase == 0:
-            rows, relay, fin = 32, self.relay1.at[rnd, unit], self.fin1.at[rnd, unit]
-            first = rnd * ROUND_ROWS + unit * 128
-            src = lambda owner: self.grad.at[pl.ds(pl.multiple_of(first + owner * 32, 8), 32)]
-        else:
-            rows, relay, fin = 8, self.relay2.at[rnd, unit], self.fin2.at[rnd, unit]
-            src = lambda owner: self.mid.at[rnd, unit, pl.ds(pl.multiple_of(owner * 8, 8), 8)]
-        every = pl.ds(0, rows)
-        send = lambda k: self.rs_sems.at[0, rnd, unit, phase, k]
-        recv = lambda k: self.rs_sems.at[1, rnd, unit, phase, k]
-        copies = [remote(src(across).at[every, low], relay.at[every, low], send(0), recv(0), to_right),
-                  remote(src(across).at[every, high], relay.at[every, high], send(1), recv(1), to_left),
-                  remote(src(right).at[every, high], fin.at[0, every, high], send(2), recv(2), to_right),
-                  remote(src(left).at[every, low], fin.at[1, every, low], send(3), recv(3), to_left),
-                  remote(relay.at[every, low], fin.at[0, every, low], send(4), recv(4), to_right),
-                  remote(relay.at[every, high], fin.at[1, every, high], send(5), recv(5), to_left)]
-        return copies, src, relay, fin, pos, right, left, low, high
-
-    def scatter_start(self, rnd, unit, phase):
-        copies = self.scatter(rnd, unit, phase)[0]
-        for copy in copies[:4]:
-            copy.start()
-
-    def scatter_relay(self, rnd, unit, phase):
-        copies, src, relay, _, _, right, left, low, high = self.scatter(rnd, unit, phase)
-        for k, owner, cols in ((0, right, low), (1, left, high)):
-            copies[k].wait_recv()
-            relay[:, cols] = relay[:, cols] + src(owner)[:, cols]
-            copies[4 + k].start()
+        for d in (2, 1, 3):
+            owner = lax.rem(self.links.pos[axis] + d, RING)
+            remote(self.source(rnd, unit, phase, owner), self.landing(rnd, unit, phase).at[d - 1],
+                   self.rs_sems.at[0, rnd, unit, phase], self.rs_sems.at[1, rnd, unit, phase], self.links.step(axis, d)).start()
 
     def scatter_end(self, rnd, unit, phase):
-        copies, src, _, fin, pos = self.scatter(rnd, unit, phase)[:5]
-        for k in (2, 3, 4, 5):
-            copies[k].wait_recv()
-        for copy in copies:
-            copy.wait_send()
-        return src(pos)[...] + (fin[0] + fin[1])
-
-    def gather(self, rnd, unit, phase):
-        links = self.links
-        order = self.axes(rnd, unit)
-        axis = order[phase]
-        pos = links.pos[axis]
-        rows = 32 if phase == 0 else 8
-        first = rnd * ROUND_ROWS + unit * 128
-        if phase == 1:
-            first = first + links.pos[order[0]] * 32
-        right, left = lax.rem(pos + 1, RING), lax.rem(pos + RING - 1, RING)
-        to_right, to_left = links.step(axis, 1), links.step(axis, RING - 1)
-        low, high, every = pl.ds(0, SPLIT), pl.ds(SPLIT, 640 - SPLIT), pl.ds(0, 640)
-
-        def copy(k, block, cols, device):
-            part = self.out.at[pl.ds(pl.multiple_of(first + block * rows, 8), rows), cols]
-            return remote(part, part, self.ag_sems.at[0, rnd, unit, phase, k], self.ag_sems.at[1, rnd, unit, phase, k], device)
-
-        return [copy(0, pos, every, to_right), copy(1, pos, every, to_left),
-                copy(2, left, low, to_right), copy(3, right, high, to_left)]
+        self.wait_all(rnd, unit, phase, self.rs_sems)
+        landing = self.landing(rnd, unit, phase)
+        mine = self.source(rnd, unit, phase, self.links.pos[self.axes(rnd, unit)[phase]])
+        return (mine[...] + landing[0]) + (landing[1] + landing[2])
 
     def gather_start(self, rnd, unit, phase):
-        for copy in self.gather(rnd, unit, phase)[:2]:
-            copy.start()
-
-    def gather_relay(self, rnd, unit, phase):
-        copies = self.gather(rnd, unit, phase)
-        for k in (0, 1):
-            copies[k].wait_recv()
-            copies[k + 2].start()
-
-    def gather_end(self, rnd, unit, phase):
-        copies = self.gather(rnd, unit, phase)
-        for k in (2, 3):
-            copies[k].wait_recv()
-        for copy in copies:
-            copy.wait_send()
+        axis = self.axes(rnd, unit)[phase]
+        first, rows = self.block(rnd, unit, phase)
+        part = self.out.at[pl.ds(pl.multiple_of(first + self.links.pos[axis] * rows, 8), rows)]
+        for d in (2, 1, 3):
+            remote(part, part, self.ag_sems.at[0, rnd, unit, phase], self.ag_sems.at[1, rnd, unit, phase],
+                   self.links.step(axis, d)).start()
 
     def z_copies(self, rnd, way):
         links = self.links
@@ -271,6 +230,10 @@
         part = self.out.at[pl.ds(rnd * ROUND_ROWS, ROUND_ROWS)]
         return remote(part, part, self.swap_sems.at[0, rnd], self.swap_sems.at[1, rnd], self.links.peer)
 
+    def store(self, rnd):
+        rows = pl.ds(rnd * ROUND_ROWS, ROUND_ROWS)
+        return pltpu.make_async_copy(self.both.at[:, rows], self.result.at[:, rows], self.store_sems.at[rnd])
+
     def stage(self, rnd, k):
         units = (0, 1)
         if k == 0:
@@ -278,15 +241,9 @@
                 self.scatter_start(rnd, u, 0)
         elif k == 1:
             for u in units:
-                self.scatter_relay(rnd, u, 0)
-        elif k == 2:
-            for u in units:
                 self.mid[rnd, u] = self.scatter_end(rnd, u, 0)
                 self.scatter_start(rnd, u, 1)
-        elif k == 3:
-            for u in units:
-                self.scatter_relay(rnd, u, 1)
-        elif k == 4:
+        elif k == 2:
             for u in units:
                 total = self.scatter_end(rnd, u, 1)
                 for j in range(5):
@@ -294,7 +251,7 @@
             self.z_src[rnd, pl.ds(10, 6)] = jnp.zeros((6, 8, 128), F32)
             for copy in self.z_copies(rnd, 0)[0]:
                 copy.start()
-        elif k == 5:
+        elif k == 3:
             self.z_wait(rnd, 0)
             copies, mine = self.z_copies(rnd, 1)
             total = self.z_src[rnd, mine]
@@ -303,41 +260,31 @@
             self.z_out[rnd, mine] = total
             for copy in copies:
                 copy.start()
-        elif k == 6:
+        elif k == 4:
             self.z_wait(rnd, 1)
             for u in units:
-                order = self.axes(rnd, u)
-                first = rnd * ROUND_ROWS + u * 128 + self.links.pos[order[0]] * 32 + self.links.pos[order[1]] * 8
+                first = self.block(rnd, u, 1)[0] + self.links.pos[self.axes(rnd, u)[1]] * 8
                 for j in range(5):
                     self.out[pl.ds(pl.multiple_of(first, 8), 8), pl.ds(j * 128, 128)] = self.z_out[rnd, u * 5 + j]
                 self.gather_start(rnd, u, 1)
-        elif k == 7:
+        elif k == 5:
             for u in units:
-                self.gather_relay(rnd, u, 1)
-        elif k == 8:
+                self.wait_all(rnd, u, 1, self.ag_sems)
+                self.gather_start(rnd, u, 0)
+        elif k == 6:
             for u in units:
-                self.gather_end(rnd, u, 1)
-                self.gather_start(rnd, u, 0)
-        elif k == 9:
-            for u in units:
-                self.gather_relay(rnd, u, 0)
-        elif k == 10:
-            for u in units:
-                self.gather_end(rnd, u, 0)
+                self.wait_all(rnd, u, 0, self.ag_sems)
             self.swap(rnd).start()
         else:
             self.swap(rnd).wait()
             self.store(rnd).start()
 
-    def store(self, rnd):
-        rows = pl.ds(rnd * ROUND_ROWS, ROUND_ROWS)
-        return pltpu.make_async_copy(self.both.at[:, rows], self.result.at[:, rows], self.store_sems.at[rnd])
-
 
 def backward_body(scale, group, depth, qt_ref, kt_ref, vt_ref, do_ref, lse_ref, delta_ref,
-                  normed_ref, dy_ref, ot_ref, x_ref, wt_ref, gamma_ref, gx_ref, out_ref, small_ref,
+                  normed_hbm, dy_hbm, ot_hbm, x_hbm, wt_hbm, gamma_ref, gx_ref, out_ref, small_ref,
+                  normed_ref, dy_ref, ot_ref, x_ref, wt_ref, load_sems,
                   k_s, v_s, dk_acc, dv_acc, grads, grads_peer, d_w, d_w_all, dx_s,
-                  relay1, fin1, mid, relay2, fin2, z_src, z_recv, z_out, small_s, small_recv,
+                  recv1, recv2, mid, z_src, z_recv, z_out, small_s, small_recv,
                   rs_sems, ag_sems, z_sems, swap_sems, store_sems, grad_sems, gx_send, gx_recv, small_sems):
     head, step = pl.program_id(0), pl.program_id(1)
     heads, steps = 4, kt_ref.shape[1] // (Q_BLOCK * group)
@@ -348,7 +295,7 @@
     tiles = tokens // KEY_TILE
     log2_scale = scale * math.log2(math.e)
     links = Links(depth)
-    reduce = GradReduce(links, d_w, d_w_all, out_ref, (relay1, fin1, mid, relay2, fin2, z_src, z_recv, z_out),
+    reduce = GradReduce(links, d_w, d_w_all, out_ref, (recv1, recv2, mid, z_src, z_recv, z_out),
                         (rs_sems, ag_sems, z_sems, swap_sems, store_sems))
     head_rows = pl.ds(pl.multiple_of(head * dim, 16), dim)
 
@@ -356,27 +303,50 @@
         rows = pl.ds(pl.multiple_of(h * dim, 16), dim)
         return remote(grads.at[:, rows, pl.ds(own, own)], grads_peer.at[:, rows], grad_sems.at[0, h], grad_sems.at[1, h], links.peer)
 
+    fixed = [links.peer]
+    fixed += [links.step(axis, d) for axis in ('x', 'y') for d in (1, 2, 3)]
+    fixed += [links.step('z', d) for d in range(1, depth)]
+    places = links.owners + links.workers
+    peer_count = len(fixed)
+    for place in places:
+        peer_count = peer_count + jnp.logical_not(links.is_self(place)).astype(jnp.int32)
+    loads = [pltpu.make_async_copy(source, target, load_sems.at[i]) for i, (source, target) in enumerate(
+        ((ot_hbm, ot_ref), (dy_hbm, dy_ref), (normed_hbm, normed_ref), (x_hbm, x_ref), (wt_hbm, wt_ref)))]
+
     @pl.when(now == 0)
     def _():
         barrier = pltpu.get_barrier_semaphore()
-        fixed = [links.peer]
-        fixed += [links.step(axis, d) for axis in ('x', 'y') for d in (1, 2, 3)]
-        fixed += [links.step('z', d) for d in range(1, depth)]
         for device in fixed:
             pl.semaphore_signal(barrier, inc=1, device_id=device, device_id_type=MESH)
-        count = len(fixed)
-        for place in links.owners + links.workers:
+        for place in places:
             other = jnp.logical_not(links.is_self(place))
-            count = count + other.astype(jnp.int32)
 
             @pl.when(other)
             def _():
                 pl.semaphore_signal(barrier, inc=1, device_id=links.at(core=place[0], x=place[1]), device_id_type=MESH)
-        pl.semaphore_wait(barrier, count)
+        for load in loads:
+            load.start()
+
+    @pl.when(now == 1)
+    def _():
+        pl.semaphore_wait(pltpu.get_barrier_semaphore(), peer_count)
+        loads[0].wait()
+        loads[1].wait()
         d_w[pl.ds(0, width)] = dot_nn(ot_ref[...], dy_ref[...])
 
-    for at in range(heads * steps):
-        todo = [(rnd, at - rnd * steps) for rnd in range(ROUNDS - 1) if 0 <= at - rnd * steps <= 11]
+    end = heads * steps
+    plan, ahead = {}, [0] * ROUNDS
+    for at in range(1, end + STAGES):
+        due = []
+        for rnd in range(ROUNDS):
+            wait = at - max(rnd * steps, 1)
+            if ahead[rnd] < STAGES and wait >= 0 and (at >= end or wait % 2 == 0):
+                due.append((rnd, ahead[rnd]))
+                ahead[rnd] += 1
+        plan[at] = due if at > end else due[::-1]
+
+    for at in range(1, heads * steps):
+        todo = plan[at]
         if todo:
             @pl.when(now == at)
             def _():
@@ -423,6 +393,11 @@
     def _():
         grads[1, head_rows] = (dk_acc[...] * scale).astype(BF)
         grads[2, head_rows] = dv_acc[...].astype(BF)
+
+        @pl.when(head == 0)
+        def _():
+            loads[2].wait()
+
         stacked = jnp.concatenate([grads[0, head_rows], grads[1, head_rows], grads[2, head_rows]], axis=0)
         d_w[pl.ds(pl.multiple_of(width + head * (3 * dim), 8), 3 * dim)] = dot_nn(stacked, normed_ref[...])
         swap_grads(head).start()
@@ -431,13 +406,14 @@
     def _():
         def tail(slot):
             last = heads * steps + slot
-            for rnd in range(ROUNDS):
-                if 0 <= last - rnd * steps <= 11:
-                    reduce.stage(rnd, last - rnd * steps)
+            for rnd, k in plan[last]:
+                reduce.stage(rnd, k)
 
         tail(0)
         for h in range(heads):
             swap_grads(h).wait()
+        loads[3].wait()
+        loads[4].wait()
         gamma = gamma_ref[...]
         sums = [jnp.zeros((1, 640), F32)] * 3
         band = own // 2
@@ -491,7 +467,8 @@
                       for d, device in enumerate(far)]
             for copy in copies:
                 copy.start()
-            tail(5 + hop)
+            if 5 + hop < STAGES:
+                tail(5 + hop)
             acc = small_s[hop]
             for d, copy in enumerate(copies):
                 copy.wait_recv()
@@ -503,8 +480,6 @@
             else:
                 small_ref[...] = acc
             first += len(far)
-        for slot in range(9, 12):
-            tail(slot)
         for rnd in range(ROUNDS):
             reduce.store(rnd).wait()
         for i in range(4):
@@ -532,16 +507,16 @@
     return pl.pallas_call(
         functools.partial(backward_body, head_dim ** -0.5, group, depth),
         grid=(heads, tokens // (Q_BLOCK * group)),
-        in_specs=[full] * 4 + [stat] * 2 + [whole(a.shape) for a in (normed, dy, o_t, x_own, w_t, gamma)],
+        in_specs=[full] * 4 + [stat] * 2 + [pl.BlockSpec(memory_space=pl.ANY)] * 5 + [whole(gamma.shape)],
         out_specs=[pl.BlockSpec(memory_space=pl.ANY)] * 2 + [whole((16, 128))],
         out_shape=[jax.ShapeDtypeStruct((2, own // 2, channels), BF), jax.ShapeDtypeStruct((2, 1280, channels), F32),
                    jax.ShapeDtypeStruct((16, 128), F32)],
-        scratch_shapes=[pltpu.VMEM((tokens, AUG), BF)] * 2 + [vm(head_dim, tokens)] * 2
+        scratch_shapes=[pltpu.VMEM(a.shape, BF) for a in (normed, dy, o_t, x_own, w_t)] + [dma((5,))]
+        + [pltpu.VMEM((tokens, AUG), BF)] * 2 + [vm(head_dim, tokens)] * 2
         + [pltpu.VMEM((3, width, tokens), BF), pltpu.VMEM((3, width, own), BF), vm(1280, channels), vm(2, 1280, channels), pltpu.VMEM((own, channels), BF),
-           vm(ROUNDS, 2, 32, channels), vm(ROUNDS, 2, 2, 32, channels), vm(ROUNDS, 2, 32, channels),
-           vm(ROUNDS, 2, 8, channels), vm(ROUNDS, 2, 2, 8, channels), vm(ROUNDS, 16, 8, 128),
+           vm(ROUNDS, 2, 3, 32, channels), vm(ROUNDS, 2, 3, 8, channels), vm(ROUNDS, 2, 32, channels), vm(ROUNDS, 16, 8, 128),
            vm(ROUNDS, far, 16 // depth, 8, 128), vm(ROUNDS, 16, 8, 128), vm(4, 16, 128), vm(7 + far, 16, 128),
-           dma((2, ROUNDS, 2, 2, 6)), dma((2, ROUNDS, 2, 2, 4)), dma((2, ROUNDS, 2)), dma((2, ROUNDS)), dma((ROUNDS,)), dma((2, 4)),
+           dma((2, ROUNDS, 2, 2)), dma((2, ROUNDS, 2, 2)), dma((2, ROUNDS, 2)), dma((2, ROUNDS)), dma((ROUNDS,)), dma((2, 4)),
            dma((4,)), dma((2, 2)), dma((2, 7 + far))],
         compiler_params=pltpu.CompilerParams(collective_id=0, has_side_effects=True, vmem_limit_bytes=60 * 2 ** 20),
         cost_estimate=pl.CostEstimate(flops=10 * heads * tokens * tokens * head_dim, bytes_accessed=16 * width * tokens,

time: 239 us -> 215 us (0.90)
  Pallas kernels: 155 us -> 132 us
    pallas_call x1, Pallas kernels: 136 us -> 113 us  [attention_backward(): pl.pallas_call(functools.partial(backward_body, head_dim ** (-0.5), group...]
  transfers between devices with their start and end apart: 11 -> 11, of which waited for: 4 -> 4; matrix products, arithmetic and copies ran while one was open for 18% -> 20% of each run, Pallas kernels for 65% -> 61%
where the time goes in v5:
time: 215 us
  Pallas kernels  132 us (61%)
  local copies, waits for them, and re-layouts  22.2 us (10%)
  starting transfers between devices  20.4 us (9%)
  other arithmetic  20.4 us (9%)
  waiting for transfers between devices  11.7 us (5%)
  matrix products  6.95 us (3%)
    pallas_call x1, Pallas kernels, attention_backward(): pl.pallas_call(functools.partial(backward_body, head_dim ** (-0.5), group...  113 us
    ppermute x11, starting transfers between devices, permute(): return lax.ppermute(value, axes, pairs)  20.4 us
    pallas_call x1, Pallas kernels, attention_forward(): pl.pallas_call(functools.partial(forward_body, head_dim ** (-0.5), group)...  18.9 us
    ppermute x11, waiting for transfers between devices, permute(): return lax.ppermute(value, axes, pairs)  11.7 us
    convert_element_type x1, other arithmetic, device_step(): normed = (centered * inv_std * ln_gamma + ln_beta).astype(BF)  5.09 us
    unnamed x49, local copies, waits for them, and re-layouts  4.68 us
  transfers between devices with their start and end apart: 11, of which 4 were waited for; matrix products, arithmetic and copies ran while one was open for 20% of the time, Pallas kernels for 61%

profile of v5, /device:TPU:1, one launch (start us, length us, event | category | flops | bytes accessed | tf_op | source)
XLA Modules:
  0.0 214.5 jit_solution(13908041428025422103)
XLA Ops:
  0.7 2.6 %dynamic-slice_bitcast_fusion.3 = (bf16[512,640]{1,0:T(8,128)(2,1)}, bf16[512,640]{1,0:T(8,128)(2,1)}) fusion(bf16[2,512,640]{2,1,0:T(8,128)(2,1)} %param.9, s32[]{:T(128)S(6)} %select_n.30, s32[]{:T(128)S(6)} %select_n.31), kind=kLoop, calls=%fused_computation.27 | loop fusion | bytes 2621448 | tf_op jit(solution)/shard_map/jit(dynamic_index_in_dim)/squeeze | solution.py:561
  3.3 3.9 %collective-permute-start.1 = (bf16[512,640]{1,0:T(8,128)(2,1)}, bf16[512,640]{1,0:T(8,128)(2,1)S(1)}, u32[]{:S(2)}, u32[]{:S(2)}) collective-permute-start(bf16[512,640]{1,0:T(8,128)(2,1)} %get-tuple-element.33), channel_id=1, source_target_pairs={{0,1},{1,0},{2,5},{3,4},{4,3},{5,2},{6,7},{7,6},{8,9},{9,8},{10,13... | collective-permute-start | bytes 1966088 | tf_op jit(solution)/shard_map/ppermute | solution.py:558
  7.1 2.2 %collective-permute-start = (bf16[512,640]{1,0:T(8,128)(2,1)}, bf16[512,640]{1,0:T(8,128)(2,1)S(1)}, u32[]{:S(2)}, u32[]{:S(2)}) collective-permute-start(bf16[512,640]{1,0:T(8,128)(2,1)} %get-tuple-element.32), channel_id=1, source_target_pairs={{0,0},{1,1},{2,4},{3,5},{4,2},{5,3},{6,6},{7,7},{8,8},{9,9},{10,12... | collective-permute-start | bytes 1966088 | tf_op jit(solution)/shard_map/ppermute | solution.py:558
  10.5 4.9 %collective-permute-start.5 = (bf16[512,640]{1,0:T(8,128)(2,1)}, bf16[512,640]{1,0:T(8,128)(2,1)}, u32[]{:S(2)}, u32[]{:S(2)}) collective-permute-start(bf16[512,640]{1,0:T(8,128)(2,1)} %get-tuple-element.31), channel_id=1, source_target_pairs={{0,0},{1,1},{2,4},{3,5},{4,2},{5,3},{6,6},{7,7},{8,8},{9,9},{10,12... | collective-permute-start | bytes 1966088 | tf_op jit(solution)/shard_map/ppermute | solution.py:558
  18.2 1.4 collective-permute-done.1
  19.7 3.4 %collective-permute-start.3 = (bf16[512,640]{1,0:T(8,128)(2,1)S(1)}, bf16[512,640]{1,0:T(8,128)(2,1)S(1)}, u32[]{:S(2)}, u32[]{:S(2)}) collective-permute-start(bf16[512,640]{1,0:T(8,128)(2,1)S(1)} %collective-permute-done.1), channel_id=1, source_target_pairs={{0,4},{1,5},{2,6},{3,7},{4,0},{5,1},{6,2},{7,3},{8,12},{9,13},{10,... | collective-permute-start | bytes 1966088 | tf_op jit(solution)/shard_map/ppermute | solution.py:558
  23.1 3.9 %collective-permute-done = bf16[512,640]{1,0:T(8,128)(2,1)S(1)} collective-permute-done((bf16[512,640]{1,0:T(8,128)(2,1)}, bf16[512,640]{1,0:T(8,128)(2,1)S(1)}, u32[]{:S(2)}, u32[]{:S(2)}) %collective-permute-start) | collective-permute-done | bytes 655392 | tf_op jit(solution)/shard_map/ppermute | solution.py:558
  27.1 1.7 pad_maximum_fusion.1.wt_hbm
  29.4 1.9 constant_dynamic-slice_fusion.3
  31.3 5.9 %collective-permute-done.5 = bf16[512,640]{1,0:T(8,128)(2,1)} collective-permute-done((bf16[512,640]{1,0:T(8,128)(2,1)}, bf16[512,640]{1,0:T(8,128)(2,1)}, u32[]{:S(2)}, u32[]{:S(2)}) %collective-permute-start.5) | collective-permute-done | bytes 655392 | tf_op jit(solution)/shard_map/ppermute | solution.py:558
  39.0 1.7 constant_dynamic-update-slice_fusion.4
  40.7 3.1 %convert_reduce_fusion = f32[2048]{0:T(1024)S(1)} fusion(bf16[512,640]{1,0:T(8,128)(2,1)S(1)} %collective-permute-done.3, bf16[512,640]{1,0:T(8,128)(2,1)S(1)} %collective-permute-done.2, bf16[512,640]{1,0:T(8,128)(2,1)S(1)} %collective-permute-done.1, bf16[512,640]{1,0:T(8,128)(2,1)S(1)} %collective-permute-done), kind=kLoop, calls=%fused_computation.1 | loop fusion | flops 11794432 | bytes 2629632 | tf_op jit(solution)/shard_map/reduce_sum | solution.py:580
  43.9 4.2 %fusion.2 = f32[2048]{0:T(1024)S(1)} fusion(f32[2048]{0:T(1024)S(1)} %broadcast_multiply_fusion, bf16[512,640]{1,0:T(8,128)(2,1)S(1)} %collective-permute-done.3, bf16[512,640]{1,0:T(8,128)(2,1)S(1)} %collective-permute-done.2, bf16[512,640]{1,0:T(8,128)(2,1)S(1)} %collective-permute-done.1, bf16[512,640]{1,0:T(8,128)(2,1)S(1)} %collective-permute-done), kind=kLoop, calls=%fused_computation.4 | loop fusion | flops 14415872 | bytes 2637824 | tf_op jit(solution)/shard_map/reduce_sum | solution.py:582
  48.1 5.1 %fusion.5.normed_hbm = bf16[2048,640]{1,0:T(8,128)(2,1)S(1)} fusion(f32[640]{0:T(1024)S(1)} %copy-done.20, f32[640]{0:T(1024)S(1)} %copy-done.19, f32[2048]{0:T(1024)S(1)} %add_rsqrt_fusion, f32[2048]{0:T(1024)S(1)} %broadcast_multiply_fusion, bf16[512,640]{1,0:T(8,128)(2,1)S(1)} %collective-permute-done.3, bf16[512,640]{1,0:T(8,128)(2,1)S(1)} %collective-permute-done.2, ...), kind=kLoop, calls=%fused_computation.7 | loop fusion | flops 17039360 | bytes 5264384 | tf_op jit(solution)/shard_map/convert_element_type | solution.py:583
  56.9 18.9 %attention_forward.1 = (bf16[320,2048]{1,0:T(8,128)(2,1)S(1)}, f32[320,2048]{1,0:T(8,128)S(1)}, bf16[64,2048]{1,0:T(8,128)(2,1)S(1)}) custom-call(bf16[320,2048]{1,0:T(8,128)(2,1)S(1)} %convolution_convert_fusion.3.qt_ref, bf16[320,2048]{1,0:T(8,128)(2,1)S(1)} %convolution_convert_fusion.2.kt_ref, bf16[320,2048]{1,0:T(8,128)(2,1)S(1)} %convolution_convert_fusion.1.vt_ref), custom_call_target="tpu_custom_call" | custom-call | flops 5368709120 | bytes 7864320 | tf_op jit(solution)/shard_map/attention_forward/pallas_call | solution.py:102
  78.4 1.9 convert_multiply_fusion
  80.3 2.0 reduce_sum.31
  85.5 3.2 %collective-permute-start.10 = (bf16[512,640]{1,0:T(8,128)(2,1)S(1)}, bf16[512,640]{1,0:T(8,128)(2,1)S(1)}, u32[]{:S(2)}, u32[]{:S(2)}) collective-permute-start(bf16[512,640]{1,0:T(8,128)(2,1)S(1)} %get-tuple-element.29), channel_id=1, source_target_pairs={{1,0},{0,1},{5,2},{4,3},{3,4},{2,5},{7,6},{6,7},{9,8},{8,9},{13,10... | collective-permute-start | bytes 1966088 | tf_op jit(solution)/shard_map/ppermute | solution.py:558
  88.7 1.9 collective-permute-start.9
  90.7 112.8 %attention_backward.1 = (bf16[2,512,640]{2,1,0:T(8,128)(2,1)}, f32[2,1280,640]{2,1,0:T(8,128)}, f32[16,128]{1,0:T(8,128)}) custom-call(bf16[320,2048]{1,0:T(8,128)(2,1)} %copy-done.1, bf16[320,2048]{1,0:T(8,128)(2,1)} %copy-done.2, bf16[320,2048]{1,0:T(8,128)(2,1)} %copy-done.3, bf16[320,2048]{1,0:T(8,128)(2,1)} %copy-done.15, bf16[64,2048]{1,0:T(8,128)(2,1)} %copy-done.4, ...), custom_call_target="tpu_custom_call" | custom-call | flops 13421772800 | bytes 10485760 | tf_op jit(solution)/shard_map/attention_backward/pallas_call | solution.py:507
  203.4 2.7 %slice.52 = f32[2,960,640]{2,1,0:T(8,128)S(1)} slice(f32[2,1280,640]{2,1,0:T(8,128)} %get-tuple-element.24), slice={[0:2], [320:1280], [0:640]} | slice | bytes 9830400 | tf_op jit(solution)/shard_map/slice | solution.py:610
  206.1 2.7 %slice.56 = f32[2,320,640]{2,1,0:T(8,128)} slice(f32[2,1280,640]{2,1,0:T(8,128)} %get-tuple-element.24), slice={[0:2], [0:320], [0:640]} | slice | bytes 3276800 | tf_op jit(solution)/shard_map/slice | solution.py:609
  209.5 2.3 %slice_bitcast_fusion = (f32[640,8,80]{0,2,1:T(8,128)}, f32[640,8,80]{0,2,1:T(8,128)}, f32[640,8,80]{0,2,1:T(8,128)}) fusion(f32[8,3,80,640]{3,2,1,0:T(8,128)S(1)} %bitcast.65), kind=kLoop, calls=%fused_computation.16 | loop fusion | bytes 9830400 | tf_op jit(solution)/shard_map/transpose | solution.py:611
  211.8 1.3 maximum_select_fusion
  (83 shorter events, 17.6 us)
Async XLA Ops:
  0.6 8.7 %copy-start.13 = (bf16[2,512,640]{2,1,0:T(8,128)(2,1)S(1)}, bf16[2,512,640]{2,1,0:T(8,128)(2,1)}, u32[]{:S(2)}) copy-start(bf16[2,512,640]{2,1,0:T(8,128)(2,1)} %param.10) | copy-start | bytes 3932164
  0.7 14.8 %copy-start.16 = (bf16[640,8,80]{0,2,1:T(8,128)(2,1)S(1)}, bf16[640,8,80]{0,2,1:T(8,128)(2,1)}, u32[]{:S(2)}) copy-start(bf16[640,8,80]{0,2,1:T(8,128)(2,1)} %param.15) | copy-start | bytes 2457604
  3.3 16.4 %collective-permute-start.1 = (bf16[512,640]{1,0:T(8,128)(2,1)}, bf16[512,640]{1,0:T(8,128)(2,1)S(1)}, u32[]{:S(2)}, u32[]{:S(2)}) collective-permute-start(bf16[512,640]{1,0:T(8,128)(2,1)} %get-tuple-element.33), channel_id=1, source_target_pairs={{0,1},{1,0},{2,5},{3,4},{4,3},{5,2},{6,7},{7,6},{8,9},{9,8},{10,13... | collective-permute-start | bytes 1966088 | tf_op jit(solution)/shard_map/ppermute | solution.py:558
  7.1 19.9 %collective-permute-start = (bf16[512,640]{1,0:T(8,128)(2,1)}, bf16[512,640]{1,0:T(8,128)(2,1)S(1)}, u32[]{:S(2)}, u32[]{:S(2)}) collective-permute-start(bf16[512,640]{1,0:T(8,128)(2,1)} %get-tuple-element.32), channel_id=1, source_target_pairs={{0,0},{1,1},{2,4},{3,5},{4,2},{5,3},{6,6},{7,7},{8,8},{9,9},{10,12... | collective-permute-start | bytes 1966088 | tf_op jit(solution)/shard_map/ppermute | solution.py:558
  10.5 26.7 %collective-permute-start.5 = (bf16[512,640]{1,0:T(8,128)(2,1)}, bf16[512,640]{1,0:T(8,128)(2,1)}, u32[]{:S(2)}, u32[]{:S(2)}) collective-permute-start(bf16[512,640]{1,0:T(8,128)(2,1)} %get-tuple-element.31), channel_id=1, source_target_pairs={{0,0},{1,1},{2,4},{3,5},{4,2},{5,3},{6,6},{7,7},{8,8},{9,9},{10,12... | collective-permute-start | bytes 1966088 | tf_op jit(solution)/shard_map/ppermute | solution.py:558
  15.4 22.2 %collective-permute-start.6 = (bf16[512,640]{1,0:T(8,128)(2,1)}, bf16[512,640]{1,0:T(8,128)(2,1)}, u32[]{:S(2)}, u32[]{:S(2)}) collective-permute-start(bf16[512,640]{1,0:T(8,128)(2,1)} %get-tuple-element.30), channel_id=1, source_target_pairs={{0,1},{1,0},{2,5},{3,4},{4,3},{5,2},{6,7},{7,6},{8,9},{9,8},{10,13... | collective-permute-start | bytes 1966088 | tf_op jit(solution)/shard_map/ppermute | solution.py:558
  18.0 5.1 %copy-start.10 = (bf16[640,4,80]{0,2,1:T(8,128)(2,1)}, bf16[640,4,80]{0,2,1:T(8,128)(2,1)S(1)}, u32[]{:S(2)}) copy-start(bf16[640,4,80]{0,2,1:T(8,128)(2,1)S(1)} %get-tuple-element.35) | copy-start | bytes 1228804
  18.2 10.6 %copy-start.19 = (f32[640]{0:T(1024)S(1)}, f32[640]{0:T(1024)}, u32[]{:S(2)}) copy-start(f32[640]{0:T(1024)} %param.11) | copy-start | bytes 7684
  19.7 21.0 %collective-permute-start.3 = (bf16[512,640]{1,0:T(8,128)(2,1)S(1)}, bf16[512,640]{1,0:T(8,128)(2,1)S(1)}, u32[]{:S(2)}, u32[]{:S(2)}) collective-permute-start(bf16[512,640]{1,0:T(8,128)(2,1)S(1)} %collective-permute-done.1), channel_id=1, source_target_pairs={{0,4},{1,5},{2,6},{3,7},{4,0},{5,1},{6,2},{7,3},{8,12},{9,13},{10,... | collective-permute-start | bytes 1966088 | tf_op jit(solution)/shard_map/ppermute | solution.py:558
  27.0 13.7 %collective-permute-start.2 = (bf16[512,640]{1,0:T(8,128)(2,1)S(1)}, bf16[512,640]{1,0:T(8,128)(2,1)S(1)}, u32[]{:S(2)}, u32[]{:S(2)}) collective-permute-start(bf16[512,640]{1,0:T(8,128)(2,1)S(1)} %collective-permute-done), channel_id=1, source_target_pairs={{0,4},{1,5},{2,6},{3,7},{4,0},{5,1},{6,2},{7,3},{8,12},{9,13},{10,... | collective-permute-start | bytes 1966088 | tf_op jit(solution)/shard_map/ppermute | solution.py:558
  31.3 45.6 %copy-start.8 = (bf16[4,80,640]{2,1,0:T(8,128)(2,1)}, bf16[4,80,640]{2,1,0:T(8,128)(2,1)S(1)}, u32[]{:S(2)}) copy-start(bf16[4,80,640]{2,1,0:T(8,128)(2,1)S(1)} %get-tuple-element.41) | copy-start | bytes 1228804
  37.2 39.5 %collective-permute-start.7 = (bf16[512,640]{1,0:T(8,128)(2,1)}, bf16[512,640]{1,0:T(8,128)(2,1)S(1)}, u32[]{:S(2)}, u32[]{:S(2)}) collective-permute-start(bf16[512,640]{1,0:T(8,128)(2,1)} %collective-permute-done.5), channel_id=1, source_target_pairs={{0,4},{1,5},{2,6},{3,7},{4,0},{5,1},{6,2},{7,3},{8,12},{9,13},{10,... | collective-permute-start | bytes 1966088 | tf_op jit(solution)/shard_map/ppermute | solution.py:558
  37.6 39.2 %collective-permute-start.8 = (bf16[512,640]{1,0:T(8,128)(2,1)}, bf16[512,640]{1,0:T(8,128)(2,1)S(1)}, u32[]{:S(2)}, u32[]{:S(2)}) collective-permute-start(bf16[512,640]{1,0:T(8,128)(2,1)} %collective-permute-done.6), channel_id=1, source_target_pairs={{0,4},{1,5},{2,6},{3,7},{4,0},{5,1},{6,2},{7,3},{8,12},{9,13},{10,... | collective-permute-start | bytes 1966088 | tf_op jit(solution)/shard_map/ppermute | solution.py:558
  40.7 7.3 %copy-start.20 = (f32[640]{0:T(1024)S(1)}, f32[640]{0:T(1024)}, u32[]{:S(2)}) copy-start(f32[640]{0:T(1024)} %param.12) | copy-start | bytes 7684
  48.1 5.1 %copy-start.11 = (bf16[640,4,80]{0,2,1:T(8,128)(2,1)S(1)}, bf16[640,4,80]{0,2,1:T(8,128)(2,1)}, u32[]{:S(2)}) copy-start(bf16[640,4,80]{0,2,1:T(8,128)(2,1)} %copy-done.10) | copy-start | bytes 1228804
  53.2 2.5 %copy-start.7 = (bf16[2048,640]{1,0:T(8,128)(2,1)}, bf16[2048,640]{1,0:T(8,128)(2,1)S(1)}, u32[]{:S(2)}) copy-start(bf16[2048,640]{1,0:T(8,128)(2,1)S(1)} %fusion.5.normed_hbm) | copy-start | bytes 7864324
  54.4 2.5 %copy-start.1 = (bf16[320,2048]{1,0:T(8,128)(2,1)}, bf16[320,2048]{1,0:T(8,128)(2,1)S(1)}, u32[]{:S(2)}) copy-start(bf16[320,2048]{1,0:T(8,128)(2,1)S(1)} %convolution_convert_fusion.3.qt_ref) | copy-start | bytes 3932164
  56.9 19.0 %copy-start.3 = (bf16[320,2048]{1,0:T(8,128)(2,1)}, bf16[320,2048]{1,0:T(8,128)(2,1)S(1)}, u32[]{:S(2)}) copy-start(bf16[320,2048]{1,0:T(8,128)(2,1)S(1)} %convolution_convert_fusion.1.vt_ref) | copy-start | bytes 3932164
  75.9 7.3 %copy-start = (bf16[320,2048]{1,0:T(8,128)(2,1)}, bf16[320,2048]{1,0:T(8,128)(2,1)S(1)}, u32[]{:S(2)}) copy-start(bf16[320,2048]{1,0:T(8,128)(2,1)S(1)} %get-tuple-element.17.ot_hbm) | copy-start | bytes 3932164
  76.0 8.2 %collective-permute-start.4 = (bf16[320,1024]{1,0:T(8,128)(2,1)S(1)}, bf16[320,1024]{1,0:T(8,128)(2,1)S(1)}, u32[]{:S(2)}, u32[]{:S(2)}) collective-permute-start(bf16[320,1024]{1,0:T(8,128)(2,1)S(1)} %slice.47), channel_id=1, source_target_pairs={{0,4},{1,5},{2,6},{3,7},{4,0},{5,1},{6,2},{7,3},{8,12},{9,13},{10,... | collective-permute-start | bytes 1966088 | tf_op jit(solution)/shard_map/ppermute | solution.py:558
  80.3 3.0 %copy-start.9 = (bf16[4,80,640]{2,1,0:T(8,128)(2,1)S(1)}, bf16[4,80,640]{2,1,0:T(8,128)(2,1)}, u32[]{:S(2)}) copy-start(bf16[4,80,640]{2,1,0:T(8,128)(2,1)} %copy-done.8) | copy-start | bytes 1228804
  85.5 126.3 %collective-permute-start.10 = (bf16[512,640]{1,0:T(8,128)(2,1)S(1)}, bf16[512,640]{1,0:T(8,128)(2,1)S(1)}, u32[]{:S(2)}, u32[]{:S(2)}) collective-permute-start(bf16[512,640]{1,0:T(8,128)(2,1)S(1)} %get-tuple-element.29), channel_id=1, source_target_pairs={{1,0},{0,1},{5,2},{4,3},{3,4},{2,5},{7,6},{6,7},{9,8},{8,9},{13,10... | collective-permute-start | bytes 1966088 | tf_op jit(solution)/shard_map/ppermute | solution.py:558
  88.7 123.1 %collective-permute-start.9 = (bf16[512,640]{1,0:T(8,128)(2,1)S(1)}, bf16[512,640]{1,0:T(8,128)(2,1)S(1)}, u32[]{:S(2)}, u32[]{:S(2)}) collective-permute-start(bf16[512,640]{1,0:T(8,128)(2,1)S(1)} %get-tuple-element.28), channel_id=1, source_target_pairs={{0,0},{1,1},{4,2},{5,3},{2,4},{3,5},{6,6},{7,7},{8,8},{9,9},{12,10... | collective-permute-start | bytes 1966088 | tf_op jit(solution)/shard_map/ppermute | solution.py:558
  206.1 2.7 %copy-start.18 = (f32[16,128]{1,0:T(8,128)S(1)}, f32[16,128]{1,0:T(8,128)}, u32[]{:S(2)}) copy-start(f32[16,128]{1,0:T(8,128)} %get-tuple-element.23) | copy-start | bytes 24580
  (9 other events, 16.0 us)
